TPU v7x, 128 devices: a whole 4x4x4 slice. The times are simulated.
128 devices in a mesh: client: 128 (over x, z, y, core).
Axes of the slice: x: 4, y: 4, z: 4, core: 2. Of those that a mesh axis runs over, the one named last changes fastest.
Arguments:
- patches: bfloat16 [16384, 192], P('client'), may hold values from -6 to 6
- labels: int32 [1024], replicated, may hold values from 0 to 9
- assign: int32 [128, 1], replicated, may hold values from 0 to 15; in each aligned block of 128 rows (0 to 127, 128 to 255, ...) at most 16 rows name the same one
- patch_embed: bfloat16 [192, 384], replicated, may hold values from -0.4375 to 0.4375
- positions: bfloat16 [16, 384], replicated, may hold values from -3 to 3
- client_in: bfloat16 [384, 3072], replicated, may hold values from -3 to 3
- client_down: bfloat16 [1536, 384], replicated, may hold values from -0.15625 to 0.15625
- server_in: bfloat16 [2, 6144, 3072], P(None, 'client'), may hold values from -3 to 3
- server_down: bfloat16 [2, 24576, 384], P(None, 'client'), may hold values from -0.15625 to 0.15625
- classifier: bfloat16 [16, 384, 10], replicated, may hold values from -15 to 15
Outputs:
- losses: float32 [128, 16], P('client')
- grad_patch_embed: float32 [192, 384], P(None, 'client')
- grad_positions: float32 [16, 384], P(None, 'client')
- grad_client_in: float32 [384, 3072], P(None, 'client')
- grad_client_down: float32 [1536, 384], P(None, 'client')
- grad_server_in: float32 [2, 6144, 3072], P(None, 'client')
- grad_server_down: float32 [2, 24576, 384], P(None, 'client')
- grad_classifier: float32 [6144, 10], P('client')
Inputs may be any that keep to these rules, and one draw needn't show every extreme that they name: `assign`: no server shard is named by more than 16 clients, a bound that some block reaches.
All inputs are finite; a program needn't handle non-finite values.
Results may differ from a plain program's by a relative error of at most 0.025.
Values may be sent and summed in bfloat16 or wider, within the bound.
A program may use at most 128 MiB of HBM per device.

v0:
```python
import math

import jax
import jax.numpy as jnp
from jax import lax
from jax.sharding import PartitionSpec as P

D = 384
HEADS = 6
FF = 1536
TOK = 16
CLASSES = 10
IMG = 8
SHARDS = 16
SLOTS = 2
SERVER_LAYERS = 2


EPSILON = 1e-06


def partner_2(block, axis, apart):
    count = lax.axis_size(axis)
    route = []
    for low in range(count):
        high = low | 1 << apart
        if high != low and high < count:
            route += [(low, high), (high, low)]
    return lax.ppermute(block, axis, route)


def layer_norm(inputs):
    centre = inputs - jnp.mean(inputs, axis=-1, keepdims=True)
    spread = jnp.mean(centre * centre, axis=-1, keepdims=True)
    return centre * lax.rsqrt(spread + EPSILON)


def encoder_block(stream, weight_in, weight_down):
    images, tokens, model_width = stream.shape
    head_dim = model_width // HEADS
    normed = layer_norm(stream).astype(jnp.bfloat16).reshape(images * tokens, model_width)
    projected = jnp.dot(normed, weight_in[:, : 3 * model_width], preferred_element_type=jnp.float32)
    projected = projected.reshape(images, tokens, 3, HEADS, head_dim)
    queries = projected[:, :, 0]
    key_rows = projected[:, :, 1]
    values = projected[:, :, 2]
    scores = jnp.einsum("bqhe,bkhe->bhqk", queries, key_rows) / math.sqrt(head_dim)
    weights_attn = jax.nn.softmax(scores, axis=-1)
    attended = jnp.einsum("bhqk,bkhe->bqhe", weights_attn, values)
    attended = attended.reshape(images * tokens, model_width).astype(jnp.bfloat16)
    stream = stream + jnp.dot(
        attended,
        weight_in[:, 3 * model_width : 4 * model_width],
        preferred_element_type=jnp.float32,
    ).reshape(images, tokens, model_width)
    normed = layer_norm(stream).astype(jnp.bfloat16).reshape(images * tokens, model_width)
    hidden = jax.nn.gelu(
        jnp.dot(normed, weight_in[:, 4 * model_width :], preferred_element_type=jnp.float32)
    ).astype(jnp.bfloat16)
    return stream + jnp.dot(hidden, weight_down, preferred_element_type=jnp.float32).reshape(
        images, tokens, model_width
    )


def client_forward(patch_rows, patch_embed, positions, client_in, client_down):
    stream = jnp.dot(patch_rows, patch_embed, preferred_element_type=jnp.float32).reshape(
        -1, TOK, D
    )
    stream = stream + positions.astype(jnp.float32)
    stream = encoder_block(stream, client_in, client_down)
    return stream.reshape(-1, D).astype(jnp.bfloat16)


def server_loss(cut_rows, slot_hot, weights_in, weights_down, class_shard):
    stream = cut_rows.astype(jnp.float32).reshape(-1, TOK, D)
    for layer in range(len(weights_in)):
        stream = encoder_block(stream, weights_in[layer], weights_down[layer])
    pooled = layer_norm(jnp.mean(stream, axis=1)).astype(jnp.bfloat16)
    logits = jnp.dot(pooled, class_shard, preferred_element_type=jnp.float32)
    per_loss = (jax.nn.logsumexp(logits, axis=-1) - jnp.sum(slot_hot * logits, axis=-1)) * jnp.sum(
        slot_hot, axis=-1
    )
    return (jnp.sum(per_loss), per_loss)


def arrival_rank(routes):
    places = jnp.arange(routes.shape[0], dtype=jnp.int32)
    earlier = (routes[:, None] == routes[None, :]) & (places[:, None] < places[None, :])
    return jnp.sum(earlier.astype(jnp.int32), axis=0)


def select_matrix(routes, arrival, shard, capacity):
    slots_here = jnp.arange(capacity, dtype=jnp.int32)[:, None]
    return ((routes[None, :] == shard) & (arrival[None, :] == slots_here)).astype(jnp.bfloat16)


def slot_labels(labels, selector, rank_in_group, per_image, members):
    label_table = labels.reshape(members, IMG)
    label_part = lax.dynamic_slice_in_dim(label_table, rank_in_group * per_image, per_image, 1)
    onehot = (label_part[:, :, None] == jnp.arange(CLASSES, dtype=jnp.int32)[None, None, :]).astype(
        jnp.float32
    )
    onehot = onehot.reshape(members, per_image * CLASSES)
    chosen = jnp.dot(selector.astype(jnp.float32), onehot)
    return chosen


def gather_group(flat_rows, group_bits, rank_in_group):
    stacked = flat_rows[None]
    for step_bit in range(group_bits):
        partner = partner_2(stacked, "client", step_bit)
        upper_half = rank_in_group >> step_bit & 1
        stacked = jnp.where(
            upper_half == 0,
            jnp.concatenate([stacked, partner], 0),
            jnp.concatenate([partner, stacked], 0),
        )
    return stacked


def reduce_group(blocks, group_bits, rank_in_group, order_bits):
    shaped = blocks.reshape((2,) * group_bits + (blocks.shape[1],))
    for step_bit in order_bits:
        axis_pos = group_bits - 1 - step_bit
        upper_half = rank_in_group >> step_bit & 1
        keeping = lax.dynamic_slice_in_dim(shaped, upper_half, 1, axis_pos)
        sending = lax.dynamic_slice_in_dim(shaped, 1 - upper_half, 1, axis_pos)
        shaped = keeping + partner_2(sending.astype(jnp.bfloat16), "client", step_bit).astype(
            sending.dtype
        )
    return shaped.reshape(-1)


def per_device(
    patches,
    labels,
    assign,
    patch_embed,
    positions,
    client_in,
    client_down,
    server_in,
    server_down,
    classifier,
):
    members = lax.axis_size("client")
    group_size = members // SHARDS
    group_bits = group_size.bit_length() - 1
    device_index = lax.axis_index("client")
    rank_in_group = device_index % group_size
    shard_here = device_index // group_size
    per_image = IMG // group_size
    piece_rows = IMG * TOK // group_size
    capacity = SLOTS * group_size
    width_all = 4 * D + FF
    rows_in = D // group_size
    rows_down = FF // group_size
    routes = assign[:, 0]
    places = jnp.arange(members, dtype=jnp.int32)
    own_shard = jnp.sum(jnp.where(places == device_index, routes, 0))

    def client_of(embed_weights, position_weights, in_weights, down_weights):
        return client_forward(patches, embed_weights, position_weights, in_weights, down_weights)

    cut_acts, client_back = jax.vjp(client_of, patch_embed, positions, client_in, client_down)
    pieces = cut_acts.reshape(group_size, piece_rows, D)
    tiled = jnp.broadcast_to(pieces[None], (SHARDS, group_size, piece_rows, D)).reshape(
        members, piece_rows, D
    )
    target = places // group_size == own_shard
    outgoing = jnp.where(target[:, None, None], tiled, jnp.zeros_like(tiled))
    arrived = lax.all_to_all(outgoing, "client", split_axis=0, concat_axis=0, tiled=True)
    arrival = arrival_rank(routes)
    selector = select_matrix(routes, arrival, shard_here, capacity)
    compact = jnp.dot(
        selector, arrived.reshape(members, piece_rows * D), preferred_element_type=jnp.float32
    )
    compact = compact.astype(jnp.bfloat16).reshape(capacity * piece_rows, D)
    slot_hot = slot_labels(labels, selector, rank_in_group, per_image, members)
    weights_in = []
    weights_down = []
    split_at = rows_in * width_all
    for layer in range(SERVER_LAYERS):
        flat_rows = jnp.concatenate([server_in[layer].reshape(-1), server_down[layer].reshape(-1)])
        stacked = gather_group(flat_rows, group_bits, rank_in_group)
        weights_in.append(stacked[:, :split_at].reshape(D, width_all))
        weights_down.append(stacked[:, split_at:].reshape(FF, D))
    class_shard = lax.dynamic_index_in_dim(classifier, shard_here, 0, keepdims=False)

    def loss_of(cut_rows, list_in, list_down, class_weights):
        return server_loss(cut_rows, slot_hot, list_in, list_down, class_weights)

    total_loss, server_back, per_loss = jax.vjp(
        loss_of, compact, tuple(weights_in), tuple(weights_down), class_shard, has_aux=True
    )
    grad_cut, grad_in, grad_down, grad_class = server_back(jnp.ones((), jnp.float32))
    returning = jnp.dot(
        selector.T, grad_cut.reshape(capacity, piece_rows * D), preferred_element_type=jnp.float32
    )
    returning = returning.astype(jnp.bfloat16).reshape(members, piece_rows, D)
    returned = lax.all_to_all(returning, "client", split_axis=0, concat_axis=0, tiled=True)
    own_grads = lax.dynamic_slice_in_dim(returned, own_shard * group_size, group_size, 0)
    own_grads = own_grads.reshape(IMG * TOK, D)
    client_parts = client_back(own_grads)
    summed = lax.psum_scatter(
        tuple((part_grad.astype(jnp.float32) for part_grad in client_parts)),
        "client",
        scatter_dimension=1,
        tiled=True,
    )
    blocks_in = (
        jnp.stack(grad_in)
        .astype(jnp.float32)
        .reshape(SERVER_LAYERS, group_size, rows_in * width_all)
    )
    blocks_in = blocks_in.transpose(1, 0, 2).reshape(group_size, -1)
    blocks_down = (
        jnp.stack(grad_down).astype(jnp.float32).reshape(SERVER_LAYERS, group_size, rows_down * D)
    )
    blocks_down = blocks_down.transpose(1, 0, 2).reshape(group_size, -1)
    blocks_class = grad_class.astype(jnp.float32).reshape(group_size, rows_in * CLASSES)
    blocks = jnp.concatenate([blocks_in, blocks_down, blocks_class], 1)
    order_bits = list(range(group_bits - 1, -1, -1))
    own_sum = reduce_group(blocks, group_bits, rank_in_group, order_bits)
    size_in = SERVER_LAYERS * rows_in * width_all
    size_down = SERVER_LAYERS * rows_down * D
    grad_server_in = own_sum[:size_in].reshape(SERVER_LAYERS, rows_in, width_all)
    grad_server_down = own_sum[size_in : size_in + size_down].reshape(SERVER_LAYERS, rows_down, D)
    grad_classifier = own_sum[size_in + size_down :].reshape(rows_in, CLASSES)
    return (
        per_loss.reshape(1, -1),
        summed[0],
        summed[1],
        summed[2],
        summed[3],
        grad_server_in,
        grad_server_down,
        grad_classifier,
    )


def solution(mesh):
    in_specs = (
        P("client", None),
        P(),
        P(),
        P(),
        P(),
        P(),
        P(),
        P(None, "client", None),
        P(None, "client", None),
        P(),
    )
    out_specs = (
        P("client", None),
        P(None, "client"),
        P(None, "client"),
        P(None, "client"),
        P(None, "client"),
        P(None, "client", None),
        P(None, "client", None),
        P("client", None),
    )
    return jax.shard_map(
        per_device, mesh=mesh, in_specs=in_specs, out_specs=out_specs, check_vma=False
    )
```

profile of v0, /device:TPU:0, one launch (start us, length us, event | category | flops | bytes accessed | tf_op | source)
XLA Modules:
  0.0 692.7 jit_solution(13165340402975691188)
XLA Ops:
  28.2 11.2 %all-to-all-start = ((bf16[128,16,384]{2,1,0:T(8,128)(2,1)}), bf16[128,16,384]{2,1,0:T(8,128)(2,1)S(1)}, u32[]{:S(2)}, u32[]{:S(2)}) async-start(bf16[128,16,384]{2,1,0:T(8,128)(2,1)} %bitcast_select_fusion), calls=%async_computation | async-start | bytes 3145728 | tf_op jit(solution)/shard_map/all_to_all | solution.py:172
  41.9 5.8 broadcast_select_fusion.1
  48.7 5.8 broadcast_select_fusion
  54.5 13.4 %collective-permute-start.4 = (bf16[2,221184]{1,0:T(2,128)(2,1)S(1)}, bf16[2,221184]{1,0:T(2,128)(2,1)S(1)}, u32[]{:S(2)}, u32[]{:S(2)}) collective-permute-start(bf16[2,221184]{1,0:T(2,128)(2,1)S(1)} %broadcast_select_fusion), channel_id=1, source_target_pairs={{0,2},{2,0},{1,3},{3,1},{4,6},{6,4},{5,7},{7,5},{8,10},{10,8},{9,1... | collective-permute-start | bytes 2654216 | tf_op jit(solution)/shard_map/ppermute | solution.py:29
  67.8 9.2 %collective-permute-done.1 = bf16[2,221184]{1,0:T(2,128)(2,1)S(1)} collective-permute-done((bf16[2,221184]{1,0:T(2,128)(2,1)S(1)}, bf16[2,221184]{1,0:T(2,128)(2,1)S(1)}, u32[]{:S(2)}, u32[]{:S(2)}) %collective-permute-start.1) | collective-permute-done | bytes 884768 | tf_op jit(solution)/shard_map/ppermute | solution.py:29
  83.8 12.2 %collective-permute-done.4 = bf16[2,221184]{1,0:T(2,128)(2,1)S(1)} collective-permute-done((bf16[2,221184]{1,0:T(2,128)(2,1)S(1)}, bf16[2,221184]{1,0:T(2,128)(2,1)S(1)}, u32[]{:S(2)}, u32[]{:S(2)}) %collective-permute-start.4) | collective-permute-done | bytes 884768 | tf_op jit(solution)/shard_map/ppermute | solution.py:29
  107.2 28.4 %collective-permute-done.2 = bf16[4,221184]{1,0:T(4,128)(2,1)} collective-permute-done((bf16[4,221184]{1,0:T(4,128)(2,1)}, bf16[4,221184]{1,0:T(4,128)(2,1)}, u32[]{:S(2)}, u32[]{:S(2)}) %collective-permute-start.2) | collective-permute-done | bytes 1769504 | tf_op jit(solution)/shard_map/ppermute | solution.py:29
  135.6 6.6 maximum_select_fusion
  163.8 9.1 %collective-permute-done.5 = bf16[4,221184]{1,0:T(4,128)(2,1)} collective-permute-done((bf16[4,221184]{1,0:T(4,128)(2,1)}, bf16[4,221184]{1,0:T(4,128)(2,1)}, u32[]{:S(2)}, u32[]{:S(2)}) %collective-permute-start.5) | collective-permute-done | bytes 1769504 | tf_op jit(solution)/shard_map/ppermute | solution.py:29
  172.9 6.7 maximum_select_fusion.1
  280.0 9.1 %maximum_bitcast_fusion.1 = bf16[8,2,73728]{2,1,0:T(2,128)(2,1)} fusion(bf16[1,8,73728]{2,0,1:T(2,128)(2,1)} %stack.27, bf16[1,8,73728]{2,0,1:T(2,128)(2,1)} %stack.26), kind=kLoop, calls=%fused_computation.27 | loop fusion | flops 4718592 | bytes 4718592 | tf_op jit(solution)/shard_map/transpose | solution.py:220
  295.9 8.9 %all-to-all-start.1 = ((bf16[128,16,384]{2,1,0:T(8,128)(2,1)}), bf16[128,16,384]{2,1,0:T(8,128)(2,1)}, u32[]{:S(2)}, u32[]{:S(2)}) async-start(bf16[128,16,384]{2,1,0:T(8,128)(2,1)} %bitcast.125), calls=%async_computation.1 | async-start | bytes 3145728 | tf_op jit(solution)/shard_map/all_to_all | solution.py:201
  307.8 7.3 %stack.24 = bf16[1,8,147456]{2,0,1:T(2,128)(2,1)} reshape(bf16[384,3072]{1,0:T(8,128)(2,1)} %pad_add_fusion.1) | data formatting | bytes 4718592 | tf_op jit(solution)/shard_map/stack | solution.py:212
  318.0 6.9 stack.25
  324.8 12.9 %maximum_bitcast_fusion = bf16[8,2,147456]{2,1,0:T(2,128)(2,1)} fusion(bf16[1,8,147456]{2,0,1:T(2,128)(2,1)} %stack.25, bf16[1,8,147456]{2,0,1:T(2,128)(2,1)} %stack.24), kind=kLoop, calls=%fused_computation.6 | loop fusion | flops 9437184 | bytes 9437184 | tf_op jit(solution)/shard_map/transpose | solution.py:216
  337.8 6.7 concatenate.71
  344.5 31.6 %maximum_convert_fusion = f32[2,2,2,442848]{3,2,1,0:T(2,128)S(1)} fusion(bf16[2,2,2,480]{3,2,1,0:T(2,128)(2,1)S(1)} %copy-done.99, bf16[2,2,2,147456]{3,2,1,0:T(2,128)(2,1)} %concatenate.72, bf16[2,2,2,294912]{3,2,1,0:T(2,128)(2,1)} %concatenate.71), kind=kLoop, calls=%fused_computation.1 | loop fusion | flops 21256704 | bytes 21256704 | tf_op jit(solution)/shard_map/concatenate | solution.py:222
  400.4 64.1 %collective-permute-done.6 = bf16[1,2,2,442848]{3,2,1,0:T(2,128)(2,1)} collective-permute-done((bf16[1,2,2,442848]{3,2,1,0:T(2,128)(2,1)}, bf16[1,2,2,442848]{3,2,1,0:T(2,128)(2,1)}, u32[]{:S(2)}, u32[]{:S(2)}) %collective-permute-start.6) | collective-permute-done | bytes 3542816 | tf_op jit(solution)/shard_map/ppermute | solution.py:29
  464.4 6.0 convert_add_fusion
  484.6 42.1 %collective-permute-done.7 = bf16[1,1,2,442848]{3,2,1,0:T(2,128)(2,1)} collective-permute-done((bf16[1,1,2,442848]{3,2,1,0:T(2,128)(2,1)}, bf16[1,1,2,442848]{3,2,1,0:T(2,128)(2,1)}, u32[]{:S(2)}, u32[]{:S(2)}) %collective-permute-start.7) | collective-permute-done | bytes 1771424 | tf_op jit(solution)/shard_map/ppermute | solution.py:29
  534.7 70.7 %all-reduce.19 = f32[16,384]{0,1:T(8,128)S(1)} all-reduce(f32[16,384]{0,1:T(8,128)S(1)} %copy.154), channel_id=3, replica_groups=mesh['client'=128] {'client'}, use_global_device_ids=true, to_apply=%region_46.47.clone | all-reduce | flops 6144 | bytes 49152
  606.0 49.1 %all-reduce.25.cloned.1.call-done = (f32[192,384]{1,0:T(8,128)}, f32[384,3072]{1,0:T(8,128)}, f32[1536,384]{0,1:T(8,128)}) async-done(((f32[192,384]{1,0:T(8,128)}, f32[384,3072]{1,0:T(8,128)}, f32[1536,384]{0,1:T(8,128)}), (f32[192,384]{1,0:T(8,128)}, f32[384,3072]{1,0:T(8,128)}, f32[1536,384]{0,1:T(8,128)})) %all-reduce.25.cloned.1.call-update) | async-done | bytes 7372816
  664.4 6.1 slice_reduce_fusion.1
  670.5 12.2 %slice_reduce_fusion = f32[294912]{0:T(1024)S(1)} fusion(f32[1,1,1,442848]{3,2,1,0:T(1,128)S(1)} %convert_add_fusion.2), kind=kLoop, calls=%fused_computation.81 | loop fusion | bytes 2359296 | tf_op jit(solution)/shard_map/slice | solution.py:227
  (508 shorter events, 233.5 us)
Async XLA Ops:
  7.2 19.1 %copy-start = (bf16[1536,384]{1,0:T(8,128)(2,1)S(1)}, bf16[1536,384]{1,0:T(8,128)(2,1)}, u32[]{:S(2)}) copy-start(bf16[1536,384]{1,0:T(8,128)(2,1)} %param.16) | copy-start | bytes 3538948
  10.8 37.8 %collective-permute-start.3 = (bf16[1,221184]{1,0:T(2,128)(2,1)}, bf16[1,221184]{1,0:T(2,128)(2,1)}, u32[]{:S(2)}, u32[]{:S(2)}) collective-permute-start(bf16[1,221184]{1,0:T(2,128)(2,1)} %broadcast_in_dim.151), channel_id=1, source_target_pairs={{0,1},{1,0},{2,3},{3,2},{4,5},{5,4},{6,7},{7,6},{8,9},{9,8},{10,11... | collective-permute-start | bytes 1327112 | tf_op jit(solution)/shard_map/ppermute | solution.py:29
  12.4 29.5 %collective-permute-start = (bf16[1,221184]{1,0:T(2,128)(2,1)}, bf16[1,221184]{1,0:T(2,128)(2,1)}, u32[]{:S(2)}, u32[]{:S(2)}) collective-permute-start(bf16[1,221184]{1,0:T(2,128)(2,1)} %broadcast_in_dim.150), channel_id=1, source_target_pairs={{0,1},{1,0},{2,3},{3,2},{4,5},{5,4},{6,7},{7,6},{8,9},{9,8},{10,11... | collective-permute-start | bytes 1327112 | tf_op jit(solution)/shard_map/ppermute | solution.py:29
  14.2 7.4 %copy-start.37 = (f32[16,384]{1,0:T(8,128)}, f32[16,384]{1,0:T(8,128)S(1)}, u32[]{:S(2)}) copy-start(f32[16,384]{1,0:T(8,128)S(1)} %convert_element_type.321) | copy-start | bytes 73732
  28.2 11.2 %copy-start.103 = (s32[1024]{0:T(1024)S(1)}, s32[1024]{0:T(1024)}, u32[]{:S(2)}) copy-start(s32[1024]{0:T(1024)} %param.11) | copy-start | bytes 12292
  28.2 74.5 %all-to-all-start = ((bf16[128,16,384]{2,1,0:T(8,128)(2,1)}), bf16[128,16,384]{2,1,0:T(8,128)(2,1)S(1)}, u32[]{:S(2)}, u32[]{:S(2)}) async-start(bf16[128,16,384]{2,1,0:T(8,128)(2,1)} %bitcast_select_fusion), calls=%async_computation | async-start | bytes 3145728 | tf_op jit(solution)/shard_map/all_to_all | solution.py:172
  41.8 61.3 %copy-start.106 = (s32[128]{0:T(128)}, s32[128]{0:T(128)S(1)}, u32[]{:S(2)}) copy-start(s32[128]{0:T(128)S(1)} %convert_reduce_fusion) | copy-start | bytes 1540
  41.8 61.3 %copy-start.109 = (pred[128]{0:T(512)(128)(4,1)}, pred[128]{0:T(512)(128)(4,1)S(1)}, u32[]{:S(2)}) copy-start(pred[128]{0:T(512)(128)(4,1)S(1)} %broadcast_compare_fusion) | copy-start | bytes 388
  47.6 29.5 %collective-permute-start.1 = (bf16[2,221184]{1,0:T(2,128)(2,1)S(1)}, bf16[2,221184]{1,0:T(2,128)(2,1)S(1)}, u32[]{:S(2)}, u32[]{:S(2)}) collective-permute-start(bf16[2,221184]{1,0:T(2,128)(2,1)S(1)} %broadcast_select_fusion.1), channel_id=1, source_target_pairs={{0,2},{2,0},{1,3},{3,1},{4,6},{6,4},{5,7},{7,5},{8,10},{10,8},{9,1... | collective-permute-start | bytes 2654216 | tf_op jit(solution)/shard_map/ppermute | solution.py:29
  54.5 41.6 %collective-permute-start.4 = (bf16[2,221184]{1,0:T(2,128)(2,1)S(1)}, bf16[2,221184]{1,0:T(2,128)(2,1)S(1)}, u32[]{:S(2)}, u32[]{:S(2)}) collective-permute-start(bf16[2,221184]{1,0:T(2,128)(2,1)S(1)} %broadcast_select_fusion), channel_id=1, source_target_pairs={{0,2},{2,0},{1,3},{3,1},{4,6},{6,4},{5,7},{7,5},{8,10},{10,8},{9,1... | collective-permute-start | bytes 2654216 | tf_op jit(solution)/shard_map/ppermute | solution.py:29
  81.3 54.3 %collective-permute-start.2 = (bf16[4,221184]{1,0:T(4,128)(2,1)}, bf16[4,221184]{1,0:T(4,128)(2,1)}, u32[]{:S(2)}, u32[]{:S(2)}) collective-permute-start(bf16[4,221184]{1,0:T(4,128)(2,1)} %maximum_select_fusion.2), channel_id=1, source_target_pairs={{0,4},{4,0},{1,5},{5,1},{2,6},{6,2},{3,7},{7,3},{8,12},{12,8},{9,1... | collective-permute-start | bytes 5308424 | tf_op jit(solution)/shard_map/ppermute | solution.py:29
  100.2 72.7 %collective-permute-start.5 = (bf16[4,221184]{1,0:T(4,128)(2,1)}, bf16[4,221184]{1,0:T(4,128)(2,1)}, u32[]{:S(2)}, u32[]{:S(2)}) collective-permute-start(bf16[4,221184]{1,0:T(4,128)(2,1)} %maximum_select_fusion.3), channel_id=1, source_target_pairs={{0,4},{4,0},{1,5},{5,1},{2,6},{6,2},{3,7},{7,3},{8,12},{12,8},{9,1... | collective-permute-start | bytes 5308424 | tf_op jit(solution)/shard_map/ppermute | solution.py:29
  155.0 8.2 %copy-start.64 = (f32[16,6,16]{2,1,0:T(8,128)}, f32[16,6,16]{2,1,0:T(8,128)S(1)}, u32[]{:S(2)}) copy-start(f32[16,6,16]{2,1,0:T(8,128)S(1)} %fusion.47) | copy-start | bytes 18436
  208.2 12.3 %copy-start.70 = (f32[16,16]{1,0:T(8,128)}, f32[16,16]{1,0:T(8,128)S(1)}, u32[]{:S(2)}) copy-start(f32[16,16]{1,0:T(8,128)S(1)} %fusion.105) | copy-start | bytes 3076
  252.2 9.1 %copy-start.34 = (bf16[16,16,384]{2,1,0:T(8,128)(2,1)S(1)}, bf16[16,16,384]{2,1,0:T(8,128)(2,1)}, u32[]{:S(2)}) copy-start(bf16[16,16,384]{2,1,0:T(8,128)(2,1)} %copy-done.33) | copy-start | bytes 589828
  254.1 9.8 %copy-start.49 = (bf16[256,384]{1,0:T(8,128)(2,1)S(1)}, bf16[256,384]{1,0:T(8,128)(2,1)}, u32[]{:S(2)}) copy-start(bf16[256,384]{1,0:T(8,128)(2,1)} %convert_element_type.397) | copy-start | bytes 589828
  295.9 8.9 %copy-start.18 = (bf16[384,1536]{1,0:T(8,128)(2,1)S(1)}, bf16[384,1536]{1,0:T(8,128)(2,1)}, u32[]{:S(2)}) copy-start(bf16[384,1536]{1,0:T(8,128)(2,1)} %fusion.146) | copy-start | bytes 3538948
  295.9 8.9 %copy-start.41 = (bf16[384,384]{1,0:T(8,128)(2,1)S(1)}, bf16[384,384]{1,0:T(8,128)(2,1)}, u32[]{:S(2)}) copy-start(bf16[384,384]{1,0:T(8,128)(2,1)} %fusion.149) | copy-start | bytes 884740
  295.9 92.3 %all-to-all-start.1 = ((bf16[128,16,384]{2,1,0:T(8,128)(2,1)}), bf16[128,16,384]{2,1,0:T(8,128)(2,1)}, u32[]{:S(2)}, u32[]{:S(2)}) async-start(bf16[128,16,384]{2,1,0:T(8,128)(2,1)} %bitcast.125), calls=%async_computation.1 | async-start | bytes 3145728 | tf_op jit(solution)/shard_map/all_to_all | solution.py:201
  304.8 350.3 %all-reduce.25.cloned.1.call-start = ((), (), s32[]{:S(2)}) async-start(), calls=%async_computation.2 | async-start | bytes 14745600
  381.2 7.9 %copy-start.26 = (f32[128,1536]{1,0:T(8,128)S(1)}, f32[128,1536]{1,0:T(8,128)}, u32[]{:S(2)}) copy-start(f32[128,1536]{1,0:T(8,128)} %copy-done.25) | copy-start | bytes 2359300
  384.7 79.7 %collective-permute-start.6 = (bf16[1,2,2,442848]{3,2,1,0:T(2,128)(2,1)}, bf16[1,2,2,442848]{3,2,1,0:T(2,128)(2,1)}, u32[]{:S(2)}, u32[]{:S(2)}) collective-permute-start(bf16[1,2,2,442848]{3,2,1,0:T(2,128)(2,1)} %dynamic-slice_convert_fusion), channel_id=1, source_target_pairs={{0,4},{4,0},{1,5},{5,1},{2,6},{6,2},{3,7},{7,3},{8,12},{12,8},{9,1... | collective-permute-start | bytes 10628360 | tf_op jit(solution)/shard_map/ppermute | solution.py:29
  475.9 50.8 %collective-permute-start.7 = (bf16[1,1,2,442848]{3,2,1,0:T(2,128)(2,1)}, bf16[1,1,2,442848]{3,2,1,0:T(2,128)(2,1)}, u32[]{:S(2)}, u32[]{:S(2)}) collective-permute-start(bf16[1,1,2,442848]{3,2,1,0:T(2,128)(2,1)} %dynamic-slice_convert_fusion.1), channel_id=1, source_target_pairs={{0,2},{2,0},{1,3},{3,1},{4,6},{6,4},{5,7},{7,5},{8,10},{10,8},{9,1... | collective-permute-start | bytes 5314184 | tf_op jit(solution)/shard_map/ppermute | solution.py:29
  534.0 126.1 %collective-permute-start.8 = (bf16[1,1,1,442848]{3,2,1,0:T(2,128)(2,1)}, bf16[1,1,1,442848]{3,2,1,0:T(2,128)(2,1)S(1)}, u32[]{:S(2)}, u32[]{:S(2)}) collective-permute-start(bf16[1,1,1,442848]{3,2,1,0:T(2,128)(2,1)} %dynamic-slice_convert_fusion.2), channel_id=1, source_target_pairs={{0,1},{1,0},{2,3},{3,2},{4,5},{5,4},{6,7},{7,6},{8,9},{9,8},{10,11... | collective-permute-start | bytes 2657096 | tf_op jit(solution)/shard_map/ppermute | solution.py:29
  (113 other events, 280.8 us)
Sparse Core Ops, SparseCore 0:
  484.7 170.3 all-reduce.24
where the time goes:
time: 704 us; the launch traced here: 693 us
  waiting for transfers between devices  214 us (30%)
  local copies, waits for them, and re-layouts  160 us (23%)
  other arithmetic  127 us (18%)
  blocking collectives  70.7 us (10%)
  matrix products  59.3 us (8%)
  starting transfers between devices  44.4 us (6%)
  between operations  17.1 us (2%)
    ppermute x9, waiting for transfers between devices, partner_2(): return lax.ppermute(block, axis, route)  165 us
    unnamed x1, blocking collectives  70.7 us
    unnamed x2, waiting for transfers between devices  49.1 us
    select_n x6, other arithmetic, gather_group(): jnp.where(upper_half == 0, jnp.concatenate([stacked, partner], 0), jnp.co...  33.1 us
    concatenate x1, other arithmetic, per_device(): blocks = jnp.concatenate([blocks_in, blocks_down, blocks_class], 1)  31.6 us
    unnamed x267, local copies, waits for them, and re-layouts  28.1 us
    ppermute x9, starting transfers between devices, partner_2(): return lax.ppermute(block, axis, route)  24.3 us
    add x3, other arithmetic, reduce_group(): keeping + partner_2(sending.astype(jnp.bfloat16), 'client', step_bit).ast...  14.4 us
  transfers between devices with their start and end apart: 12, of which 7 were waited for; matrix products, arithmetic and copies ran while one was open for 25% of the time, Pallas kernels for 0%

commit v1 on v0

v1 whole, which is shorter than its diff:
```python
import math

import jax
import jax.numpy as jnp
from jax import lax
from jax.experimental import pallas as pl
from jax.experimental.pallas import tpu as pltpu
from jax.sharding import PartitionSpec as P

D = 384
FF = 1536
TOK = 16
IMG = 8
CLASSES = 10
LAYERS = 2
CAP = 16
EPSILON = 1e-06
SCALE = 0.125
GELU_A = math.sqrt(2.0 / math.pi)
GELU_B = 0.044715
PACK = LAYERS * (D + FF // 8) + D // 8
CUT_A = 576

bf16 = jnp.bfloat16
f32 = jnp.float32
MESH = pl.DeviceIdType.MESH
VMEM = pl.BlockSpec(memory_space=pltpu.VMEM)
SMEM = pl.BlockSpec(memory_space=pltpu.SMEM)
ANY = pl.BlockSpec(memory_space=pl.ANY)


def mm(a, b, ca=1, cb=0):
    return lax.dot_general(a, b, (((ca,), (cb,)), ((), ())), preferred_element_type=f32)


def iota(shape, dim):
    return lax.broadcasted_iota(jnp.int32, shape, dim)


def norm(v):
    centre = v - jnp.mean(v, axis=-1, keepdims=True)
    rstd = lax.rsqrt(jnp.mean(centre * centre, axis=-1, keepdims=True) + EPSILON)
    return centre * rstd, rstd


def norm_back(v, grad):
    hat, rstd = norm(v)
    along = jnp.mean(grad * hat, axis=-1, keepdims=True)
    return rstd * (grad - jnp.mean(grad, axis=-1, keepdims=True) - hat * along)


def rounded(v):
    return v.astype(bf16).astype(f32)


def head_masks(rows):
    low = (iota((rows, 128), 1) < 64).astype(f32)
    return low.astype(bf16), (1.0 - low).astype(bf16)


def two_heads(v):
    low, high = head_masks(v.shape[0])
    return jnp.concatenate([v * low, v * high], axis=0)


def merge_heads(v):
    rows = v.shape[0] // 2
    return jnp.where(iota((rows, 128), 1) < 64, v[:rows], v[rows:])


def block_forward(l, rows, S, win, wdn):
    x = S["x"][l]
    hat, _ = norm(x)
    u1 = hat.astype(bf16)
    S["u1"][l] = u1
    for n in range(3):
        cols = slice(D * n, D * n + D)
        S["qkv"][l, :, cols] = mm(u1, win[l, :, cols]).astype(bf16)
    same = ((iota((256, 128), 0) & 127) >> 4) == (iota((256, 128), 1) >> 4)
    for g in range(rows // 128):
        part = slice(128 * g, 128 * g + 128)
        for p in range(3):
            q2 = S["qkv"][l, part, 128 * p : 128 * p + 128]
            k2 = S["qkv"][l, part, D + 128 * p : D + 128 * p + 128]
            v2 = S["qkv"][l, part, 2 * D + 128 * p : 2 * D + 128 * p + 128]
            scores = mm(two_heads(q2), k2, 1, 1) * SCALE
            scores = jnp.where(same, scores, -1e30)
            grown = jnp.exp(scores - jnp.max(scores, axis=-1, keepdims=True))
            prob = grown / jnp.sum(grown, axis=-1, keepdims=True)
            S["prob"][l, 3 * g + p] = prob
            S["att"][l, part, 128 * p : 128 * p + 128] = merge_heads(mm(prob.astype(bf16), v2)).astype(bf16)
    x1 = S["x"][l] + mm(S["att"][l], win[l, :, 3 * D : 4 * D])
    S["x1"][l] = x1
    hat, _ = norm(x1)
    u2 = hat.astype(bf16)
    S["u2"][l] = u2
    for n in range(4):
        pre = mm(u2, win[l, :, 4 * D + D * n : 5 * D + D * n])
        S["pre"][l, :, D * n : D * n + D] = pre
        bent = jnp.tanh(GELU_A * (pre + GELU_B * pre * pre * pre))
        S["h"][l, :, D * n : D * n + D] = (0.5 * pre * (1.0 + bent)).astype(bf16)
    return S["x1"][l] + mm(S["h"][l], wdn[l])


def block_backward(l, rows, S, win, wdn, dy_ref, emit_in, emit_down):
    dyb = dy_ref[...].astype(bf16)
    for n in range(4):
        cols = slice(D * n, D * n + D)
        dh = rounded(mm(dyb, wdn[l, cols, :], 1, 1))
        pre = S["pre"][l, :, cols]
        bent = jnp.tanh(GELU_A * (pre + GELU_B * pre * pre * pre))
        slope = 0.5 * (1.0 + bent) + 0.5 * pre * (1.0 - bent * bent) * GELU_A * (1.0 + 3.0 * GELU_B * pre * pre)
        S["dpre"][:, cols] = (dh * slope).astype(bf16)
        emit_down(n, S["h"][l, :, cols], dyb)
        emit_in(4 + n, S["u2"][l], S["dpre"][:, cols])
    du2 = rounded(mm(S["dpre"][...], win[l, :, 4 * D :], 1, 1))
    dx1 = dy_ref[...] + norm_back(S["x1"][l], du2)
    dy_ref[...] = dx1
    dx1b = dx1.astype(bf16)
    emit_in(3, S["att"][l], dx1b)
    datt = mm(dx1b, win[l, :, 3 * D : 4 * D], 1, 1).astype(bf16)
    S["datt"][...] = datt
    for g in range(rows // 128):
        part = slice(128 * g, 128 * g + 128)
        for p in range(3):
            cq = slice(128 * p, 128 * p + 128)
            ck = slice(D + 128 * p, D + 128 * p + 128)
            cv = slice(2 * D + 128 * p, 2 * D + 128 * p + 128)
            qs = two_heads(S["qkv"][l, part, cq])
            dos = two_heads(S["datt"][part, cq])
            prob = S["prob"][l, 3 * g + p]
            dprob = mm(dos, S["qkv"][l, part, cv], 1, 1)
            dscore = prob * (dprob - jnp.sum(prob * dprob, axis=-1, keepdims=True)) * SCALE
            dsb = dscore.astype(bf16)
            S["dqkv"][part, cq] = merge_heads(mm(dsb, S["qkv"][l, part, ck])).astype(bf16)
            S["dqkv"][part, ck] = mm(dsb, qs, 0, 0).astype(bf16)
            S["dqkv"][part, cv] = mm(prob.astype(bf16), dos, 0, 0).astype(bf16)
    for n in range(3):
        emit_in(n, S["u1"][l], S["dqkv"][:, D * n : D * n + D])
    du1 = rounded(mm(S["dqkv"][...], win[l, :, : 3 * D], 1, 1))
    dy_ref[...] = dy_ref[...] + norm_back(S["x"][l], du1)


def saved_shapes(layers, rows):
    return dict(
        x1=((layers, rows, D), f32),
        u1=((layers, rows, D), bf16),
        u2=((layers, rows, D), bf16),
        qkv=((layers, rows, 3 * D), bf16),
        prob=((layers, 3 * rows // 128, 256, 128), f32),
        att=((layers, rows, D), bf16),
        pre=((layers, rows, FF), f32),
        h=((layers, rows, FF), bf16),
    )


SAVED = tuple(saved_shapes(1, 128))


def client_forward_kernel(patches, embed, positions, win, wdn, *refs):
    S = dict(zip(("cut", "x") + SAVED, refs))
    tiled = jnp.concatenate([positions[...].astype(f32)] * IMG, axis=0)
    S["x"][0] = mm(patches[...], embed[...]) + tiled
    y = block_forward(0, 128, S, win, wdn)
    S["cut"][...] = y.astype(bf16)


def client_forward(patches, embed, positions, win, wdn):
    shapes = saved_shapes(1, 128)
    out = [jax.ShapeDtypeStruct((128, D), bf16), jax.ShapeDtypeStruct((1, 128, D), f32)]
    out += [jax.ShapeDtypeStruct(*shapes[k]) for k in SAVED]
    return pl.pallas_call(
        client_forward_kernel,
        out_shape=out,
        in_specs=[VMEM] * 5,
        out_specs=[VMEM] * len(out),
        compiler_params=pltpu.CompilerParams(vmem_limit_bytes=56 << 20),
        name="client_forward",
    )(patches, embed, positions, win, wdn)


def client_backward_kernel(grads, patches, win, wdn, *refs):
    n_in = 1 + len(SAVED)
    S = dict(zip(("x",) + SAVED, refs[:n_in]))
    packed, dy, dpre, datt, dqkv, tail, pp = refs[n_in:]
    S.update(dpre=dpre, datt=datt, dqkv=dqkv)
    dy[...] = grads[...].astype(f32)
    tail[...] = jnp.zeros_like(tail)

    def emit_in(b, u, dout):
        val = mm(dout, u, 0, 0).astype(bf16)
        for i in range(2):
            packed[2 * b + i, 0] = val[192 * i : 192 * i + 160]
            packed[2 * b + i, 1, 0:32] = val[192 * i + 160 : 192 * i + 192]

    def emit_tail(q, dout, right):
        val = mm(dout, right, 0, 0)
        for i in range(16):
            tail[i, 24 * q : 24 * q + 24] = val[24 * i : 24 * i + 24]

    block_backward(0, 128, S, win, wdn, dy, emit_in, lambda n, h, dyb: emit_tail(n, dyb, h))
    pp[...] = (iota((128, D), 1) - 192 == (iota((128, D), 0) & 15)).astype(f32).astype(bf16)
    pp[:, 0:192] = patches[...]
    emit_tail(4, dy[...].astype(bf16), pp[...])
    for i in range(16):
        packed[i, 1, 32:160] = tail[i].astype(bf16)


def client_backward(grads, patches, win, wdn, saved):
    return pl.pallas_call(
        client_backward_kernel,
        out_shape=jax.ShapeDtypeStruct((16, 2, 160, D), bf16),
        in_specs=[VMEM] * (4 + len(saved)),
        out_specs=VMEM,
        scratch_shapes=[
            pltpu.VMEM((128, D), f32),
            pltpu.VMEM((128, FF), bf16),
            pltpu.VMEM((128, D), bf16),
            pltpu.VMEM((128, 3 * D), bf16),
            pltpu.VMEM((16, 128, D), f32),
            pltpu.VMEM((128, D), bf16),
        ],
        compiler_params=pltpu.CompilerParams(vmem_limit_bytes=56 << 20),
        name="client_backward",
    )(grads, patches, win, wdn, *saved)


def server_kernel(arrived, acol, arow, labels, win, wdn, classes, losses, packed, gcut, source, *refs):
    names = ("x",) + SAVED + ("dpre", "datt", "dqkv", "dy", "cls", "sem")
    S = dict(zip(names, refs))
    me = lax.axis_index("client")
    shard, rank_in = me // 8, me % 8
    copy = pltpu.make_async_copy(classes.at[shard], S["cls"], S["sem"])
    copy.start()
    earlier = (acol[...] == arow[...]) & (iota((128, 128), 0) < iota((128, 128), 1))
    rank = jnp.sum(earlier.astype(f32), axis=0, keepdims=True)
    rank_i = rank.astype(jnp.int32)
    source[...] = arow[...] * CAP + rank_i
    chosen = (jnp.broadcast_to(arow[...], (CAP, 128)) == shard) & (
        jnp.broadcast_to(rank_i, (CAP, 128)) == iota((CAP, 128), 0)
    )
    selector = chosen.astype(f32).astype(bf16)
    label = jnp.sum(jnp.where(iota((128, IMG), 1) == rank_in, labels[...], 0), axis=1, keepdims=True)
    onehot = (label == iota((128, CLASSES), 1)).astype(f32).astype(bf16)
    hot = mm(selector, onehot)
    filled = jnp.sum(hot, axis=1, keepdims=True)
    spread = (iota((128, 2048), 0) == (iota((128, 2048), 1) >> 4)).astype(f32).astype(bf16)
    wide = mm(selector, spread).astype(bf16)
    repeat = ((iota((256, CAP), 0) >> 4) == iota((256, CAP), 1)).astype(f32).astype(bf16)
    tall = mm(repeat, wide)
    same = (iota((256, 2048), 0) & 15) == (iota((256, 2048), 1) & 15)
    S["x"][0] = mm(jnp.where(same, tall, 0.0).astype(bf16), arrived[...])

    def forward(l, carry):
        S["x"][l + 1] = block_forward(l, 256, S, win, wdn)
        return carry

    lax.fori_loop(0, LAYERS, forward, 0)
    copy.wait()
    mean = jnp.mean(S["x"][LAYERS].reshape(CAP, TOK, D), axis=1)
    hat, _ = norm(mean)
    pooled = hat.astype(bf16)
    logits = mm(pooled, S["cls"][...])
    top = jnp.max(logits, axis=1, keepdims=True)
    grown = jnp.exp(logits - top)
    total = jnp.sum(grown, axis=1, keepdims=True)
    per = (jnp.log(total) + top - jnp.sum(hot * logits, axis=1, keepdims=True)) * filled
    eye = iota((CAP, CAP), 0) == iota((CAP, CAP), 1)
    losses[...] = jnp.sum(jnp.where(eye, per, 0.0), axis=0, keepdims=True)
    dlogits = ((grown / total) * filled - hot).astype(bf16)
    gcls = mm(pooled, dlogits, 0, 0).astype(bf16)
    for r in range(8):
        packed[r, PACK - 48 :, :] = jnp.zeros((48, D), bf16)
        packed[r, PACK - 48 :, 0:CLASSES] = gcls[48 * r : 48 * r + 48]
    dpooled = rounded(mm(dlogits, S["cls"][...], 1, 1))
    dmean = norm_back(mean, dpooled) * (1.0 / TOK)
    S["dy"][...] = jnp.broadcast_to(dmean[:, None, :], (CAP, TOK, D)).reshape(CAP * TOK, D)

    def backward(i, carry):
        l = LAYERS - 1 - i
        base = 576 * l

        def emit_in(b, u, dout):
            val = mm(u, dout, 0, 0).astype(bf16)
            for r in range(8):
                packed[r, pl.ds(pl.multiple_of(base + 48 * b, 16), 48), :] = val[48 * r : 48 * r + 48]

        def emit_down(n, h, dyb):
            val = mm(h, dyb, 0, 0).astype(bf16)
            for j in range(2):
                packed[2 * n + j, pl.ds(pl.multiple_of(base + D, 16), 192), :] = val[192 * j : 192 * j + 192]

        block_backward(l, 256, S, win, wdn, S["dy"], emit_in, emit_down)
        return carry

    lax.fori_loop(0, LAYERS, backward, 0)
    gcut[...] = S["dy"][...].astype(bf16)


def server(arrived, acol, arow, labels, win, wdn, classes):
    shapes = saved_shapes(LAYERS, 256)
    return pl.pallas_call(
        server_kernel,
        out_shape=[
            jax.ShapeDtypeStruct((1, CAP), f32),
            jax.ShapeDtypeStruct((8, PACK, D), bf16),
            jax.ShapeDtypeStruct((256, D), bf16),
            jax.ShapeDtypeStruct((1, 128), jnp.int32),
        ],
        in_specs=[VMEM] * 6 + [ANY],
        out_specs=[VMEM] * 4,
        scratch_shapes=[pltpu.VMEM((LAYERS + 1, 256, D), f32)]
        + [pltpu.VMEM(*shapes[k]) for k in SAVED]
        + [
            pltpu.VMEM((256, FF), bf16),
            pltpu.VMEM((256, D), bf16),
            pltpu.VMEM((256, 3 * D), bf16),
            pltpu.VMEM((256, D), f32),
            pltpu.VMEM((D, CLASSES), bf16),
            pltpu.SemaphoreType.DMA,
        ],
        compiler_params=pltpu.CompilerParams(vmem_limit_bytes=60 << 20),
        name="server",
    )(arrived, acol, arow, labels, win, wdn, classes)


class Place:
    def __init__(self):
        me = lax.axis_index("client")
        self.me = me
        self.c, self.y, self.z, self.x = me % 2, me // 2 % 4, me // 8 % 4, me // 32
        self.r, self.group = me % 8, me // 8 * 8
        self.partner = me + 1 - 2 * self.c
        self.yp, self.ym = self.at(0, 0, 1), self.at(0, 0, 3)
        self.xp, self.xm = self.at(1, 0, 0), self.at(3, 0, 0)
        self.zp, self.zm = self.at(0, 1, 0), self.at(0, 3, 0)

    def at(self, dx, dz, dy):
        x, z, y = (self.x + dx) % 4, (self.z + dz) % 4, (self.y + dy) % 4
        return ((x * 4 + z) * 4 + y) * 2 + self.c

    def greet(self, group, plane):
        peers = []
        if group:
            peers += [self.group + (self.r + i) % 8 for i in range(1, 8)]
        if plane:
            peers += [self.xp, self.xm, self.zp, self.zm]
        barrier = pltpu.get_barrier_semaphore()
        for peer in peers:
            pl.semaphore_signal(barrier, inc=1, device_id=(peer,), device_id_type=MESH)
        pl.semaphore_wait(barrier, len(peers))


class Wire:
    def __init__(self, send_sem, recv_sem):
        self.send_sem, self.recv_sem, self.sent = send_sem, recv_sem, []

    def make(self, src, dst, k, device):
        return pltpu.make_async_remote_copy(
            src_ref=src,
            dst_ref=dst,
            send_sem=self.send_sem.at[k],
            recv_sem=self.recv_sem.at[k],
            device_id=(device,),
            device_id_type=MESH,
        )

    def send(self, src, dst, k, device):
        copy = self.make(src, dst, k, device)
        copy.start()
        self.sent.append(copy)

    def wait(self, landed, k, device):
        self.make(landed, landed, k, device).wait_recv()

    def finish(self):
        for copy in self.sent:
            copy.wait_send()


def plane_gather(wire, place, buf, count, k0):
    half, quarter = count // 2, count // 4
    x, z = place.x, place.z
    xm, xp, zm, zp = (x + 3) % 4, (x + 1) % 4, (z + 3) % 4, (z + 1) % 4
    xo, zo = (x + 2) % 4, (z + 2) % 4
    X, XA, XB = pl.ds(0, half), pl.ds(0, quarter), pl.ds(quarter, quarter)
    Z, ZA, ZB = pl.ds(half, half), pl.ds(half, quarter), pl.ds(half + quarter, quarter)

    def both(ref, k, device):
        wire.send(ref, ref, k0 + k, device)

    def first():
        both(buf.at[x, z, X], 0, place.xp)
        both(buf.at[x, z, X], 1, place.xm)
        both(buf.at[x, z, Z], 2, place.zp)
        both(buf.at[x, z, Z], 3, place.zm)

    def second():
        wire.wait(buf.at[xm, z, X], k0 + 0, place.xm)
        both(buf.at[xm, z, XA], 4, place.xp)
        wire.wait(buf.at[xp, z, X], k0 + 1, place.xp)
        both(buf.at[xp, z, XB], 5, place.xm)
        wire.wait(buf.at[x, zm, Z], k0 + 2, place.zm)
        both(buf.at[x, zm, ZA], 6, place.zp)
        wire.wait(buf.at[x, zp, Z], k0 + 3, place.zp)
        both(buf.at[x, zp, ZB], 7, place.zm)

    def third():
        wire.wait(buf.at[xo, z, XA], k0 + 4, place.xm)
        wire.wait(buf.at[xo, z, XB], k0 + 5, place.xp)
        both(buf.at[:, z, X], 8, place.zp)
        both(buf.at[:, z, X], 9, place.zm)
        wire.wait(buf.at[x, zo, ZA], k0 + 6, place.zm)
        wire.wait(buf.at[x, zo, ZB], k0 + 7, place.zp)
        both(buf.at[x, :, Z], 10, place.xp)
        both(buf.at[x, :, Z], 11, place.xm)

    def fourth():
        wire.wait(buf.at[:, zm, X], k0 + 8, place.zm)
        both(buf.at[0:2, zm, X], 12, place.zp)
        wire.wait(buf.at[:, zp, X], k0 + 9, place.zp)
        both(buf.at[2:4, zp, X], 13, place.zm)
        wire.wait(buf.at[xm, :, Z], k0 + 10, place.xm)
        both(buf.at[xm, 0:2, Z], 14, place.xp)
        wire.wait(buf.at[xp, :, Z], k0 + 11, place.xp)
        both(buf.at[xp, 2:4, Z], 15, place.xm)

    def fifth():
        wire.wait(buf.at[0:2, zo, X], k0 + 12, place.zm)
        wire.wait(buf.at[2:4, zo, X], k0 + 13, place.zp)
        wire.wait(buf.at[xo, 0:2, Z], k0 + 14, place.xm)
        wire.wait(buf.at[xo, 2:4, Z], k0 + 15, place.xp)

    return first, second, third, fourth, fifth


def gather_kernel(cut, win_s, wdn_s, arrived, win, wdn, send_sem, recv_sem, local_sem):
    place = Place()
    x, z, y, r = place.x, place.z, place.y, place.r
    place.greet(True, True)
    wire = Wire(send_sem, recv_sem)
    for i in range(1, 8):
        j = (r + i) % 8
        wire.send(cut.at[j], arrived.at[x, z, r], i, place.group + j)
    arrived[x, z, r] = cut[r]

    def owner(dy, other=False):
        c = 1 - place.c if other else place.c
        return (y + dy) % 4 * 2 + c

    def window(l, down, rank, part):
        if down:
            low, size = {None: (0, 192), 0: (0, 96), 1: (96, 96)}[part]
            return wdn.at[l, pl.ds(pl.multiple_of(rank * 192 + low, 16), size), :]
        cols = {None: pl.ds(0, 3072), 0: pl.ds(0, 1536), 1: pl.ds(1536, 1536)}[part]
        return win.at[l, pl.ds(pl.multiple_of(rank * 48, 16), 48), cols]

    local = []
    pieces = [(l, down) for l in range(LAYERS) for down in (False, True)]
    base = {piece: 8 + 9 * n for n, piece in enumerate(pieces)}
    for n, piece in enumerate(pieces):
        l, down = piece
        shard = (wdn_s if down else win_s).at[l]
        here = window(l, down, r, None)
        wire.send(shard, here, base[piece] + 0, place.yp)
        wire.send(shard, here, base[piece] + 1, place.ym)
        wire.send(shard, here, base[piece] + 4, place.partner)
        copy = pltpu.make_async_copy(shard, here, local_sem.at[n])
        copy.start()
        local.append(copy)

    def forward(piece):
        l, down = piece
        b = base[piece]
        left, right = owner(3), owner(1)
        wire.wait(window(l, down, left, None), b + 0, place.ym)
        half = window(l, down, left, 0)
        wire.send(half, half, b + 2, place.yp)
        whole = window(l, down, left, None)
        wire.send(whole, whole, b + 5, place.partner)
        wire.wait(window(l, down, right, None), b + 1, place.yp)
        half = window(l, down, right, 1)
        wire.send(half, half, b + 3, place.ym)
        whole = window(l, down, right, None)
        wire.send(whole, whole, b + 6, place.partner)

    def across(piece):
        l, down = piece
        b = base[piece]
        far = owner(2)
        for part, device in ((0, place.ym), (1, place.yp)):
            half = window(l, down, far, part)
            wire.wait(half, b + 2 + part, device)
            wire.send(half, half, b + 7 + part, place.partner)

    def settle(piece):
        l, down = piece
        b = base[piece]
        wire.wait(window(l, down, owner(0, True), None), b + 4, place.partner)
        wire.wait(window(l, down, owner(3, True), None), b + 5, place.partner)
        wire.wait(window(l, down, owner(1, True), None), b + 6, place.partner)
        for part in range(2):
            wire.wait(window(l, down, owner(2, True), part), b + 7 + part, place.partner)

    first, second, third, fourth, fifth = plane_gather(wire, place, arrived, IMG, 44)
    for i in range(1, 8):
        j = (r - i + 8) % 8
        wire.wait(arrived.at[x, z, j], i, place.group + j)
    first()
    second()
    forward(pieces[0])
    third()
    forward(pieces[1])
    fourth()
    across(pieces[0])
    forward(pieces[2])
    fifth()
    across(pieces[1])
    forward(pieces[3])
    across(pieces[2])
    across(pieces[3])
    for piece in pieces:
        settle(piece)
    for copy in local:
        copy.wait()
    wire.finish()


def gather(cut, win_s, wdn_s):
    return pl.pallas_call(
        gather_kernel,
        out_shape=[
            jax.ShapeDtypeStruct((4, 4, IMG, TOK, D), bf16),
            jax.ShapeDtypeStruct((LAYERS, D, 4 * D + FF), bf16),
            jax.ShapeDtypeStruct((LAYERS, FF, D), bf16),
        ],
        in_specs=[VMEM] * 3,
        out_specs=[VMEM, ANY, ANY],
        scratch_shapes=[
            pltpu.SemaphoreType.DMA((60,)),
            pltpu.SemaphoreType.DMA((60,)),
            pltpu.SemaphoreType.DMA((4,)),
        ],
        compiler_params=pltpu.CompilerParams(collective_id=0, has_side_effects=True, vmem_limit_bytes=16 << 20),
        name="gather",
    )(cut, win_s, wdn_s)


def add_rows(start, stop, step, body):
    def run(i, carry):
        body(pl.ds(pl.multiple_of(start + i * step, 16), step))
        return carry

    lax.fori_loop(0, (stop - start) // step, run, 0)


def reduce_kernel(packed, gcut, source, gin, gdn, gcls, own, swapped, mine, from_m, from_p, fin_p, fin_m, plane, picked, acc, send_sem, recv_sem):
    place = Place()
    x, z, y, c, r = place.x, place.z, place.y, place.c, place.r
    place.greet(True, True)
    wire = Wire(send_sem, recv_sem)
    A, B = pl.ds(0, CUT_A), pl.ds(CUT_A, PACK - CUT_A)

    def row(k, core):
        return (y + k) % 4 * 2 + core

    for k in (2, 1, 3, 0):
        wire.send(packed.at[row(k, 1 - c)], swapped.at[k], k, place.partner)
    plane[x, z] = gcut[...]
    first, second, third, fourth, fifth = plane_gather(wire, place, plane, CAP, 16)
    first()

    def combine(k):
        wire.wait(swapped.at[k], k, place.partner)

        def body(rows):
            total = packed[row(k, c), rows, :].astype(f32) + swapped[k, rows, :].astype(f32)
            mine[k, rows, :] = total.astype(bf16)

        add_rows(0, PACK, 48, body)

    combine(2)
    wire.send(mine.at[2, A], from_m, 4, place.yp)
    wire.send(mine.at[2, B], from_p, 5, place.ym)
    combine(1)
    wire.send(mine.at[1, B], fin_p.at[B], 6, place.yp)
    combine(3)
    wire.send(mine.at[3, A], fin_m.at[A], 7, place.ym)
    second()
    wire.wait(swapped.at[0], 0, place.partner)

    def start_own(rows):
        acc[rows, :] = packed[row(0, c), rows, :].astype(f32) + swapped[0, rows, :].astype(f32)

    add_rows(0, PACK, 48, start_own)
    third()
    wire.wait(from_m, 4, place.ym)

    def add_a(rows):
        mine[1, rows, :] = (mine[1, rows, :].astype(f32) + from_m[rows, :].astype(f32)).astype(bf16)

    add_rows(0, CUT_A, 48, add_a)
    wire.send(mine.at[1, A], fin_p.at[A], 8, place.yp)
    wire.wait(from_p, 5, place.yp)

    def add_b(i, carry):
        here = pl.ds(pl.multiple_of(i * 48, 16), 48)
        rows = pl.ds(pl.multiple_of(CUT_A + i * 48, 16), 48)
        mine[3, rows, :] = (mine[3, rows, :].astype(f32) + from_p[here, :].astype(f32)).astype(bf16)
        return carry

    lax.fori_loop(0, (PACK - CUT_A) // 48, add_b, 0)
    wire.send(mine.at[3, B], fin_m.at[B], 9, place.ym)
    fourth()
    fifth()
    for m in range(8):
        at = source[0, place.group + m]
        piece = plane[at // 64, at // 16 % 4, at % 16]
        picked[m] = piece
    own[r] = picked[r]
    for i in range(1, 8):
        m = (r + i) % 8
        wire.send(picked.at[m], own.at[r], 32 + i, place.group + m)
    wire.wait(fin_p.at[B], 6, place.ym)
    wire.wait(fin_m.at[A], 7, place.yp)
    wire.wait(fin_p.at[A], 8, place.ym)
    wire.wait(fin_m.at[B], 9, place.yp)

    def total(first_row, rows):
        at = pl.ds(first_row, rows)
        return acc[at, :] + fin_p[at, :].astype(f32) + fin_m[at, :].astype(f32)

    for l in range(LAYERS):
        for b in range(8):
            gin[l, :, D * b : D * b + D] = total(576 * l + 48 * b, 48)
        for b in range(4):
            gdn[l, 48 * b : 48 * b + 48, :] = total(576 * l + D + 48 * b, 48)
    gcls[...] = total(PACK - 48, 48)[:, 0:CLASSES]
    for i in range(1, 8):
        j = (r - i + 8) % 8
        wire.wait(own.at[j], 32 + i, place.group + j)
    wire.finish()


def reduce(packed, gcut, source):
    return pl.pallas_call(
        reduce_kernel,
        out_shape=[
            jax.ShapeDtypeStruct((LAYERS, 48, 4 * D + FF), f32),
            jax.ShapeDtypeStruct((LAYERS, 192, D), f32),
            jax.ShapeDtypeStruct((48, CLASSES), f32),
            jax.ShapeDtypeStruct((IMG, TOK, D), bf16),
        ],
        in_specs=[VMEM, VMEM, SMEM],
        out_specs=[VMEM] * 4,
        scratch_shapes=[
            pltpu.VMEM((4, PACK, D), bf16),
            pltpu.VMEM((4, PACK, D), bf16),
            pltpu.VMEM((CUT_A, D), bf16),
            pltpu.VMEM((PACK - CUT_A, D), bf16),
            pltpu.VMEM((PACK, D), bf16),
            pltpu.VMEM((PACK, D), bf16),
            pltpu.VMEM((4, 4, CAP, TOK, D), bf16),
            pltpu.VMEM((IMG, TOK, D), bf16),
            pltpu.VMEM((PACK, D), f32),
            pltpu.SemaphoreType.DMA((40,)),
            pltpu.SemaphoreType.DMA((40,)),
        ],
        compiler_params=pltpu.CompilerParams(collective_id=1, has_side_effects=True, vmem_limit_bytes=56 << 20),
        name="reduce",
    )(packed, gcut, source)


def client_reduce_kernel(packed, out, swapped, mine, hop_x, hop_z, fin_x, fin_z, half_x, half_z, hop2_x, hop2_z, fin2_x, fin2_z, last, ring, send_sem, recv_sem):
    place = Place()
    x, z, y, c, r = place.x, place.z, place.y, place.c, place.r
    place.greet(True, True)
    wire = Wire(send_sem, recv_sem)
    for q in range(4):
        wire.send(packed.at[pl.ds(4 * q, 4), 1 - c], swapped.at[pl.ds(4 * q, 4)], q, place.partner)
    for q in range(4):
        wire.wait(swapped.at[pl.ds(4 * q, 4)], q, place.partner)
        for i in range(4):
            at = 4 * q + i
            mine[q, i] = (packed[at, c].astype(f32) + swapped[at].astype(f32)).astype(bf16)

    X, Z = pl.ds(0, 80), pl.ds(80, 80)

    def src_x(k, part=None):
        to = (x + k) % 4
        if part is None:
            return mine.at[to, :, X]
        return mine.at[to, pl.ds(2 * part, 2), X]

    def src_z(k, part=None):
        to = (z + k) % 4
        if part is None:
            return mine.at[:, to, Z]
        return mine.at[pl.ds(2 * part, 2), to, Z]

    def ring_one(src, hop, fin, up, down, k0):
        wire.send(src(2, 0), hop.at[0], k0, up)
        wire.send(src(2, 1), hop.at[1], k0 + 1, down)
        wire.send(src(1, 1), fin.at[0, pl.ds(2, 2)], k0 + 2, up)
        wire.send(src(3, 0), fin.at[1, pl.ds(0, 2)], k0 + 3, down)

    def ring_two(src, load, hop, fin, up, down, k0):
        wire.wait(hop.at[0], k0, down)
        load(1, 0, hop)
        wire.send(src(1, 0), fin.at[0, pl.ds(0, 2)], k0 + 4, up)
        wire.wait(hop.at[1], k0 + 1, up)
        load(3, 1, hop)
        wire.send(src(3, 1), fin.at[1, pl.ds(2, 2)], k0 + 5, down)

    def ring_three(fin, up, down, k0):
        wire.wait(fin.at[0, pl.ds(2, 2)], k0 + 2, down)
        wire.wait(fin.at[1, pl.ds(0, 2)], k0 + 3, up)
        wire.wait(fin.at[0, pl.ds(0, 2)], k0 + 4, down)
        wire.wait(fin.at[1, pl.ds(2, 2)], k0 + 5, up)

    def load_x(k, part, hop):
        to = (x + k) % 4
        for i in range(2):
            at = 2 * part + i
            mine[to, at, 0:80] = (mine[to, at, 0:80].astype(f32) + hop[part, i].astype(f32)).astype(bf16)

    def load_z(k, part, hop):
        to = (z + k) % 4
        for i in range(2):
            at = 2 * part + i
            mine[at, to, 80:160] = (mine[at, to, 80:160].astype(f32) + hop[part, i].astype(f32)).astype(bf16)

    ring_one(src_x, hop_x, fin_x, place.xp, place.xm, 4)
    ring_one(src_z, hop_z, fin_z, place.zp, place.zm, 10)
    ring_two(src_x, load_x, hop_x, fin_x, place.xp, place.xm, 4)
    ring_two(src_z, load_z, hop_z, fin_z, place.zp, place.zm, 10)
    ring_three(fin_x, place.xp, place.xm, 4)
    for i in range(4):
        half_x[i] = (mine[x, i, 0:80].astype(f32) + fin_x[0, i].astype(f32) + fin_x[1, i].astype(f32)).astype(bf16)
    ring_three(fin_z, place.zp, place.zm, 10)
    for i in range(4):
        half_z[i] = (mine[i, z, 80:160].astype(f32) + fin_z[0, i].astype(f32) + fin_z[1, i].astype(f32)).astype(bf16)

    for k in range(1, 4):
        wire.send(half_x.at[(z + k) % 4], fin2_x.at[k - 1], 15 + k, place.at(0, k, 0))
        wire.send(half_z.at[(x + k) % 4], fin2_z.at[k - 1], 18 + k, place.at(k, 0, 0))
    for k in range(1, 4):
        wire.wait(fin2_x.at[k - 1], 15 + k, place.at(0, 4 - k, 0))
        wire.wait(fin2_z.at[k - 1], 18 + k, place.at(4 - k, 0, 0))
    top = half_x[z].astype(f32)
    low = half_z[x].astype(f32)
    for k in range(3):
        top = top + fin2_x[k].astype(f32)
        low = low + fin2_z[k].astype(f32)
    last[y, c, 0:80] = top.astype(bf16)
    last[y, c, 80:160] = low.astype(bf16)

    wire.send(last.at[y, c], last.at[y, c], 22, place.yp)
    wire.send(last.at[y, c], last.at[y, c], 23, place.ym)
    wire.send(last.at[y, c], last.at[y, c], 24, place.partner)
    left, right, far = (y + 3) % 4, (y + 1) % 4, (y + 2) % 4
    lo, hi = pl.ds(0, 80), pl.ds(80, 80)
    wire.wait(last.at[left, c], 22, place.ym)
    wire.send(last.at[left, c, lo], last.at[left, c, lo], 25, place.yp)
    wire.send(last.at[left, c], last.at[left, c], 27, place.partner)
    wire.wait(last.at[right, c], 23, place.yp)
    wire.send(last.at[right, c, hi], last.at[right, c, hi], 26, place.ym)
    wire.send(last.at[right, c], last.at[right, c], 28, place.partner)
    wire.wait(last.at[far, c, lo], 25, place.ym)
    wire.send(last.at[far, c, lo], last.at[far, c, lo], 29, place.partner)
    wire.wait(last.at[far, c, hi], 26, place.yp)
    wire.send(last.at[far, c, hi], last.at[far, c, hi], 30, place.partner)
    o = 1 - c
    wire.wait(last.at[y, o], 24, place.partner)
    wire.wait(last.at[left, o], 27, place.partner)
    wire.wait(last.at[right, o], 28, place.partner)
    wire.wait(last.at[far, o, lo], 29, place.partner)
    wire.wait(last.at[far, o, hi], 30, place.partner)
    for core in range(2):
        total = last[0, core].astype(f32)
        for k in range(1, 4):
            total = total + last[k, core].astype(f32)
        ring[160 * core : 160 * core + 160, :] = total
    col, line = iota((320, 128), 1), iota((320, 128), 0)
    wanted = jnp.where(
        col < 24,
        24 * r + col,
        jnp.where(col < 36, 192 + 24 * ((col - 24) // 3) + 3 * r + (col - 24) % 3, 288 + 3 * r + col - 36),
    )
    pick = ((line == wanted) & (col < 39)).astype(f32)
    out[...] = lax.dot_general(
        ring[...], pick, (((0,), (0,)), ((), ())), precision=lax.Precision.HIGHEST, preferred_element_type=f32
    )
    wire.finish()


def client_reduce(packed):
    return pl.pallas_call(
        client_reduce_kernel,
        out_shape=jax.ShapeDtypeStruct((D, 128), f32),
        in_specs=[VMEM],
        out_specs=VMEM,
        scratch_shapes=[
            pltpu.VMEM((16, 160, D), bf16),
            pltpu.VMEM((4, 4, 160, D), bf16),
            pltpu.VMEM((2, 2, 80, D), bf16),
            pltpu.VMEM((2, 2, 80, D), bf16),
            pltpu.VMEM((2, 4, 80, D), bf16),
            pltpu.VMEM((2, 4, 80, D), bf16),
            pltpu.VMEM((4, 80, D), bf16),
            pltpu.VMEM((4, 80, D), bf16),
            pltpu.VMEM((8, 128), f32),
            pltpu.VMEM((8, 128), f32),
            pltpu.VMEM((3, 80, D), bf16),
            pltpu.VMEM((3, 80, D), bf16),
            pltpu.VMEM((4, 2, 160, D), bf16),
            pltpu.VMEM((320, D), f32),
            pltpu.SemaphoreType.DMA((32,)),
            pltpu.SemaphoreType.DMA((32,)),
        ],
        compiler_params=pltpu.CompilerParams(collective_id=2, has_side_effects=True, vmem_limit_bytes=56 << 20),
        name="client_reduce",
    )(packed)


def per_device(patches, labels, assign, patch_embed, positions, client_in, client_down, server_in, server_down, classifier):
    win_c, wdn_c = client_in[None], client_down[None]
    cut, *saved = client_forward(patches, patch_embed, positions, win_c, wdn_c)
    arrived, win, wdn = gather(cut.reshape(IMG, TOK, D), server_in, server_down)
    losses, packed, gcut, source = server(
        arrived.reshape(2048, D), assign, assign.reshape(1, 128), labels.reshape(128, IMG), win, wdn, classifier
    )
    gin, gdn, gcls, own = reduce(packed, gcut.reshape(CAP, TOK, D), source)
    packed_c = client_backward(own.reshape(128, D), patches, win_c, wdn_c, saved)
    cols = client_reduce(packed_c)
    grad_down = jnp.concatenate([cols[:, 24 + 3 * q : 27 + 3 * q] for q in range(4)], axis=0)
    return (
        losses,
        cols[:192, 36:39],
        cols[192:208, 36:39],
        cols[:, :24],
        grad_down,
        gin,
        gdn,
        gcls,
    )


def solution(mesh):
    in_specs = (
        P("client", None),
        P(),
        P(),
        P(),
        P(),
        P(),
        P(),
        P(None, "client", None),
        P(None, "client", None),
        P(),
    )
    out_specs = (
        P("client", None),
        P(None, "client"),
        P(None, "client"),
        P(None, "client"),
        P(None, "client"),
        P(None, "client", None),
        P(None, "client", None),
        P("client", None),
    )
    return jax.shard_map(per_device, mesh=mesh, in_specs=in_specs, out_specs=out_specs, check_vma=False)
```

time: 704 us -> 185 us (0.26); the launches traced: 693 us -> 182 us
  waiting for transfers between devices: 214 us -> 0 us
  Pallas kernels: 0 us -> 158 us
  local copies, waits for them, and re-layouts: 160 us -> 22.6 us
  other arithmetic: 127 us -> 0.65 us
  blocking collectives: 70.7 us -> 0 us
  matrix products: 59.3 us -> 0 us
  starting transfers between devices: 44.4 us -> 0 us
  between operations: 17.1 us -> 0.73 us
    ppermute x9 -> x0, waiting for transfers between devices: 165 us -> none  [partner_2(): return lax.ppermute(block, axis, route)]
    pallas_call x0 -> x6, Pallas kernels: none -> 158 us  [the longest x1 43.6 us: reduce(): pl.pallas_call(reduce_kernel, out_shape=[jax.ShapeDtypeStruct((LAYERS, 48...]
    unnamed x1 -> x0, blocking collectives: 70.7 us -> none
    dot_general x62 -> x0, matrix products: 59.3 us -> none  [the longest x9 14.4 us: encoder_block(): jnp.dot(normed, weight_in[:, :3 * model_width], preferred_element_type=jn...]
    unnamed x2 -> x0, waiting for transfers between devices: 49.1 us -> none
    select_n x8 -> x0, other arithmetic: 34.6 us -> none  [the longest x6 33.1 us: gather_group(): jnp.where(upper_half == 0, jnp.concatenate([stacked, partner], 0), jnp.co...]
    concatenate x3 -> x1, other arithmetic: 31.7 us -> 0.65 us  [per_device(): jnp.concatenate([cols[:, 24 + 3 * q:27 + 3 * q] for q in range(4)], axis=0)]
    reshape x16 -> x1, local copies, waits for them, and re-layouts: 27.7 us -> 1.39 us  [per_device(): labels.reshape(128, IMG)]
  transfers between devices with their start and end apart: 12 -> 0, of which waited for: 7 -> 0; matrix products, arithmetic and copies ran while one was open for 25% -> 0% of each run, Pallas kernels for 0% -> 0%
where the time goes in v1:
time: 185 us; the launch traced here: 182 us
  Pallas kernels  158 us (85%)
  local copies, waits for them, and re-layouts  22.6 us (12%)
    pallas_call x1, Pallas kernels, reduce(): pl.pallas_call(reduce_kernel, out_shape=[jax.ShapeDtypeStruct((LAYERS, 48...  43.6 us
    pallas_call x1, Pallas kernels, gather(): pl.pallas_call(gather_kernel, out_shape=[jax.ShapeDtypeStruct((4, 4, IMG,...  39.2 us
    pallas_call x1, Pallas kernels, client_reduce(): pl.pallas_call(client_reduce_kernel, out_shape=jax.ShapeDtypeStruct((D, 1...  34.9 us
    pallas_call x1, Pallas kernels, server(): pl.pallas_call(server_kernel, out_shape=[jax.ShapeDtypeStruct((1, CAP), f...  25.9 us
    unnamed x25, local copies, waits for them, and re-layouts  17.3 us
    pallas_call x1, Pallas kernels, client_backward(): pl.pallas_call(client_backward_kernel, out_shape=jax.ShapeDtypeStruct((16...  9.14 us
    pallas_call x1, Pallas kernels, client_forward(): pl.pallas_call(client_forward_kernel, out_shape=out, in_specs=[VMEM] * 5,...  5.35 us

profile of v1, /device:TPU:0, one launch (start us, length us, event | category | flops | bytes accessed | tf_op | source)
XLA Modules:
  0.0 182.0 jit_solution(16286856632554471724)
XLA Ops:
  0.6 1.5 copy.36.patches
  2.2 1.4 reshape.37.labels
  3.5 1.4 copy.37.acol
  4.9 2.5 %copy.38.classes = bf16[16,384,10]{2,1,0:T(8,128)(2,1)} copy(bf16[16,384,10]{1,0,2:T(8,128)(2,1)} %param.19) | data formatting | bytes 245760 | tf_op args[9]
  7.4 5.3 %client_forward.1 = (bf16[128,384]{1,0:T(8,128)(2,1)}, f32[1,128,384]{2,1,0:T(8,128)}, f32[1,128,384]{2,1,0:T(8,128)}, bf16[1,128,384]{2,1,0:T(8,128)(2,1)}, bf1...) custom-call(bf16[128,192]{1,0:T(8,128)(2,1)} %copy.36.patches, ...), custom_call_target="tpu_custom_call" | custom-call | tf_op jit(solution)/shard_map/client_forward/pallas_call | solution.py:172
  12.8 0.9 copy-done.5
  13.7 39.2 %gather.1 = (bf16[4,4,8,16,384]{4,3,2,1,0:T(8,128)(2,1)S(1)}, bf16[2,384,3072]{2,1,0:T(8,128)(2,1)S(1)}, bf16[2,1536,384]{2,1,0:T(8,128)(2,1)S(1)}) custom-call(bf16[8,16,384]{2,1,0:T(8,128)(2,1)S(1)} %bitcast.9, bf16[2,48,3072]{2,1,0:T(8,128)(2,1)S(1)} %copy-done.3, bf16[2,192,384]{2,1,0:T(8,128)(2,1)S(1)} %copy-done.4), custom_call_target="tpu_custom_call" | custom-call | tf_op jit(solution)/shard_map/gather/pallas_call | solution.py:530
  52.9 2.1 %copy-done = bf16[2,384,3072]{2,1,0:T(8,128)(2,1)} copy-done((bf16[2,384,3072]{2,1,0:T(8,128)(2,1)}, bf16[2,384,3072]{2,1,0:T(8,128)(2,1)S(1)}, u32[]{:S(2)}) %copy-start) | copy-done | bytes 4718616
  55.1 1.5 copy-done.1
  56.5 1.2 copy-done.2
  57.7 25.9 %server.1 = (f32[1,16]{1,0:T(1,128)}, bf16[8,1200,384]{2,1,0:T(8,128)(2,1)}, bf16[256,384]{1,0:T(8,128)(2,1)}, s32[1,128]{1,0:T(1,128)}) custom-call(bf16[2048,384]{1,0:T(8,128)(2,1)} %bitcast.8, s32[128,1]{1,0:T(8,128)} %copy.37.acol, s32[1,128]{1,0:T(1,128)} %bitcast.17, s32[128,8]{1,0:T(8,128)} %reshape.37.labels, bf16[2,384,3072]{2,1,0:T(8,128)(2,1)} %copy-done, ...), custom_call_target="tpu_custom_call" | custom-call | tf_op jit(solution)/shard_map/server/pallas_call | solution.py:302
  83.6 43.6 %reduce.1 = (f32[2,48,3072]{2,1,0:T(8,128)}, f32[2,192,384]{2,1,0:T(8,128)}, f32[48,10]{1,0:T(8,128)}, bf16[8,16,384]{2,1,0:T(8,128)(2,1)}) custom-call(bf16[8,1200,384]{2,1,0:T(8,128)(2,1)} %get-tuple-element.34.packed, bf16[16,16,384]{2,1,0:T(8,128)(2,1)} %bitcast.15, s32[1,128]{1,0:T(1,128)} %get-tuple-element.36.source), custom_call_target="tpu_custom_call" | custom-call | tf_op jit(solution)/shard_map/reduce/pallas_call | solution.py:646
  127.2 1.4 copy.47
  128.6 9.1 %client_backward.1.packed = bf16[16,2,160,384]{3,2,1,0:T(8,128)(2,1)} custom-call(bf16[128,384]{1,0:T(8,128)(2,1)} %bitcast.16, bf16[128,192]{1,0:T(8,128)(2,1)} %copy.36.patches, bf16[1,384,3072]{2,1,0:T(8,128)(2,1)} %bitcast.11, bf16[1,1536,384]{2,1,0:T(8,128)(2,1)} %bitcast.14, f32[1,128,384]{2,1,0:T(8,128)} %get-tuple-element.38.refs_0_, ...), custom_call_target="tpu_custom_call" | custom-call | tf_op jit(solution)/shard_map/client_backward/pallas_call | solution.py:210
  137.8 34.9 %client_reduce.1 = f32[384,128]{1,0:T(8,128)} custom-call(bf16[16,2,160,384]{3,2,1,0:T(8,128)(2,1)} %client_backward.1.packed), custom_call_target="tpu_custom_call" | custom-call | tf_op jit(solution)/shard_map/client_reduce/pallas_call | solution.py:798
  172.7 0.9 slice.22
  173.5 0.7 copy.45
  174.2 1.6 copy.46
  175.8 1.0 slice.21
  176.8 0.7 copy.44
  177.5 1.6 fusion
  179.6 0.6 pad_maximum_fusion
  180.2 1.0 copy.50
  181.2 0.8 copy.51
  (16 shorter events, 0.5 us)
Async XLA Ops:
  4.9 7.9 %copy-start.3 = (bf16[2,48,3072]{2,1,0:T(8,128)(2,1)S(1)}, bf16[2,48,3072]{2,1,0:T(8,128)(2,1)}, u32[]{:S(2)}) copy-start(bf16[2,48,3072]{2,1,0:T(8,128)(2,1)} %win_s.1) | copy-start | bytes 1769476
  4.9 7.9 %copy-start.4 = (bf16[2,192,384]{2,1,0:T(8,128)(2,1)S(1)}, bf16[2,192,384]{2,1,0:T(8,128)(2,1)}, u32[]{:S(2)}) copy-start(bf16[2,192,384]{2,1,0:T(8,128)(2,1)} %wdn_s.1) | copy-start | bytes 884740
  12.8 0.9 copy-start.5
  52.9 2.2 %copy-start = (bf16[2,384,3072]{2,1,0:T(8,128)(2,1)}, bf16[2,384,3072]{2,1,0:T(8,128)(2,1)S(1)}, u32[]{:S(2)}) copy-start(bf16[2,384,3072]{2,1,0:T(8,128)(2,1)S(1)} %get-tuple-element.31.win) | copy-start | bytes 14155780
  55.0 1.5 copy-start.1
  56.5 1.2 copy-start.2
  172.6 7.6 %copy-start.6 = (f32[2,48,3072]{2,1,0:T(8,128)S(1)}, f32[2,48,3072]{2,1,0:T(8,128)}, u32[]{:S(2)}) copy-start(f32[2,48,3072]{2,1,0:T(8,128)} %get-tuple-element.91) | copy-start | bytes 3538948
  177.5 3.7 %copy-start.7 = (f32[2,192,384]{2,1,0:T(8,128)S(1)}, f32[2,192,384]{2,1,0:T(8,128)}, u32[]{:S(2)}) copy-start(f32[2,192,384]{2,1,0:T(8,128)} %get-tuple-element.92) | copy-start | bytes 1769476

commit v2 on v1

v2 whole, which is shorter than its diff:
```python
import math

import jax
import jax.numpy as jnp
from jax import lax
from jax.experimental import pallas as pl
from jax.experimental.pallas import tpu as pltpu
from jax.sharding import PartitionSpec as P

D = 384
FF = 1536
TOK = 16
IMG = 8
CLASSES = 10
LAYERS = 2
CAP = 16
EPSILON = 1e-06
SCALE = 0.125
GELU_A = math.sqrt(2.0 / math.pi)
GELU_B = 0.044715
PACK = LAYERS * (D + FF // 8) + D // 8
CUT_A = 576
MAIN = 96
TAIL = 80
BLOCK = MAIN + TAIL

bf16 = jnp.bfloat16
f32 = jnp.float32
MESH = pl.DeviceIdType.MESH
VMEM = pl.BlockSpec(memory_space=pltpu.VMEM)
SMEM = pl.BlockSpec(memory_space=pltpu.SMEM)
ANY = pl.BlockSpec(memory_space=pl.ANY)


def mm(a, b, ca=1, cb=0):
    return lax.dot_general(a, b, (((ca,), (cb,)), ((), ())), preferred_element_type=f32)


def iota(shape, dim):
    return lax.broadcasted_iota(jnp.int32, shape, dim)


def norm(v):
    centre = v - jnp.mean(v, axis=-1, keepdims=True)
    rstd = lax.rsqrt(jnp.mean(centre * centre, axis=-1, keepdims=True) + EPSILON)
    return centre * rstd, rstd


def norm_back(v, grad):
    hat, rstd = norm(v)
    along = jnp.mean(grad * hat, axis=-1, keepdims=True)
    return rstd * (grad - jnp.mean(grad, axis=-1, keepdims=True) - hat * along)


def rounded(v):
    return v.astype(bf16).astype(f32)


def head_masks(rows):
    low = (iota((rows, 128), 1) < 64).astype(f32)
    return low.astype(bf16), (1.0 - low).astype(bf16)


def two_heads(v):
    low, high = head_masks(v.shape[0])
    return jnp.concatenate([v * low, v * high], axis=0)


def merge_heads(v):
    rows = v.shape[0] // 2
    return jnp.where(iota((rows, 128), 1) < 64, v[:rows], v[rows:])


def block_forward(l, rows, S, win, wdn):
    x = S["x"][l]
    hat, _ = norm(x)
    u1 = hat.astype(bf16)
    S["u1"][l] = u1
    for n in range(3):
        cols = slice(D * n, D * n + D)
        S["qkv"][l, :, cols] = mm(u1, win[l, :, cols]).astype(bf16)
    same = ((iota((256, 128), 0) & 127) >> 4) == (iota((256, 128), 1) >> 4)
    for g in range(rows // 128):
        part = slice(128 * g, 128 * g + 128)
        for p in range(3):
            q2 = S["qkv"][l, part, 128 * p : 128 * p + 128]
            k2 = S["qkv"][l, part, D + 128 * p : D + 128 * p + 128]
            v2 = S["qkv"][l, part, 2 * D + 128 * p : 2 * D + 128 * p + 128]
            scores = mm(two_heads(q2), k2, 1, 1) * SCALE
            scores = jnp.where(same, scores, -1e30)
            grown = jnp.exp(scores - jnp.max(scores, axis=-1, keepdims=True))
            prob = grown / jnp.sum(grown, axis=-1, keepdims=True)
            S["prob"][l, 3 * g + p] = prob
            S["att"][l, part, 128 * p : 128 * p + 128] = merge_heads(mm(prob.astype(bf16), v2)).astype(bf16)
    x1 = S["x"][l] + mm(S["att"][l], win[l, :, 3 * D : 4 * D])
    S["x1"][l] = x1
    hat, _ = norm(x1)
    u2 = hat.astype(bf16)
    S["u2"][l] = u2
    for n in range(4):
        pre = mm(u2, win[l, :, 4 * D + D * n : 5 * D + D * n])
        S["pre"][l, :, D * n : D * n + D] = pre
        bent = jnp.tanh(GELU_A * (pre + GELU_B * pre * pre * pre))
        S["h"][l, :, D * n : D * n + D] = (0.5 * pre * (1.0 + bent)).astype(bf16)
    return S["x1"][l] + mm(S["h"][l], wdn[l])


def block_backward(l, rows, S, win, wdn, dy_ref):
    dyb = dy_ref[...].astype(bf16)
    S["dyb"][l] = dyb
    for n in range(4):
        cols = slice(D * n, D * n + D)
        dh = rounded(mm(dyb, wdn[l, cols, :], 1, 1))
        pre = S["pre"][l, :, cols]
        bent = jnp.tanh(GELU_A * (pre + GELU_B * pre * pre * pre))
        slope = 0.5 * (1.0 + bent) + 0.5 * pre * (1.0 - bent * bent) * GELU_A * (1.0 + 3.0 * GELU_B * pre * pre)
        S["dpre"][l, :, cols] = (dh * slope).astype(bf16)
    du2 = rounded(mm(S["dpre"][l], win[l, :, 4 * D :], 1, 1))
    dx1 = dy_ref[...] + norm_back(S["x1"][l], du2)
    dy_ref[...] = dx1
    dx1b = dx1.astype(bf16)
    S["dx1b"][l] = dx1b
    S["datt"][...] = mm(dx1b, win[l, :, 3 * D : 4 * D], 1, 1).astype(bf16)
    for g in range(rows // 128):
        part = slice(128 * g, 128 * g + 128)
        for p in range(3):
            cq = slice(128 * p, 128 * p + 128)
            ck = slice(D + 128 * p, D + 128 * p + 128)
            cv = slice(2 * D + 128 * p, 2 * D + 128 * p + 128)
            qs = two_heads(S["qkv"][l, part, cq])
            dos = two_heads(S["datt"][part, cq])
            prob = S["prob"][l, 3 * g + p]
            dprob = mm(dos, S["qkv"][l, part, cv], 1, 1)
            dscore = prob * (dprob - jnp.sum(prob * dprob, axis=-1, keepdims=True)) * SCALE
            dsb = dscore.astype(bf16)
            S["dqkv"][l, part, cq] = merge_heads(mm(dsb, S["qkv"][l, part, ck])).astype(bf16)
            S["dqkv"][l, part, ck] = mm(dsb, qs, 0, 0).astype(bf16)
            S["dqkv"][l, part, cv] = mm(prob.astype(bf16), dos, 0, 0).astype(bf16)
    du1 = rounded(mm(S["dqkv"][l], win[l, :, : 3 * D], 1, 1))
    dy_ref[...] = dy_ref[...] + norm_back(S["x"][l], du1)


def weight_pairs(S, l):
    pairs = []
    for n in range(3):
        pairs.append((n, S["u1"].at[l], S["dqkv"].at[l, :, pl.ds(D * n, D)]))
    pairs.append((3, S["att"].at[l], S["dx1b"].at[l]))
    for n in range(4):
        pairs.append((4 + n, S["u2"].at[l], S["dpre"].at[l, :, pl.ds(D * n, D)]))
    return pairs


def block_shapes(layers, rows):
    return dict(
        x=((layers + 1, rows, D), f32),
        x1=((layers, rows, D), f32),
        u1=((layers, rows, D), bf16),
        u2=((layers, rows, D), bf16),
        qkv=((layers, rows, 3 * D), bf16),
        prob=((layers, 3 * rows // 128, 256, 128), f32),
        att=((layers, rows, D), bf16),
        pre=((layers, rows, FF), f32),
        h=((layers, rows, FF), bf16),
        dyb=((layers, rows, D), bf16),
        dpre=((layers, rows, FF), bf16),
        dx1b=((layers, rows, D), bf16),
        datt=((rows, D), bf16),
        dqkv=((layers, rows, 3 * D), bf16),
        dy=((rows, D), f32),
    )


class Place:
    def __init__(self):
        me = lax.axis_index("client")
        self.me = me
        self.c, self.y, self.z, self.x = me % 2, me // 2 % 4, me // 8 % 4, me // 32
        self.r, self.group = me % 8, me // 8 * 8
        self.partner = me + 1 - 2 * self.c
        self.yp, self.ym = self.at(0, 0, 1), self.at(0, 0, 3)
        self.xp, self.xm = self.at(1, 0, 0), self.at(3, 0, 0)
        self.zp, self.zm = self.at(0, 1, 0), self.at(0, 3, 0)

    def at(self, dx, dz, dy):
        x, z, y = (self.x + dx) % 4, (self.z + dz) % 4, (self.y + dy) % 4
        return ((x * 4 + z) * 4 + y) * 2 + self.c

    def greet(self, group, plane):
        peers = []
        if group:
            peers += [self.group + (self.r + i) % 8 for i in range(1, 8)]
        if plane:
            peers += [self.xp, self.xm, self.zp, self.zm]
        barrier = pltpu.get_barrier_semaphore()
        for peer in peers:
            pl.semaphore_signal(barrier, inc=1, device_id=(peer,), device_id_type=MESH)
        pl.semaphore_wait(barrier, len(peers))


class Wire:
    def __init__(self, send_sem, recv_sem):
        self.send_sem, self.recv_sem, self.sent = send_sem, recv_sem, []

    def make(self, src, dst, k, device):
        return pltpu.make_async_remote_copy(
            src_ref=src,
            dst_ref=dst,
            send_sem=self.send_sem.at[k],
            recv_sem=self.recv_sem.at[k],
            device_id=(device,),
            device_id_type=MESH,
        )

    def send(self, src, dst, k, device):
        copy = self.make(src, dst, k, device)
        copy.start()
        self.sent.append(copy)

    def wait(self, landed, k, device):
        self.make(landed, landed, k, device).wait_recv()

    def finish(self):
        for copy in self.sent:
            copy.wait_send()


def plane_gather(wire, place, buf, count, k0):
    half, quarter = count // 2, count // 4
    x, z = place.x, place.z
    xm, xp, zm, zp = (x + 3) % 4, (x + 1) % 4, (z + 3) % 4, (z + 1) % 4
    xo, zo = (x + 2) % 4, (z + 2) % 4
    X, XA, XB = pl.ds(0, half), pl.ds(0, quarter), pl.ds(quarter, quarter)
    Z, ZA, ZB = pl.ds(half, half), pl.ds(half, quarter), pl.ds(half + quarter, quarter)

    def both(ref, k, device):
        wire.send(ref, ref, k0 + k, device)

    def first():
        both(buf.at[x, z, X], 0, place.xp)
        both(buf.at[x, z, X], 1, place.xm)
        both(buf.at[x, z, Z], 2, place.zp)
        both(buf.at[x, z, Z], 3, place.zm)

    def second():
        wire.wait(buf.at[xm, z, X], k0 + 0, place.xm)
        both(buf.at[xm, z, XA], 4, place.xp)
        wire.wait(buf.at[xp, z, X], k0 + 1, place.xp)
        both(buf.at[xp, z, XB], 5, place.xm)
        wire.wait(buf.at[x, zm, Z], k0 + 2, place.zm)
        both(buf.at[x, zm, ZA], 6, place.zp)
        wire.wait(buf.at[x, zp, Z], k0 + 3, place.zp)
        both(buf.at[x, zp, ZB], 7, place.zm)

    def third():
        wire.wait(buf.at[xo, z, XA], k0 + 4, place.xm)
        wire.wait(buf.at[xo, z, XB], k0 + 5, place.xp)
        both(buf.at[:, z, X], 8, place.zp)
        both(buf.at[:, z, X], 9, place.zm)
        wire.wait(buf.at[x, zo, ZA], k0 + 6, place.zm)
        wire.wait(buf.at[x, zo, ZB], k0 + 7, place.zp)
        both(buf.at[x, :, Z], 10, place.xp)
        both(buf.at[x, :, Z], 11, place.xm)

    def fourth():
        wire.wait(buf.at[:, zm, X], k0 + 8, place.zm)
        both(buf.at[0:2, zm, X], 12, place.zp)
        wire.wait(buf.at[:, zp, X], k0 + 9, place.zp)
        both(buf.at[2:4, zp, X], 13, place.zm)
        wire.wait(buf.at[xm, :, Z], k0 + 10, place.xm)
        both(buf.at[xm, 0:2, Z], 14, place.xp)
        wire.wait(buf.at[xp, :, Z], k0 + 11, place.xp)
        both(buf.at[xp, 2:4, Z], 15, place.xm)

    def fifth():
        wire.wait(buf.at[0:2, zo, X], k0 + 12, place.zm)
        wire.wait(buf.at[2:4, zo, X], k0 + 13, place.zp)
        wire.wait(buf.at[xo, 0:2, Z], k0 + 14, place.xm)
        wire.wait(buf.at[xo, 2:4, Z], k0 + 15, place.xp)

    return first, second, third, fourth, fifth


def add_rows(start, stop, step, body):
    def run(i, carry):
        body(pl.ds(pl.multiple_of(start + i * step, 16), step))
        return carry

    lax.fori_loop(0, (stop - start) // step, run, 0)


def route(arow, labels, shard, rank_in):
    eye = iota((128, 128), 0) == iota((128, 128), 1)
    acol = jnp.sum(jnp.where(eye, arow.astype(f32), 0.0), axis=1, keepdims=True).astype(jnp.int32)
    earlier = (acol == arow) & (iota((128, 128), 0) < iota((128, 128), 1))
    rank = jnp.sum(earlier.astype(f32), axis=0, keepdims=True).astype(jnp.int32)
    chosen = (jnp.broadcast_to(arow, (CAP, 128)) == shard) & (
        jnp.broadcast_to(rank, (CAP, 128)) == iota((CAP, 128), 0)
    )
    selector = chosen.astype(f32).astype(bf16)
    take = (iota((128, 16), 0) == iota((128, 16), 1) * IMG + rank_in).astype(f32).astype(bf16)
    by_row = mm(labels.astype(f32).astype(bf16), take).astype(bf16)
    lift = ((iota((128, 8), 0) >> 4) == iota((128, 8), 1)).astype(f32).astype(bf16)
    tall = mm(lift, by_row)
    mine = (iota((128, 16), 0) & 15) == iota((128, 16), 1)
    label = jnp.sum(jnp.where(mine, tall, 0.0), axis=1, keepdims=True)
    onehot = (label == iota((128, CLASSES), 1).astype(f32)).astype(f32).astype(bf16)
    return selector, mm(selector, onehot)


def slot_rows(selector, arrived):
    spread = (iota((128, 2048), 0) == (iota((128, 2048), 1) >> 4)).astype(f32).astype(bf16)
    wide = mm(selector, spread).astype(bf16)
    repeat = ((iota((256, CAP), 0) >> 4) == iota((256, CAP), 1)).astype(f32).astype(bf16)
    tall = mm(repeat, wide)
    same = (iota((256, 2048), 0) & 15) == (iota((256, 2048), 1) & 15)
    return mm(jnp.where(same, tall, 0.0).astype(bf16), arrived)


def head_loss(last, classes, hot):
    filled = jnp.sum(hot, axis=1, keepdims=True)
    mean = jnp.mean(last.reshape(CAP, TOK, D), axis=1)
    hat, _ = norm(mean)
    pooled = hat.astype(bf16)
    logits = mm(pooled, classes, 1, 1)
    top = jnp.max(logits, axis=1, keepdims=True)
    grown = jnp.exp(logits - top)
    total = jnp.sum(grown, axis=1, keepdims=True)
    per = (jnp.log(total) + top - jnp.sum(hot * logits, axis=1, keepdims=True)) * filled
    eye = iota((CAP, CAP), 0) == iota((CAP, CAP), 1)
    losses = jnp.sum(jnp.where(eye, per, 0.0), axis=0, keepdims=True)
    dlogits = ((grown / total) * filled - hot).astype(bf16)
    gcls = mm(pooled, dlogits, 0, 0).astype(bf16)
    dpooled = rounded(mm(dlogits, classes))
    dmean = norm_back(mean, dpooled) * (1.0 / TOK)
    dlast = jnp.broadcast_to(dmean[:, None, :], (CAP, TOK, D)).reshape(CAP * TOK, D)
    return losses, gcls, dlast


CLIENT = block_shapes(1, 128)
SERVER = block_shapes(LAYERS, 256)
BUFFERS = dict(
    arrived=((4, 4, IMG, TOK, D), bf16),
    win=((LAYERS, D, 4 * D + FF), bf16),
    wdn=((LAYERS, FF, D), bf16),
    cls=((CLASSES, D), bf16),
    cut=((IMG, TOK, D), bf16),
    packed=((8, PACK, D), bf16),
    swapped=((4, PACK, D), bf16),
    from_m=((CUT_A, D), bf16),
    from_p=((PACK - CUT_A, D), bf16),
    fin_p=((PACK, D), bf16),
    fin_m=((PACK, D), bf16),
    line_x=((4, 8, TOK, D), bf16),
    line_z=((4, 8, TOK, D), bf16),
    pick_x=((4, 8, TOK, D), bf16),
    pick_z=((4, 8, TOK, D), bf16),
    got_x=((3, 8, TOK, D), bf16),
    got_z=((3, 8, TOK, D), bf16),
    picked=((8, TOK, D), bf16),
    own=((IMG, TOK, D), bf16),
    order=((D, 512), bf16),
    dperm=((128, 512), bf16),
    pp=((128, D), bf16),
    cpack=((16, 2, BLOCK, D), bf16),
    cswap=((16, BLOCK, D), bf16),
    cmine=((4, 4, BLOCK, D), bf16),
    hop_x=((2, 2, MAIN, D), bf16),
    hop_z=((2, 2, TAIL, D), bf16),
    end_x=((2, 4, MAIN, D), bf16),
    end_z=((2, 4, TAIL, D), bf16),
    half_x=((4, MAIN, D), bf16),
    half_z=((4, TAIL, D), bf16),
    two_x=((3, MAIN, D), bf16),
    two_z=((3, TAIL, D), bf16),
    low_x=((4, 24, D), bf16),
    low_z=((4, 16, D), bf16),
    three_x=((3, 24, D), bf16),
    three_z=((3, 16, D), bf16),
)
N_SEM = 160


def step_kernel(patches_t, embed, positions, win_c, wdn_c, win_s, wdn_s, arow, labels, source, classes, *refs):
    losses, gin, gdn, gcls_out, out_in, out_dn, out_pe, out_pos = refs[:8]
    refs = list(refs[8:])
    C = dict(zip(CLIENT, refs[: len(CLIENT)]))
    refs = refs[len(CLIENT) :]
    S = dict(zip(SERVER, refs[: len(SERVER)]))
    refs = refs[len(SERVER) :]
    B = dict(zip(BUFFERS, refs[: len(BUFFERS)]))
    send_sem, recv_sem, local_sem = refs[len(BUFFERS) :]
    place = Place()
    x, z, y, c, r = place.x, place.z, place.y, place.c, place.r
    shard = place.me // 8
    win, wdn, arrived, packed = B["win"], B["wdn"], B["arrived"], B["packed"]
    place.greet(True, True)
    wire = Wire(send_sem, recv_sem)

    def owner(dy, other=False):
        return (y + dy) % 4 * 2 + (1 - c if other else c)

    def window(l, down, rank, part):
        if down:
            low, size = {None: (0, 192), 0: (0, 96), 1: (96, 96)}[part]
            return wdn.at[l, pl.ds(pl.multiple_of(rank * 192 + low, 16), size), :]
        cols = {None: pl.ds(0, 3072), 0: pl.ds(0, 1536), 1: pl.ds(1536, 1536)}[part]
        return win.at[l, pl.ds(pl.multiple_of(rank * 48, 16), 48), cols]

    pieces = [(l, down) for l in range(LAYERS) for down in (False, True)]
    base = {piece: 8 + 9 * n for n, piece in enumerate(pieces)}
    for piece in pieces:
        l, down = piece
        mine = (wdn_s if down else win_s).at[l]
        here = window(l, down, r, None)
        wire.send(mine, here, base[piece] + 0, place.yp)
        wire.send(mine, here, base[piece] + 1, place.ym)
        wire.send(mine, here, base[piece] + 4, place.partner)
        here[...] = mine[...]
    copy = pltpu.make_async_copy(classes.at[shard], B["cls"], local_sem)
    copy.start()

    def forward(piece):
        l, down = piece
        b = base[piece]
        left, right = owner(3), owner(1)
        whole, half = window(l, down, left, None), window(l, down, left, 0)
        wire.wait(whole, b + 0, place.ym)
        wire.send(half, half, b + 2, place.yp)
        wire.send(whole, whole, b + 5, place.partner)
        whole, half = window(l, down, right, None), window(l, down, right, 1)
        wire.wait(whole, b + 1, place.yp)
        wire.send(half, half, b + 3, place.ym)
        wire.send(whole, whole, b + 6, place.partner)

    def across(piece):
        l, down = piece
        b = base[piece]
        for part, device in ((0, place.ym), (1, place.yp)):
            half = window(l, down, owner(2), part)
            wire.wait(half, b + 2 + part, device)
            wire.send(half, half, b + 7 + part, place.partner)

    def settle(piece):
        l, down = piece
        b = base[piece]
        wire.wait(window(l, down, owner(0, True), None), b + 4, place.partner)
        wire.wait(window(l, down, owner(3, True), None), b + 5, place.partner)
        wire.wait(window(l, down, owner(1, True), None), b + 6, place.partner)
        for part in range(2):
            wire.wait(window(l, down, owner(2, True), part), b + 7 + part, place.partner)

    tiled = jnp.concatenate([positions[...].astype(f32)] * IMG, axis=0)
    C["x"][0] = mm(patches_t[...], embed[...], 0, 0) + tiled
    cut = block_forward(0, 128, C, win_c, wdn_c).astype(bf16)
    B["cut"][...] = cut.reshape(IMG, TOK, D)
    for i in range(1, 8):
        j = (r + i) % 8
        wire.send(B["cut"].at[j], arrived.at[x, z, r], i, place.group + j)
    arrived[x, z, r] = B["cut"][r]
    first, second, third, fourth, fifth = plane_gather(wire, place, arrived, IMG, 44)
    forward(pieces[0])
    for i in range(1, 8):
        j = (r - i + 8) % 8
        wire.wait(arrived.at[x, z, j], i, place.group + j)
    first()
    forward(pieces[1])
    second()
    selector, hot = route(arow[...], labels[...], shard, r)
    col = iota((1, 512), 1)
    at = col & 15
    wanted = ((col >> 4) & 15) * 24 + (at // 3) * 6 + (col >> 8) * 3 + at % 3
    B["order"][...] = ((iota((D, 512), 0) == wanted) & (at < 12)).astype(f32).astype(bf16)
    B["pp"][...] = (iota((128, D), 1) - 256 == (iota((128, D), 0) & 15)).astype(f32).astype(bf16)
    B["pp"][:, 0:192] = patches_t[...].T
    packed[:, PACK - 48 :, :] = jnp.zeros((8, 48, D), bf16)
    third()
    across(pieces[0])
    forward(pieces[2])
    across(pieces[1])
    fourth()
    forward(pieces[3])
    fifth()
    across(pieces[2])
    settle(pieces[0])
    settle(pieces[1])

    S["x"][0] = slot_rows(selector, arrived[...].reshape(2048, D))
    S["x"][1] = block_forward(0, 256, S, win, wdn)
    across(pieces[3])
    settle(pieces[2])
    settle(pieces[3])
    S["x"][2] = block_forward(1, 256, S, win, wdn)
    copy.wait()
    loss, gcls, dlast = head_loss(S["x"][LAYERS], B["cls"][...], hot)
    losses[...] = loss
    for k in range(8):
        packed[k, PACK - 48 :, 0:CLASSES] = gcls[48 * k : 48 * k + 48]
    S["dy"][...] = dlast

    def backward(i, carry):
        block_backward(LAYERS - 1 - i, 256, S, win, wdn, S["dy"])
        return carry

    lax.fori_loop(0, LAYERS, backward, 0)

    line_x, line_z = B["line_x"], B["line_z"]
    gcut = S["dy"][...].astype(bf16).reshape(CAP, TOK, D)
    line_x[x] = gcut[:8]
    line_z[z] = gcut[8:]
    lo, hi, all8 = pl.ds(0, 4), pl.ds(4, 4), pl.ds(0, 8)
    lines = ((line_x, x, place.xp, place.xm, 60), (line_z, z, place.zp, place.zm, 64))
    for buf, me, up, down, k0 in lines:
        wire.send(buf.at[me], buf.at[me], k0, up)
        wire.send(buf.at[me], buf.at[me], k0 + 1, down)

    def server_weights(l):
        for b, u, dout in weight_pairs(S, l):
            val = mm(u[...], dout[...], 0, 0).astype(bf16)
            for k in range(8):
                packed[k, 576 * l + 48 * b : 576 * l + 48 * b + 48, :] = val[48 * k : 48 * k + 48]
        for n in range(4):
            val = mm(S["h"][l, :, D * n : D * n + D], S["dyb"][l], 0, 0).astype(bf16)
            for j in range(2):
                packed[2 * n + j, 576 * l + D : 576 * l + 576, :] = val[192 * j : 192 * j + 192]

    rows_a, rows_b = pl.ds(0, CUT_A), pl.ds(CUT_A, PACK - CUT_A)

    def row(k, core):
        return (y + k) % 4 * 2 + core

    def swap(part, k0):
        for k in (2, 1, 3, 0):
            wire.send(packed.at[row(k, 1 - c), part], B["swapped"].at[k, part], k0 + k, place.partner)

    def combine(k, part, k0, start, stop):
        wire.wait(B["swapped"].at[k, part], k0 + k, place.partner)

        def body(rows):
            total = packed[row(k, c), rows, :].astype(f32) + B["swapped"][k, rows, :].astype(f32)
            packed[row(k, c), rows, :] = total.astype(bf16)

        add_rows(start, stop, 48, body)

    def combine_a(k):
        combine(k, rows_a, 80, 0, CUT_A)

    def combine_b(k):
        combine(k, rows_b, 84, CUT_A, PACK)

    server_weights(1)
    swap(rows_b, 84)
    for buf, me, up, down, k0 in lines:
        left, right = (me + 3) % 4, (me + 1) % 4
        wire.wait(buf.at[left], k0, down)
        wire.send(buf.at[left, lo], buf.at[left, lo], k0 + 2, up)
        wire.wait(buf.at[right], k0 + 1, up)
        wire.send(buf.at[right, hi], buf.at[right, hi], k0 + 3, down)
    combine_b(2)
    wire.send(packed.at[row(2, c), rows_b], B["from_p"], 88, place.ym)
    combine_b(1)
    wire.send(packed.at[row(1, c), rows_b], B["fin_p"].at[rows_b], 89, place.yp)
    for buf, me, up, down, k0 in lines:
        far = (me + 2) % 4
        wire.wait(buf.at[far, lo], k0 + 2, down)
        wire.wait(buf.at[far, hi], k0 + 3, up)
    for k in (2, 1, 3, 0):
        for m in range(8):
            zd, xd = (z + k) % 4, (x + k) % 4
            at = source[(x * 4 + zd) * 8 + m]
            here = (at // 16 % 4 == z) & (at % 16 < 8)
            B["pick_x"][k, m] = jnp.where(here, line_x[at // 64, at % 8].astype(f32), 0.0).astype(bf16)
            at = source[(xd * 4 + z) * 8 + m]
            here = (at // 64 == x) & (at % 16 >= 8)
            B["pick_z"][k, m] = jnp.where(here, line_z[at // 16 % 4, at % 8].astype(f32), 0.0).astype(bf16)
        if k:
            wire.send(B["pick_x"].at[k], B["got_x"].at[k - 1], 67 + k, place.at(0, k, 0))
            wire.send(B["pick_z"].at[k], B["got_z"].at[k - 1], 70 + k, place.at(k, 0, 0))
    server_weights(0)
    swap(rows_a, 80)
    for k in range(1, 4):
        wire.wait(B["got_x"].at[k - 1], 67 + k, place.at(0, 4 - k, 0))
        wire.wait(B["got_z"].at[k - 1], 70 + k, place.at(4 - k, 0, 0))
    for m in range(8):
        piece = B["pick_x"][0, m].astype(f32) + B["pick_z"][0, m].astype(f32)
        for k in range(3):
            piece = piece + B["got_x"][k, m].astype(f32) + B["got_z"][k, m].astype(f32)
        B["picked"][m] = piece.astype(bf16)
    own = B["own"]
    own[r] = B["picked"][r]
    for i in range(1, 8):
        m = (r + i) % 8
        wire.send(B["picked"].at[m], own.at[r], 91 + i, place.group + m)
    combine_a(2)
    wire.send(packed.at[row(2, c), rows_a], B["from_m"], 90, place.yp)
    combine_a(3)
    wire.send(packed.at[row(3, c), rows_a], B["fin_m"].at[rows_a], 91, place.ym)
    combine_a(1)
    combine_b(3)
    for i in range(1, 8):
        j = (r - i + 8) % 8
        wire.wait(own.at[j], 91 + i, place.group + j)

    C["dy"][...] = own[...].reshape(128, D).astype(f32)
    block_backward(0, 128, C, win_c, wdn_c, C["dy"])
    cpack, cswap, cmine = B["cpack"], B["cswap"], B["cmine"]
    B["dperm"][...] = mm(C["dyb"][0], B["order"][...]).astype(bf16)
    for q in range(5):
        if q == 4:
            B["dperm"][...] = mm(C["dy"][...].astype(bf16), B["order"][...]).astype(bf16)
        right = B["pp"][...] if q == 4 else C["h"][0, :, D * q : D * q + D]
        val = mm(B["dperm"][...], right, 0, 0).astype(bf16)
        for core in range(2):
            for i in range(16):
                cpack[i, core, MAIN + 16 * q : MAIN + 16 * q + 16] = val[256 * core + 16 * i : 256 * core + 16 * i + 16]
    wire.send(cpack.at[:, 1 - c, pl.ds(MAIN, TAIL)], cswap.at[:, pl.ds(MAIN, TAIL)], 108, place.partner)
    for b, u, dout in weight_pairs(C, 0):
        val = mm(dout[...], u[...], 0, 0).astype(bf16)
        for i in range(2):
            for k in range(4):
                for core in range(2):
                    low = 192 * i + 48 * k + 24 * core
                    cpack[2 * b + i, core, 24 * k : 24 * k + 24] = val[low : low + 24]
        pair = pl.ds(2 * b, 2)
        wire.send(cpack.at[pair, 1 - c, pl.ds(0, MAIN)], cswap.at[pair, pl.ds(0, MAIN)], 100 + b, place.partner)

    X, Z = pl.ds(0, MAIN), pl.ds(MAIN, TAIL)

    def fold(low, high):
        for i in range(16):
            total = cpack[i, c, low:high].astype(f32) + cswap[i, low:high].astype(f32)
            cmine[i // 4, i % 4, low:high] = total.astype(bf16)

    def src_x(k, part):
        return cmine.at[(x + k) % 4, pl.ds(2 * part, 2), X]

    def src_z(k, part):
        return cmine.at[pl.ds(2 * part, 2), (z + k) % 4, Z]

    def ring_one(src, hop, end, up, down, k0):
        wire.send(src(2, 0), hop.at[0], k0, up)
        wire.send(src(2, 1), hop.at[1], k0 + 1, down)
        wire.send(src(1, 1), end.at[0, pl.ds(2, 2)], k0 + 2, up)
        wire.send(src(3, 0), end.at[1, pl.ds(0, 2)], k0 + 3, down)

    def ring_two(src, load, hop, end, up, down, k0):
        wire.wait(hop.at[0], k0, down)
        load(1, 0, hop)
        wire.send(src(1, 0), end.at[0, pl.ds(0, 2)], k0 + 4, up)
        wire.wait(hop.at[1], k0 + 1, up)
        load(3, 1, hop)
        wire.send(src(3, 1), end.at[1, pl.ds(2, 2)], k0 + 5, down)

    def ring_three(end, up, down, k0):
        wire.wait(end.at[0, pl.ds(2, 2)], k0 + 2, down)
        wire.wait(end.at[1, pl.ds(0, 2)], k0 + 3, up)
        wire.wait(end.at[0, pl.ds(0, 2)], k0 + 4, down)
        wire.wait(end.at[1, pl.ds(2, 2)], k0 + 5, up)

    def load_x(k, part, hop):
        to = (x + k) % 4
        for i in range(2):
            at = 2 * part + i
            cmine[to, at, :MAIN] = (cmine[to, at, :MAIN].astype(f32) + hop[part, i].astype(f32)).astype(bf16)

    def load_z(k, part, hop):
        to = (z + k) % 4
        for i in range(2):
            at = 2 * part + i
            cmine[at, to, MAIN:] = (cmine[at, to, MAIN:].astype(f32) + hop[part, i].astype(f32)).astype(bf16)

    wire.wait(cswap.at[:, Z], 108, place.partner)
    fold(MAIN, BLOCK)
    ring_one(src_z, B["hop_z"], B["end_z"], place.zp, place.zm, 116)
    for b in range(8):
        wire.wait(cswap.at[pl.ds(2 * b, 2), X], 100 + b, place.partner)
    fold(0, MAIN)
    ring_one(src_x, B["hop_x"], B["end_x"], place.xp, place.xm, 110)

    wire.wait(B["from_m"], 90, place.ym)

    def add_a(rows):
        packed[row(1, c), rows, :] = (packed[row(1, c), rows, :].astype(f32) + B["from_m"][rows, :].astype(f32)).astype(bf16)

    add_rows(0, CUT_A, 48, add_a)
    wire.send(packed.at[row(1, c), rows_a], B["fin_p"].at[rows_a], 122, place.yp)
    wire.wait(B["from_p"], 88, place.yp)

    def add_b(i, carry):
        here = pl.ds(pl.multiple_of(i * 48, 16), 48)
        rows = pl.ds(pl.multiple_of(CUT_A + i * 48, 16), 48)
        packed[row(3, c), rows, :] = (packed[row(3, c), rows, :].astype(f32) + B["from_p"][here, :].astype(f32)).astype(bf16)
        return carry

    lax.fori_loop(0, (PACK - CUT_A) // 48, add_b, 0)
    wire.send(packed.at[row(3, c), rows_b], B["fin_m"].at[rows_b], 123, place.ym)

    ring_two(src_z, load_z, B["hop_z"], B["end_z"], place.zp, place.zm, 116)
    ring_two(src_x, load_x, B["hop_x"], B["end_x"], place.xp, place.xm, 110)
    half_x, half_z = B["half_x"], B["half_z"]
    ring_three(B["end_z"], place.zp, place.zm, 116)
    for i in range(4):
        total = cmine[i, z, MAIN:].astype(f32) + B["end_z"][0, i].astype(f32) + B["end_z"][1, i].astype(f32)
        half_z[i] = total.astype(bf16)
    for k in (2, 1, 3):
        wire.send(half_z.at[(x + k) % 4], B["two_z"].at[k - 1], 127 + k, place.at(k, 0, 0))
    ring_three(B["end_x"], place.xp, place.xm, 110)
    for i in range(4):
        total = cmine[x, i, :MAIN].astype(f32) + B["end_x"][0, i].astype(f32) + B["end_x"][1, i].astype(f32)
        half_x[i] = total.astype(bf16)
    for k in (2, 1, 3):
        wire.send(half_x.at[(z + k) % 4], B["two_x"].at[k - 1], 124 + k, place.at(0, k, 0))
    combine_a(0)
    combine_b(0)
    for k in range(1, 4):
        wire.wait(B["two_z"].at[k - 1], 127 + k, place.at(4 - k, 0, 0))
    tail = half_z[x].astype(f32)
    for k in range(3):
        tail = tail + B["two_z"][k].astype(f32)
    line, column = iota((64, TAIL), 0), iota((64, TAIL), 1)
    inside = line & 15
    pick = (column == (inside // 3) * 16 + (line >> 4) * 3 + inside % 3) & (inside < 15)
    ordered = mm(pick.astype(f32).astype(bf16), tail.astype(bf16)).astype(bf16)
    for k in range(4):
        B["low_z"][k] = ordered[16 * k : 16 * k + 16]
    for k in range(1, 4):
        wire.wait(B["two_x"].at[k - 1], 124 + k, place.at(0, 4 - k, 0))
    main = half_x[z].astype(f32)
    for k in range(3):
        main = main + B["two_x"][k].astype(f32)
    for k in range(4):
        B["low_x"][k] = main[24 * k : 24 * k + 24].astype(bf16)
    for k in (2, 1, 3):
        to = (y + k) % 4
        wire.send(B["low_x"].at[to], B["three_x"].at[k - 1], 130 + k, place.at(0, 0, k))
        wire.send(B["low_z"].at[to], B["three_z"].at[k - 1], 133 + k, place.at(0, 0, k))

    wire.wait(B["fin_p"].at[rows_b], 89, place.ym)
    wire.wait(B["fin_m"].at[rows_a], 91, place.yp)
    wire.wait(B["fin_p"].at[rows_a], 122, place.ym)
    wire.wait(B["fin_m"].at[rows_b], 123, place.yp)

    def total_of(first_row, rows):
        at = pl.ds(first_row, rows)
        return packed[row(0, c), at, :].astype(f32) + B["fin_p"][at, :].astype(f32) + B["fin_m"][at, :].astype(f32)

    for l in range(LAYERS):
        for b in range(8):
            gin[l, :, D * b : D * b + D] = total_of(576 * l + 48 * b, 48)
        for b in range(4):
            gdn[l, 48 * b : 48 * b + 48, :] = total_of(576 * l + D + 48 * b, 48)
    gcls_out[...] = total_of(PACK - 48, 48)[:, 0:CLASSES]

    for k in range(1, 4):
        wire.wait(B["three_x"].at[k - 1], 130 + k, place.at(0, 0, 4 - k))
        wire.wait(B["three_z"].at[k - 1], 133 + k, place.at(0, 0, 4 - k))
    main = B["low_x"][y].astype(f32)
    tail = B["low_z"][y].astype(f32)
    for k in range(3):
        main = main + B["three_x"][k].astype(f32)
        tail = tail + B["three_z"][k].astype(f32)
    out_in[...] = main
    for q in range(4):
        out_dn[:, D * q : D * q + D] = tail[3 * q : 3 * q + 3]
    out_pe[...] = tail[12:15, 0:192]
    out_pos[...] = tail[12:15, 256:272]
    wire.finish()


def per_device(patches, labels, assign, patch_embed, positions, client_in, client_down, server_in, server_down, classifier):
    routes = assign[:, 0]
    places = jnp.arange(128, dtype=jnp.int32)
    earlier = (routes[:, None] == routes[None, :]) & (places[:, None] < places[None, :])
    source = routes * CAP + jnp.sum(earlier.astype(jnp.int32), axis=0)
    shapes = [
        ((1, CAP), f32),
        ((LAYERS, 48, 4 * D + FF), f32),
        ((LAYERS, 192, D), f32),
        ((48, CLASSES), f32),
        ((24, D), f32),
        ((3, FF), f32),
        ((3, 192), f32),
        ((3, TOK), f32),
    ]
    scratch = list(CLIENT.values()) + list(SERVER.values()) + list(BUFFERS.values())
    losses, gin, gdn, gcls, out_in, out_dn, out_pe, out_pos = pl.pallas_call(
        step_kernel,
        out_shape=[jax.ShapeDtypeStruct(*s) for s in shapes],
        in_specs=[VMEM] * 9 + [SMEM, ANY],
        out_specs=[VMEM] * len(shapes),
        scratch_shapes=[pltpu.VMEM(*s) for s in scratch]
        + [pltpu.SemaphoreType.DMA((N_SEM,)), pltpu.SemaphoreType.DMA((N_SEM,)), pltpu.SemaphoreType.DMA],
        compiler_params=pltpu.CompilerParams(collective_id=0, has_side_effects=True, vmem_limit_bytes=67043328),
        name="step",
    )(
        patches.T,
        patch_embed,
        positions,
        client_in[None],
        client_down[None],
        server_in,
        server_down,
        assign.reshape(1, 128),
        labels.reshape(8, 128),
        source,
        classifier.transpose(0, 2, 1),
    )
    return losses, out_pe.T, out_pos.T, out_in.T, out_dn.T, gin, gdn, gcls


def solution(mesh):
    in_specs = (
        P("client", None),
        P(),
        P(),
        P(),
        P(),
        P(),
        P(),
        P(None, "client", None),
        P(None, "client", None),
        P(),
    )
    out_specs = (
        P("client", None),
        P(None, "client"),
        P(None, "client"),
        P(None, "client"),
        P(None, "client"),
        P(None, "client", None),
        P(None, "client", None),
        P("client", None),
    )
    return jax.shard_map(per_device, mesh=mesh, in_specs=in_specs, out_specs=out_specs, check_vma=False)
```

time: 185 us -> 136 us (0.74); the launches traced: 182 us -> 135 us
  Pallas kernels: 158 us -> 120 us
  local copies, waits for them, and re-layouts: 22.6 us -> 12.6 us
    pallas_call x6 -> x1, Pallas kernels: 158 us -> 120 us  [per_device(): pl.pallas_call(step_kernel, out_shape=[jax.ShapeDtypeStruct(*s) for s in...]
    unnamed x25 -> x11, local copies, waits for them, and re-layouts: 17.3 us -> 12.6 us
    slice x7 -> x0, local copies, waits for them, and re-layouts: 3.9 us -> none  [the longest x5 2.07 us: per_device(): cols[:, 24 + 3 * q:27 + 3 * q]]
where the time goes in v2:
time: 136 us; the launch traced here: 135 us
  Pallas kernels  120 us (88%)
  local copies, waits for them, and re-layouts  12.6 us (9%)
  other arithmetic  2 us (1%)
    pallas_call x1, Pallas kernels, per_device(): pl.pallas_call(step_kernel, out_shape=[jax.ShapeDtypeStruct(*s) for s in...  120 us
    unnamed x11, local copies, waits for them, and re-layouts  12.6 us

profile of v2, /device:TPU:0, one launch (start us, length us, event | category | flops | bytes accessed | tf_op | source)
XLA Modules:
  0.0 135.2 jit_solution(17080556682593721755)
XLA Ops:
  0.6 0.8 convert_reduce_fusion
  1.5 1.2 multiply_add_fusion.source
  2.6 1.6 %copy.23 = bf16[16,384,10]{1,2,0:T(8,128)(2,1)} copy(bf16[16,384,10]{1,0,2:T(8,128)(2,1)} %param.19) | data formatting | bytes 245760 | tf_op args[9]
  4.2 119.9 %step.1 = (f32[1,16]{1,0:T(1,128)}, f32[2,48,3072]{2,1,0:T(8,128)}, f32[2,192,384]{2,1,0:T(8,128)}, f32[48,10]{1,0:T(8,128)}, f32[24,384]{1,0:T(8,128)}, /*index...) custom-call(bf16[192,128]{1,0:T(8,128)(2,1)} %bitcast.17, bf16[192,384]{1,0:T(8,128)(2,1)} %embed.1, ...), custom_call_target="tpu_custom_call" | custom-call | tf_op jit(solution)/shard_map/step/pallas_call | solution.py:785
  124.2 1.4 %copy.21 = f32[48,10]{0,1:T(8,128)} copy(f32[48,10]{1,0:T(8,128)} %get-tuple-element.39) | data formatting | bytes 3840
  125.6 1.1 copy.31
  126.7 1.3 copy.32
  127.9 1.3 copy.33
  129.2 1.4 %copy.34 = f32[384,24]{0,1:T(8,128)} copy(f32[384,24]{0,1:T(8,128)} %bitcast.18) | data formatting | bytes 73728
  130.6 1.3 copy.35
  131.9 0.0 copy-start
  131.9 2.4 %copy.36 = f32[2,48,3072]{2,1,0:T(8,128)} copy(f32[2,48,3072]{2,1,0:T(8,128)} %get-tuple-element.53) | data formatting | bytes 2359296
  134.4 0.0 copy-done
  134.4 0.8 copy.37
Async XLA Ops:
  131.9 2.4 %copy-start = (f32[2,192,384]{2,1,0:T(8,128)S(1)}, f32[2,192,384]{2,1,0:T(8,128)}, u32[]{:S(2)}) copy-start(f32[2,192,384]{2,1,0:T(8,128)} %get-tuple-element.54) | copy-start | bytes 1769476

commit v3 on v2

--- a/solution.py
+++ b/solution.py
@@ -12,6 +12,7 @@
 TOK = 16
 IMG = 8
 CLASSES = 10
+SHARDS = 16
 LAYERS = 2
 CAP = 16
 EPSILON = 1e-06
@@ -30,6 +31,7 @@
 VMEM = pl.BlockSpec(memory_space=pltpu.VMEM)
 SMEM = pl.BlockSpec(memory_space=pltpu.SMEM)
 ANY = pl.BlockSpec(memory_space=pl.ANY)
+HBM = pl.BlockSpec(memory_space=pltpu.HBM)
 
 
 def mm(a, b, ca=1, cb=0):
@@ -304,7 +306,7 @@
     mine = (iota((128, 16), 0) & 15) == iota((128, 16), 1)
     label = jnp.sum(jnp.where(mine, tall, 0.0), axis=1, keepdims=True)
     onehot = (label == iota((128, CLASSES), 1).astype(f32)).astype(f32).astype(bf16)
-    return selector, mm(selector, onehot)
+    return selector, mm(selector, onehot), arow * CAP + rank
 
 
 def slot_rows(selector, arrived):
@@ -342,7 +344,11 @@
     arrived=((4, 4, IMG, TOK, D), bf16),
     win=((LAYERS, D, 4 * D + FF), bf16),
     wdn=((LAYERS, FF, D), bf16),
-    cls=((CLASSES, D), bf16),
+    win_c=((1, D, 4 * D + FF), bf16),
+    wdn_c=((1, FF, D), bf16),
+    win_s=((LAYERS, 48, 4 * D + FF), bf16),
+    wdn_s=((LAYERS, 192, D), bf16),
+    table=((1, 128), jnp.int32),
     cut=((IMG, TOK, D), bf16),
     packed=((8, PACK, D), bf16),
     swapped=((4, PACK, D), bf16),
@@ -380,7 +386,8 @@
 N_SEM = 160
 
 
-def step_kernel(patches_t, embed, positions, win_c, wdn_c, win_s, wdn_s, arow, labels, source, classes, *refs):
+def step_kernel(patches_t, embed, positions, arow, labels, classes, *refs):
+    sources, refs = refs[:4], refs[4:]
     losses, gin, gdn, gcls_out, out_in, out_dn, out_pe, out_pos = refs[:8]
     refs = list(refs[8:])
     C = dict(zip(CLIENT, refs[: len(CLIENT)]))
@@ -388,7 +395,13 @@
     S = dict(zip(SERVER, refs[: len(SERVER)]))
     refs = refs[len(SERVER) :]
     B = dict(zip(BUFFERS, refs[: len(BUFFERS)]))
-    send_sem, recv_sem, local_sem = refs[len(BUFFERS) :]
+    send_sem, recv_sem, local_sem, source = refs[len(BUFFERS) :]
+    win_c, wdn_c, win_s, wdn_s = B["win_c"], B["wdn_c"], B["win_s"], B["wdn_s"]
+    loads = []
+    for n, (src, dst) in enumerate(zip(sources, (win_c, wdn_c, win_s, wdn_s))):
+        loads.append(pltpu.make_async_copy(src, dst, local_sem.at[n]))
+    for n in (2, 3, 0, 1):
+        loads[n].start()
     place = Place()
     x, z, y, c, r = place.x, place.z, place.y, place.c, place.r
     shard = place.me // 8
@@ -408,7 +421,8 @@
 
     pieces = [(l, down) for l in range(LAYERS) for down in (False, True)]
     base = {piece: 8 + 9 * n for n, piece in enumerate(pieces)}
-    for piece in pieces:
+
+    def spread_own(piece):
         l, down = piece
         mine = (wdn_s if down else win_s).at[l]
         here = window(l, down, r, None)
@@ -416,8 +430,11 @@
         wire.send(mine, here, base[piece] + 1, place.ym)
         wire.send(mine, here, base[piece] + 4, place.partner)
         here[...] = mine[...]
-    copy = pltpu.make_async_copy(classes.at[shard], B["cls"], local_sem)
-    copy.start()
+
+    loads[2].wait()
+    spread_own(pieces[0])
+    for n in (3, 0, 1):
+        loads[n].wait()
 
     def forward(piece):
         l, down = piece
@@ -456,7 +473,13 @@
     for i in range(1, 8):
         j = (r + i) % 8
         wire.send(B["cut"].at[j], arrived.at[x, z, r], i, place.group + j)
+    for piece in pieces[1:]:
+        spread_own(piece)
     arrived[x, z, r] = B["cut"][r]
+    selector, hot, table = route(arow[...], labels[...], shard, r)
+    B["table"][...] = table
+    to_scalar = pltpu.make_async_copy(B["table"], source, local_sem.at[4])
+    to_scalar.start()
     first, second, third, fourth, fifth = plane_gather(wire, place, arrived, IMG, 44)
     forward(pieces[0])
     for i in range(1, 8):
@@ -465,7 +488,6 @@
     first()
     forward(pieces[1])
     second()
-    selector, hot = route(arow[...], labels[...], shard, r)
     col = iota((1, 512), 1)
     at = col & 15
     wanted = ((col >> 4) & 15) * 24 + (at // 3) * 6 + (col >> 8) * 3 + at % 3
@@ -490,8 +512,10 @@
     settle(pieces[2])
     settle(pieces[3])
     S["x"][2] = block_forward(1, 256, S, win, wdn)
-    copy.wait()
-    loss, gcls, dlast = head_loss(S["x"][LAYERS], B["cls"][...], hot)
+    to_scalar.wait()
+    ours = iota((CLASSES, SHARDS, D), 1) == shard
+    table = jnp.sum(jnp.where(ours, classes[...].astype(f32), 0.0), axis=1).astype(bf16)
+    loss, gcls, dlast = head_loss(S["x"][LAYERS], table, hot)
     losses[...] = loss
     for k in range(8):
         packed[k, PACK - 48 :, 0:CLASSES] = gcls[48 * k : 48 * k + 48]
@@ -566,12 +590,12 @@
     for k in (2, 1, 3, 0):
         for m in range(8):
             zd, xd = (z + k) % 4, (x + k) % 4
-            at = source[(x * 4 + zd) * 8 + m]
-            here = (at // 16 % 4 == z) & (at % 16 < 8)
-            B["pick_x"][k, m] = jnp.where(here, line_x[at // 64, at % 8].astype(f32), 0.0).astype(bf16)
-            at = source[(xd * 4 + z) * 8 + m]
-            here = (at // 64 == x) & (at % 16 >= 8)
-            B["pick_z"][k, m] = jnp.where(here, line_z[at // 16 % 4, at % 8].astype(f32), 0.0).astype(bf16)
+            at = source[0, (x * 4 + zd) * 8 + m]
+            here = ((at >> 4) & 3 == z) & ((at & 15) < 8)
+            B["pick_x"][k, m] = jnp.where(here, line_x[(at >> 6) & 3, at & 7].astype(f32), 0.0).astype(bf16)
+            at = source[0, (xd * 4 + z) * 8 + m]
+            here = ((at >> 6) & 3 == x) & ((at & 15) >= 8)
+            B["pick_z"][k, m] = jnp.where(here, line_z[(at >> 4) & 3, at & 7].astype(f32), 0.0).astype(bf16)
         if k:
             wire.send(B["pick_x"].at[k], B["got_x"].at[k - 1], 67 + k, place.at(0, k, 0))
             wire.send(B["pick_z"].at[k], B["got_z"].at[k - 1], 70 + k, place.at(k, 0, 0))
@@ -748,7 +772,7 @@
             gin[l, :, D * b : D * b + D] = total_of(576 * l + 48 * b, 48)
         for b in range(4):
             gdn[l, 48 * b : 48 * b + 48, :] = total_of(576 * l + D + 48 * b, 48)
-    gcls_out[...] = total_of(PACK - 48, 48)[:, 0:CLASSES]
+    gcls_out[...] = total_of(PACK - 48, 48)[:, 0:128].T[0:CLASSES]
 
     for k in range(1, 4):
         wire.wait(B["three_x"].at[k - 1], 130 + k, place.at(0, 0, 4 - k))
@@ -766,45 +790,69 @@
     wire.finish()
 
 
+def finish_kernel(*refs):
+    count = len(refs) // 3
+    given, results, held = refs[:count], refs[count : 2 * count], refs[2 * count : 3 * count]
+    sem = refs[-1]
+    inward = [pltpu.make_async_copy(given[n], held[n], sem.at[0, n]) for n in range(count)]
+    outward = [pltpu.make_async_copy(held[n], results[n], sem.at[1, n]) for n in range(count)]
+    for copy in inward:
+        copy.start()
+    for copy, onward in zip(inward, outward):
+        copy.wait()
+        onward.start()
+    for copy in outward:
+        copy.wait()
+
+
 def per_device(patches, labels, assign, patch_embed, positions, client_in, client_down, server_in, server_down, classifier):
-    routes = assign[:, 0]
-    places = jnp.arange(128, dtype=jnp.int32)
-    earlier = (routes[:, None] == routes[None, :]) & (places[:, None] < places[None, :])
-    source = routes * CAP + jnp.sum(earlier.astype(jnp.int32), axis=0)
     shapes = [
         ((1, CAP), f32),
         ((LAYERS, 48, 4 * D + FF), f32),
         ((LAYERS, 192, D), f32),
-        ((48, CLASSES), f32),
+        ((CLASSES, 48), f32),
         ((24, D), f32),
         ((3, FF), f32),
         ((3, 192), f32),
         ((3, TOK), f32),
     ]
     scratch = list(CLIENT.values()) + list(SERVER.values()) + list(BUFFERS.values())
-    losses, gin, gdn, gcls, out_in, out_dn, out_pe, out_pos = pl.pallas_call(
+    results = pl.pallas_call(
         step_kernel,
         out_shape=[jax.ShapeDtypeStruct(*s) for s in shapes],
-        in_specs=[VMEM] * 9 + [SMEM, ANY],
+        in_specs=[VMEM] * 6 + [ANY] * 4,
         out_specs=[VMEM] * len(shapes),
         scratch_shapes=[pltpu.VMEM(*s) for s in scratch]
-        + [pltpu.SemaphoreType.DMA((N_SEM,)), pltpu.SemaphoreType.DMA((N_SEM,)), pltpu.SemaphoreType.DMA],
+        + [
+            pltpu.SemaphoreType.DMA((N_SEM,)),
+            pltpu.SemaphoreType.DMA((N_SEM,)),
+            pltpu.SemaphoreType.DMA((5,)),
+            pltpu.SMEM((1, 128), jnp.int32),
+        ],
         compiler_params=pltpu.CompilerParams(collective_id=0, has_side_effects=True, vmem_limit_bytes=67043328),
         name="step",
     )(
         patches.T,
         patch_embed,
         positions,
+        assign.reshape(1, 128),
+        labels.reshape(8, 128),
+        classifier.transpose(2, 0, 1),
         client_in[None],
         client_down[None],
         server_in,
         server_down,
-        assign.reshape(1, 128),
-        labels.reshape(8, 128),
-        source,
-        classifier.transpose(0, 2, 1),
     )
-    return losses, out_pe.T, out_pos.T, out_in.T, out_dn.T, gin, gdn, gcls
+    losses, gin, gdn, gcls, out_in, out_dn, out_pe, out_pos = pl.pallas_call(
+        finish_kernel,
+        out_shape=[jax.ShapeDtypeStruct(*s) for s in shapes],
+        in_specs=[HBM] * len(shapes),
+        out_specs=[HBM] * len(shapes),
+        scratch_shapes=[pltpu.VMEM(*s) for s in shapes] + [pltpu.SemaphoreType.DMA((2, len(shapes)))],
+        compiler_params=pltpu.CompilerParams(vmem_limit_bytes=67043328),
+        name="finish",
+    )(*results)
+    return losses, out_pe.T, out_pos.T, out_in.T, out_dn.T, gin, gdn, gcls.T
 
 
 def solution(mesh):

time: 136 us -> 113 us (0.83)
  local copies, waits for them, and re-layouts: 12.6 us -> 0 us
  Pallas kernels: 120 us -> 112 us
  other arithmetic: 2 us -> 0 us
    unnamed x11 -> x0, local copies, waits for them, and re-layouts: 12.6 us -> none
    pallas_call x1, Pallas kernels: 120 us -> 109 us  [per_device(): pl.pallas_call(step_kernel, out_shape=[jax.ShapeDtypeStruct(*s) for s in...]
    pallas_call x0 -> x1, Pallas kernels: none -> 2.63 us  [per_device(): pl.pallas_call(finish_kernel, out_shape=[jax.ShapeDtypeStruct(*s) for s i...]
where the time goes in v3:
time: 113 us
  Pallas kernels  112 us (99%)
    pallas_call x1, Pallas kernels, per_device(): pl.pallas_call(step_kernel, out_shape=[jax.ShapeDtypeStruct(*s) for s in...  109 us
    pallas_call x1, Pallas kernels, per_device(): pl.pallas_call(finish_kernel, out_shape=[jax.ShapeDtypeStruct(*s) for s i...  2.63 us

profile of v3, /device:TPU:0, one launch (start us, length us, event | category | flops | bytes accessed | tf_op | source)
XLA Modules:
  0.0 112.6 jit_solution(13614837334216100701)
XLA Ops:
  0.6 109.2 %step.1 = (f32[1,16]{1,0:T(1,128)}, f32[2,48,3072]{2,1,0:T(8,128)}, f32[2,192,384]{2,1,0:T(8,128)}, f32[10,48]{1,0:T(8,128)}, f32[24,384]{1,0:T(8,128)}, /*index...) custom-call(bf16[192,128]{1,0:T(8,128)(2,1)} %bitcast.14, bf16[192,384]{1,0:T(8,128)(2,1)} %embed.1, ...), custom_call_target="tpu_custom_call" | custom-call | tf_op jit(solution)/shard_map/step/pallas_call | solution.py:820
  109.8 2.6 %finish.1 = (f32[1,16]{1,0:T(1,128)}, f32[2,48,3072]{2,1,0:T(8,128)}, f32[2,192,384]{2,1,0:T(8,128)}, f32[10,48]{1,0:T(8,128)}, f32[24,384]{1,0:T(8,128)}, /*ind...) custom-call(f32[1,16]{1,0:T(1,128)} %get-tuple-element.24.refs_0_, f32[2,48,3072]{2,1,0:T(8,128)} %get-tuple-element.25.refs_1_, ...), custom_call_target="tpu_custom_call" | custom-call | tf_op jit(solution)/shard_map/finish/pallas_call | solution.py:846

commit v4 on v3

--- a/solution.py
+++ b/solution.py
@@ -22,7 +22,8 @@
 PACK = LAYERS * (D + FF // 8) + D // 8
 CUT_A = 576
 MAIN = 96
-TAIL = 80
+TAIL = 64
+PART = 80
 BLOCK = MAIN + TAIL
 
 bf16 = jnp.bfloat16
@@ -107,7 +108,7 @@
     return S["x1"][l] + mm(S["h"][l], wdn[l])
 
 
-def block_backward(l, rows, S, win, wdn, dy_ref):
+def block_backward(l, rows, S, win, wdn, dy_ref, early=None):
     dyb = dy_ref[...].astype(bf16)
     S["dyb"][l] = dyb
     for n in range(4):
@@ -117,6 +118,8 @@
         bent = jnp.tanh(GELU_A * (pre + GELU_B * pre * pre * pre))
         slope = 0.5 * (1.0 + bent) + 0.5 * pre * (1.0 - bent * bent) * GELU_A * (1.0 + 3.0 * GELU_B * pre * pre)
         S["dpre"][l, :, cols] = (dh * slope).astype(bf16)
+    if early is not None:
+        early()
     du2 = rounded(mm(S["dpre"][l], win[l, :, 4 * D :], 1, 1))
     dx1 = dy_ref[...] + norm_back(S["x1"][l], du2)
     dy_ref[...] = dx1
@@ -226,58 +229,64 @@
             copy.wait_send()
 
 
-def plane_gather(wire, place, buf, count, k0):
-    half, quarter = count // 2, count // 4
+class Line:
+    def __init__(self, wire, me, up, down, k, view):
+        self.wire, self.me, self.up, self.down, self.k, self.view = wire, me, up, down, k, view
+
+    def both(self, ref, k, device):
+        self.wire.send(ref, ref, self.k + k, device)
+
+    def send(self):
+        self.both(self.view(self.me, 0), 0, self.up)
+        self.both(self.view(self.me, 1), 1, self.down)
+        self.both(self.view(self.me, 1), 2, self.up)
+        self.both(self.view(self.me, 0), 3, self.down)
+
+    def relay(self):
+        left, right = (self.me + 3) % 4, (self.me + 1) % 4
+        self.wire.wait(self.view(left, 0), self.k, self.down)
+        self.both(self.view(left, 0), 4, self.up)
+        self.wire.wait(self.view(right, 1), self.k + 1, self.up)
+        self.both(self.view(right, 1), 5, self.down)
+
+    def rest(self):
+        left, right, far = (self.me + 3) % 4, (self.me + 1) % 4, (self.me + 2) % 4
+        self.wire.wait(self.view(left, 1), self.k + 2, self.down)
+        self.wire.wait(self.view(right, 0), self.k + 3, self.up)
+        self.wire.wait(self.view(far, 0), self.k + 4, self.down)
+        self.wire.wait(self.view(far, 1), self.k + 5, self.up)
+
+
+def plane_gather(wire, place, buf, k0):
     x, z = place.x, place.z
-    xm, xp, zm, zp = (x + 3) % 4, (x + 1) % 4, (z + 3) % 4, (z + 1) % 4
-    xo, zo = (x + 2) % 4, (z + 2) % 4
-    X, XA, XB = pl.ds(0, half), pl.ds(0, quarter), pl.ds(quarter, quarter)
-    Z, ZA, ZB = pl.ds(half, half), pl.ds(half, quarter), pl.ds(half + quarter, quarter)
-
-    def both(ref, k, device):
-        wire.send(ref, ref, k0 + k, device)
+    lines = (
+        Line(wire, x, place.xp, place.xm, k0, lambda at, h: buf.at[at, z, pl.ds(2 * h, 2)]),
+        Line(wire, z, place.zp, place.zm, k0 + 6, lambda at, h: buf.at[x, at, pl.ds(4 + 2 * h, 2)]),
+        Line(wire, z, place.zp, place.zm, k0 + 12, lambda at, h: buf.at[pl.ds(2 * h, 2), at, pl.ds(0, 4)]),
+        Line(wire, x, place.xp, place.xm, k0 + 18, lambda at, h: buf.at[at, pl.ds(2 * h, 2), pl.ds(4, 4)]),
+    )
 
     def first():
-        both(buf.at[x, z, X], 0, place.xp)
-        both(buf.at[x, z, X], 1, place.xm)
-        both(buf.at[x, z, Z], 2, place.zp)
-        both(buf.at[x, z, Z], 3, place.zm)
+        lines[0].send()
+        lines[1].send()
 
     def second():
-        wire.wait(buf.at[xm, z, X], k0 + 0, place.xm)
-        both(buf.at[xm, z, XA], 4, place.xp)
-        wire.wait(buf.at[xp, z, X], k0 + 1, place.xp)
-        both(buf.at[xp, z, XB], 5, place.xm)
-        wire.wait(buf.at[x, zm, Z], k0 + 2, place.zm)
-        both(buf.at[x, zm, ZA], 6, place.zp)
-        wire.wait(buf.at[x, zp, Z], k0 + 3, place.zp)
-        both(buf.at[x, zp, ZB], 7, place.zm)
+        lines[0].relay()
+        lines[1].relay()
 
     def third():
-        wire.wait(buf.at[xo, z, XA], k0 + 4, place.xm)
-        wire.wait(buf.at[xo, z, XB], k0 + 5, place.xp)
-        both(buf.at[:, z, X], 8, place.zp)
-        both(buf.at[:, z, X], 9, place.zm)
-        wire.wait(buf.at[x, zo, ZA], k0 + 6, place.zm)
-        wire.wait(buf.at[x, zo, ZB], k0 + 7, place.zp)
-        both(buf.at[x, :, Z], 10, place.xp)
-        both(buf.at[x, :, Z], 11, place.xm)
+        lines[0].rest()
+        lines[2].send()
+        lines[1].rest()
+        lines[3].send()
 
     def fourth():
-        wire.wait(buf.at[:, zm, X], k0 + 8, place.zm)
-        both(buf.at[0:2, zm, X], 12, place.zp)
-        wire.wait(buf.at[:, zp, X], k0 + 9, place.zp)
-        both(buf.at[2:4, zp, X], 13, place.zm)
-        wire.wait(buf.at[xm, :, Z], k0 + 10, place.xm)
-        both(buf.at[xm, 0:2, Z], 14, place.xp)
-        wire.wait(buf.at[xp, :, Z], k0 + 11, place.xp)
-        both(buf.at[xp, 2:4, Z], 15, place.xm)
+        lines[2].relay()
+        lines[3].relay()
 
     def fifth():
-        wire.wait(buf.at[0:2, zo, X], k0 + 12, place.zm)
-        wire.wait(buf.at[2:4, zo, X], k0 + 13, place.zp)
-        wire.wait(buf.at[xo, 0:2, Z], k0 + 14, place.xm)
-        wire.wait(buf.at[xo, 2:4, Z], k0 + 15, place.xp)
+        lines[2].rest()
+        lines[3].rest()
 
     return first, second, third, fourth, fifth
 
@@ -364,24 +373,26 @@
     got_z=((3, 8, TOK, D), bf16),
     picked=((8, TOK, D), bf16),
     own=((IMG, TOK, D), bf16),
-    order=((D, 512), bf16),
-    dperm=((128, 512), bf16),
+    order=((4, D, 512), bf16),
+    dperm=((2, 128, 512), bf16),
     pp=((128, D), bf16),
     cpack=((16, 2, BLOCK, D), bf16),
     cswap=((16, BLOCK, D), bf16),
     cmine=((4, 4, BLOCK, D), bf16),
-    hop_x=((2, 2, MAIN, D), bf16),
-    hop_z=((2, 2, TAIL, D), bf16),
-    end_x=((2, 4, MAIN, D), bf16),
-    end_z=((2, 4, TAIL, D), bf16),
-    half_x=((4, MAIN, D), bf16),
-    half_z=((4, TAIL, D), bf16),
-    two_x=((3, MAIN, D), bf16),
-    two_z=((3, TAIL, D), bf16),
+    hop_x=((2, 2, PART, D), bf16),
+    hop_z=((2, 2, PART, D), bf16),
+    end_x=((2, 4, PART, D), bf16),
+    end_z=((2, 4, PART, D), bf16),
+    half_x=((4, PART, D), bf16),
+    half_z=((4, PART, D), bf16),
+    two_x=((3, PART, D), bf16),
+    two_z=((3, PART, D), bf16),
     low_x=((4, 24, D), bf16),
     low_z=((4, 16, D), bf16),
     three_x=((3, 24, D), bf16),
     three_z=((3, 16, D), bf16),
+    gin=((LAYERS, 48, 4 * D + FF), f32),
+    gdn=((LAYERS, 192, D), f32),
 )
 N_SEM = 160
 
@@ -420,19 +431,29 @@
         return win.at[l, pl.ds(pl.multiple_of(rank * 48, 16), 48), cols]
 
     pieces = [(l, down) for l in range(LAYERS) for down in (False, True)]
-    base = {piece: 8 + 9 * n for n, piece in enumerate(pieces)}
-
-    def spread_own(piece):
+    base = {piece: 8 + 11 * n for n, piece in enumerate(pieces)}
+
+    def own_part(piece, part):
+        l, down = piece
+        if down:
+            return wdn_s.at[l, pl.ds(96 * part, 96), :]
+        return win_s.at[l, :, pl.ds(1536 * part, 1536)]
+
+    def spread_first(piece):
+        for part, device in ((0, place.yp), (1, place.ym)):
+            wire.send(own_part(piece, part), window(*piece, r, part), base[piece] + part, device)
+
+    def spread_last(piece):
+        for part, device in ((1, place.yp), (0, place.ym)):
+            wire.send(own_part(piece, part), window(*piece, r, part), base[piece] + 3 - part, device)
         l, down = piece
         mine = (wdn_s if down else win_s).at[l]
         here = window(l, down, r, None)
-        wire.send(mine, here, base[piece] + 0, place.yp)
-        wire.send(mine, here, base[piece] + 1, place.ym)
-        wire.send(mine, here, base[piece] + 4, place.partner)
+        wire.send(mine, here, base[piece] + 6, place.partner)
         here[...] = mine[...]
 
     loads[2].wait()
-    spread_own(pieces[0])
+    spread_first(pieces[0])
     for n in (3, 0, 1):
         loads[n].wait()
 
@@ -440,31 +461,36 @@
         l, down = piece
         b = base[piece]
         left, right = owner(3), owner(1)
-        whole, half = window(l, down, left, None), window(l, down, left, 0)
-        wire.wait(whole, b + 0, place.ym)
-        wire.send(half, half, b + 2, place.yp)
-        wire.send(whole, whole, b + 5, place.partner)
-        whole, half = window(l, down, right, None), window(l, down, right, 1)
-        wire.wait(whole, b + 1, place.yp)
-        wire.send(half, half, b + 3, place.ym)
-        wire.send(whole, whole, b + 6, place.partner)
+        half = window(l, down, left, 0)
+        wire.wait(half, b + 0, place.ym)
+        wire.send(half, half, b + 4, place.yp)
+        half = window(l, down, right, 1)
+        wire.wait(half, b + 1, place.yp)
+        wire.send(half, half, b + 5, place.ym)
 
     def across(piece):
         l, down = piece
         b = base[piece]
+        left, right, far = owner(3), owner(1), owner(2)
+        wire.wait(window(l, down, left, 1), b + 2, place.ym)
+        whole = window(l, down, left, None)
+        wire.send(whole, whole, b + 7, place.partner)
+        wire.wait(window(l, down, right, 0), b + 3, place.yp)
+        whole = window(l, down, right, None)
+        wire.send(whole, whole, b + 8, place.partner)
         for part, device in ((0, place.ym), (1, place.yp)):
-            half = window(l, down, owner(2), part)
-            wire.wait(half, b + 2 + part, device)
-            wire.send(half, half, b + 7 + part, place.partner)
+            half = window(l, down, far, part)
+            wire.wait(half, b + 4 + part, device)
+            wire.send(half, half, b + 9 + part, place.partner)
 
     def settle(piece):
         l, down = piece
         b = base[piece]
-        wire.wait(window(l, down, owner(0, True), None), b + 4, place.partner)
-        wire.wait(window(l, down, owner(3, True), None), b + 5, place.partner)
-        wire.wait(window(l, down, owner(1, True), None), b + 6, place.partner)
+        wire.wait(window(l, down, owner(0, True), None), b + 6, place.partner)
+        wire.wait(window(l, down, owner(3, True), None), b + 7, place.partner)
+        wire.wait(window(l, down, owner(1, True), None), b + 8, place.partner)
         for part in range(2):
-            wire.wait(window(l, down, owner(2, True), part), b + 7 + part, place.partner)
+            wire.wait(window(l, down, owner(2, True), part), b + 9 + part, place.partner)
 
     tiled = jnp.concatenate([positions[...].astype(f32)] * IMG, axis=0)
     C["x"][0] = mm(patches_t[...], embed[...], 0, 0) + tiled
@@ -473,41 +499,48 @@
     for i in range(1, 8):
         j = (r + i) % 8
         wire.send(B["cut"].at[j], arrived.at[x, z, r], i, place.group + j)
+    spread_last(pieces[0])
     for piece in pieces[1:]:
-        spread_own(piece)
+        spread_first(piece)
+        spread_last(piece)
     arrived[x, z, r] = B["cut"][r]
     selector, hot, table = route(arow[...], labels[...], shard, r)
     B["table"][...] = table
     to_scalar = pltpu.make_async_copy(B["table"], source, local_sem.at[4])
     to_scalar.start()
-    first, second, third, fourth, fifth = plane_gather(wire, place, arrived, IMG, 44)
-    forward(pieces[0])
+    first, second, third, fourth, fifth = plane_gather(wire, place, arrived, 52)
     for i in range(1, 8):
         j = (r - i + 8) % 8
         wire.wait(arrived.at[x, z, j], i, place.group + j)
     first()
-    forward(pieces[1])
+    forward(pieces[0])
     second()
     col = iota((1, 512), 1)
     at = col & 15
-    wanted = ((col >> 4) & 15) * 24 + (at // 3) * 6 + (col >> 8) * 3 + at % 3
-    B["order"][...] = ((iota((D, 512), 0) == wanted) & (at < 12)).astype(f32).astype(bf16)
+    lane = ((col >> 4) & 15) * 24 + (col >> 8) * 3
+    wanted = lane + (at // 3) * 6 + at % 3
+    B["order"][0] = ((iota((D, 512), 0) == wanted) & (at < 12)).astype(f32).astype(bf16)
+    for q in range(3):
+        entry = jnp.maximum(at - 12, 0) + 4 * q
+        wanted = lane + (entry // 3) * 6 + entry % 3
+        B["order"][1 + q] = ((iota((D, 512), 0) == wanted) & (at >= 12)).astype(f32).astype(bf16)
     B["pp"][...] = (iota((128, D), 1) - 256 == (iota((128, D), 0) & 15)).astype(f32).astype(bf16)
     B["pp"][:, 0:192] = patches_t[...].T
     packed[:, PACK - 48 :, :] = jnp.zeros((8, 48, D), bf16)
+    forward(pieces[1])
     third()
-    across(pieces[0])
     forward(pieces[2])
-    across(pieces[1])
     fourth()
     forward(pieces[3])
+    across(pieces[0])
     fifth()
-    across(pieces[2])
+    across(pieces[1])
     settle(pieces[0])
     settle(pieces[1])
 
     S["x"][0] = slot_rows(selector, arrived[...].reshape(2048, D))
     S["x"][1] = block_forward(0, 256, S, win, wdn)
+    across(pieces[2])
     across(pieces[3])
     settle(pieces[2])
     settle(pieces[3])
@@ -531,11 +564,12 @@
     gcut = S["dy"][...].astype(bf16).reshape(CAP, TOK, D)
     line_x[x] = gcut[:8]
     line_z[z] = gcut[8:]
-    lo, hi, all8 = pl.ds(0, 4), pl.ds(4, 4), pl.ds(0, 8)
-    lines = ((line_x, x, place.xp, place.xm, 60), (line_z, z, place.zp, place.zm, 64))
-    for buf, me, up, down, k0 in lines:
-        wire.send(buf.at[me], buf.at[me], k0, up)
-        wire.send(buf.at[me], buf.at[me], k0 + 1, down)
+    lines = (
+        Line(wire, x, place.xp, place.xm, 76, lambda at, h: line_x.at[at, pl.ds(4 * h, 4)]),
+        Line(wire, z, place.zp, place.zm, 82, lambda at, h: line_z.at[at, pl.ds(4 * h, 4)]),
+    )
+    for line in lines:
+        line.send()
 
     def server_weights(l):
         for b, u, dout in weight_pairs(S, l):
@@ -566,27 +600,21 @@
         add_rows(start, stop, 48, body)
 
     def combine_a(k):
-        combine(k, rows_a, 80, 0, CUT_A)
+        combine(k, rows_a, 94, 0, CUT_A)
 
     def combine_b(k):
-        combine(k, rows_b, 84, CUT_A, PACK)
+        combine(k, rows_b, 98, CUT_A, PACK)
 
     server_weights(1)
-    swap(rows_b, 84)
-    for buf, me, up, down, k0 in lines:
-        left, right = (me + 3) % 4, (me + 1) % 4
-        wire.wait(buf.at[left], k0, down)
-        wire.send(buf.at[left, lo], buf.at[left, lo], k0 + 2, up)
-        wire.wait(buf.at[right], k0 + 1, up)
-        wire.send(buf.at[right, hi], buf.at[right, hi], k0 + 3, down)
+    swap(rows_b, 98)
+    for line in lines:
+        line.relay()
     combine_b(2)
-    wire.send(packed.at[row(2, c), rows_b], B["from_p"], 88, place.ym)
+    wire.send(packed.at[row(2, c), rows_b], B["from_p"], 102, place.ym)
     combine_b(1)
-    wire.send(packed.at[row(1, c), rows_b], B["fin_p"].at[rows_b], 89, place.yp)
-    for buf, me, up, down, k0 in lines:
-        far = (me + 2) % 4
-        wire.wait(buf.at[far, lo], k0 + 2, down)
-        wire.wait(buf.at[far, hi], k0 + 3, up)
+    wire.send(packed.at[row(1, c), rows_b], B["fin_p"].at[rows_b], 103, place.yp)
+    for line in lines:
+        line.rest()
     for k in (2, 1, 3, 0):
         for m in range(8):
             zd, xd = (z + k) % 4, (x + k) % 4
@@ -597,13 +625,13 @@
             here = ((at >> 6) & 3 == x) & ((at & 15) >= 8)
             B["pick_z"][k, m] = jnp.where(here, line_z[(at >> 4) & 3, at & 7].astype(f32), 0.0).astype(bf16)
         if k:
-            wire.send(B["pick_x"].at[k], B["got_x"].at[k - 1], 67 + k, place.at(0, k, 0))
-            wire.send(B["pick_z"].at[k], B["got_z"].at[k - 1], 70 + k, place.at(k, 0, 0))
+            wire.send(B["pick_x"].at[k], B["got_x"].at[k - 1], 87 + k, place.at(0, k, 0))
+            wire.send(B["pick_z"].at[k], B["got_z"].at[k - 1], 90 + k, place.at(k, 0, 0))
     server_weights(0)
-    swap(rows_a, 80)
+    swap(rows_a, 94)
     for k in range(1, 4):
-        wire.wait(B["got_x"].at[k - 1], 67 + k, place.at(0, 4 - k, 0))
-        wire.wait(B["got_z"].at[k - 1], 70 + k, place.at(4 - k, 0, 0))
+        wire.wait(B["got_x"].at[k - 1], 87 + k, place.at(0, 4 - k, 0))
+        wire.wait(B["got_z"].at[k - 1], 90 + k, place.at(4 - k, 0, 0))
     for m in range(8):
         piece = B["pick_x"][0, m].astype(f32) + B["pick_z"][0, m].astype(f32)
         for k in range(3):
@@ -613,31 +641,22 @@
     own[r] = B["picked"][r]
     for i in range(1, 8):
         m = (r + i) % 8
-        wire.send(B["picked"].at[m], own.at[r], 91 + i, place.group + m)
+        wire.send(B["picked"].at[m], own.at[r], 108 + i, place.group + m)
     combine_a(2)
-    wire.send(packed.at[row(2, c), rows_a], B["from_m"], 90, place.yp)
+    wire.send(packed.at[row(2, c), rows_a], B["from_m"], 104, place.yp)
     combine_a(3)
-    wire.send(packed.at[row(3, c), rows_a], B["fin_m"].at[rows_a], 91, place.ym)
+    wire.send(packed.at[row(3, c), rows_a], B["fin_m"].at[rows_a], 105, place.ym)
     combine_a(1)
     combine_b(3)
     for i in range(1, 8):
         j = (r - i + 8) % 8
-        wire.wait(own.at[j], 91 + i, place.group + j)
+        wire.wait(own.at[j], 108 + i, place.group + j)
 
     C["dy"][...] = own[...].reshape(128, D).astype(f32)
-    block_backward(0, 128, C, win_c, wdn_c, C["dy"])
     cpack, cswap, cmine = B["cpack"], B["cswap"], B["cmine"]
-    B["dperm"][...] = mm(C["dyb"][0], B["order"][...]).astype(bf16)
-    for q in range(5):
-        if q == 4:
-            B["dperm"][...] = mm(C["dy"][...].astype(bf16), B["order"][...]).astype(bf16)
-        right = B["pp"][...] if q == 4 else C["h"][0, :, D * q : D * q + D]
-        val = mm(B["dperm"][...], right, 0, 0).astype(bf16)
-        for core in range(2):
-            for i in range(16):
-                cpack[i, core, MAIN + 16 * q : MAIN + 16 * q + 16] = val[256 * core + 16 * i : 256 * core + 16 * i + 16]
-    wire.send(cpack.at[:, 1 - c, pl.ds(MAIN, TAIL)], cswap.at[:, pl.ds(MAIN, TAIL)], 108, place.partner)
-    for b, u, dout in weight_pairs(C, 0):
+    pairs = weight_pairs(C, 0)
+
+    def emit(b, u, dout):
         val = mm(dout[...], u[...], 0, 0).astype(bf16)
         for i in range(2):
             for k in range(4):
@@ -645,9 +664,30 @@
                     low = 192 * i + 48 * k + 24 * core
                     cpack[2 * b + i, core, 24 * k : 24 * k + 24] = val[low : low + 24]
         pair = pl.ds(2 * b, 2)
-        wire.send(cpack.at[pair, 1 - c, pl.ds(0, MAIN)], cswap.at[pair, pl.ds(0, MAIN)], 100 + b, place.partner)
-
-    X, Z = pl.ds(0, MAIN), pl.ds(MAIN, TAIL)
+        wire.send(cpack.at[pair, 1 - c, pl.ds(0, MAIN)], cswap.at[pair, pl.ds(0, MAIN)], 116 + b, place.partner)
+
+    def early():
+        for pair in pairs[4:]:
+            emit(*pair)
+        B["dperm"][0] = mm(C["dyb"][0], B["order"][0]).astype(bf16)
+
+    block_backward(0, 128, C, win_c, wdn_c, C["dy"], early)
+    for pair in pairs[:4]:
+        emit(*pair)
+    last = C["dy"][...].astype(bf16)
+    for q in range(4):
+        val = mm(B["dperm"][0], C["h"][0, :, D * q : D * q + D], 0, 0)
+        if q < 3:
+            B["dperm"][1] = mm(last, B["order"][1 + q]).astype(bf16)
+            val = val + mm(B["dperm"][1], B["pp"][...], 0, 0)
+        val = val.astype(bf16)
+        for core in range(2):
+            for i in range(16):
+                low = 256 * core + 16 * i
+                cpack[i, core, MAIN + 16 * q : MAIN + 16 * q + 16] = val[low : low + 16]
+    wire.send(cpack.at[:, 1 - c, pl.ds(MAIN, TAIL)], cswap.at[:, pl.ds(MAIN, TAIL)], 124, place.partner)
+
+    X, Z = pl.ds(0, PART), pl.ds(PART, PART)
 
     def fold(low, high):
         for i in range(16):
@@ -684,30 +724,30 @@
         to = (x + k) % 4
         for i in range(2):
             at = 2 * part + i
-            cmine[to, at, :MAIN] = (cmine[to, at, :MAIN].astype(f32) + hop[part, i].astype(f32)).astype(bf16)
+            cmine[to, at, :PART] = (cmine[to, at, :PART].astype(f32) + hop[part, i].astype(f32)).astype(bf16)
 
     def load_z(k, part, hop):
         to = (z + k) % 4
         for i in range(2):
             at = 2 * part + i
-            cmine[at, to, MAIN:] = (cmine[at, to, MAIN:].astype(f32) + hop[part, i].astype(f32)).astype(bf16)
-
-    wire.wait(cswap.at[:, Z], 108, place.partner)
-    fold(MAIN, BLOCK)
-    ring_one(src_z, B["hop_z"], B["end_z"], place.zp, place.zm, 116)
-    for b in range(8):
-        wire.wait(cswap.at[pl.ds(2 * b, 2), X], 100 + b, place.partner)
-    fold(0, MAIN)
-    ring_one(src_x, B["hop_x"], B["end_x"], place.xp, place.xm, 110)
-
-    wire.wait(B["from_m"], 90, place.ym)
+            cmine[at, to, PART:] = (cmine[at, to, PART:].astype(f32) + hop[part, i].astype(f32)).astype(bf16)
+
+    for b in (4, 5, 6, 7, 0, 1, 2, 3):
+        wire.wait(cswap.at[pl.ds(2 * b, 2), pl.ds(0, MAIN)], 116 + b, place.partner)
+    fold(0, PART)
+    ring_one(src_x, B["hop_x"], B["end_x"], place.xp, place.xm, 125)
+    wire.wait(cswap.at[:, pl.ds(MAIN, TAIL)], 124, place.partner)
+    fold(PART, BLOCK)
+    ring_one(src_z, B["hop_z"], B["end_z"], place.zp, place.zm, 131)
+
+    wire.wait(B["from_m"], 104, place.ym)
 
     def add_a(rows):
         packed[row(1, c), rows, :] = (packed[row(1, c), rows, :].astype(f32) + B["from_m"][rows, :].astype(f32)).astype(bf16)
 
     add_rows(0, CUT_A, 48, add_a)
-    wire.send(packed.at[row(1, c), rows_a], B["fin_p"].at[rows_a], 122, place.yp)
-    wire.wait(B["from_p"], 88, place.yp)
+    wire.send(packed.at[row(1, c), rows_a], B["fin_p"].at[rows_a], 106, place.yp)
+    wire.wait(B["from_p"], 102, place.yp)
 
     def add_b(i, carry):
         here = pl.ds(pl.multiple_of(i * 48, 16), 48)
@@ -716,52 +756,54 @@
         return carry
 
     lax.fori_loop(0, (PACK - CUT_A) // 48, add_b, 0)
-    wire.send(packed.at[row(3, c), rows_b], B["fin_m"].at[rows_b], 123, place.ym)
-
-    ring_two(src_z, load_z, B["hop_z"], B["end_z"], place.zp, place.zm, 116)
-    ring_two(src_x, load_x, B["hop_x"], B["end_x"], place.xp, place.xm, 110)
+    wire.send(packed.at[row(3, c), rows_b], B["fin_m"].at[rows_b], 107, place.ym)
+
+    ring_two(src_x, load_x, B["hop_x"], B["end_x"], place.xp, place.xm, 125)
+    ring_two(src_z, load_z, B["hop_z"], B["end_z"], place.zp, place.zm, 131)
     half_x, half_z = B["half_x"], B["half_z"]
-    ring_three(B["end_z"], place.zp, place.zm, 116)
+    ring_three(B["end_x"], place.xp, place.xm, 125)
     for i in range(4):
-        total = cmine[i, z, MAIN:].astype(f32) + B["end_z"][0, i].astype(f32) + B["end_z"][1, i].astype(f32)
+        total = cmine[x, i, :PART].astype(f32) + B["end_x"][0, i].astype(f32) + B["end_x"][1, i].astype(f32)
+        half_x[i] = total.astype(bf16)
+    for k in (2, 1, 3):
+        wire.send(half_x.at[(z + k) % 4], B["two_x"].at[k - 1], 136 + k, place.at(0, k, 0))
+    ring_three(B["end_z"], place.zp, place.zm, 131)
+    for i in range(4):
+        total = cmine[i, z, PART:].astype(f32) + B["end_z"][0, i].astype(f32) + B["end_z"][1, i].astype(f32)
         half_z[i] = total.astype(bf16)
     for k in (2, 1, 3):
-        wire.send(half_z.at[(x + k) % 4], B["two_z"].at[k - 1], 127 + k, place.at(k, 0, 0))
-    ring_three(B["end_x"], place.xp, place.xm, 110)
-    for i in range(4):
-        total = cmine[x, i, :MAIN].astype(f32) + B["end_x"][0, i].astype(f32) + B["end_x"][1, i].astype(f32)
-        half_x[i] = total.astype(bf16)
-    for k in (2, 1, 3):
-        wire.send(half_x.at[(z + k) % 4], B["two_x"].at[k - 1], 124 + k, place.at(0, k, 0))
+        wire.send(half_z.at[(x + k) % 4], B["two_z"].at[k - 1], 139 + k, place.at(k, 0, 0))
     combine_a(0)
     combine_b(0)
     for k in range(1, 4):
-        wire.wait(B["two_z"].at[k - 1], 127 + k, place.at(4 - k, 0, 0))
-    tail = half_z[x].astype(f32)
+        wire.wait(B["two_x"].at[k - 1], 136 + k, place.at(0, 4 - k, 0))
+    upper = half_x[z].astype(f32)
     for k in range(3):
-        tail = tail + B["two_z"][k].astype(f32)
+        upper = upper + B["two_x"][k].astype(f32)
+    for k in range(1, 4):
+        wire.wait(B["two_z"].at[k - 1], 139 + k, place.at(4 - k, 0, 0))
+    lower = half_z[x].astype(f32)
+    for k in range(3):
+        lower = lower + B["two_z"][k].astype(f32)
     line, column = iota((64, TAIL), 0), iota((64, TAIL), 1)
-    inside = line & 15
-    pick = (column == (inside // 3) * 16 + (line >> 4) * 3 + inside % 3) & (inside < 15)
-    ordered = mm(pick.astype(f32).astype(bf16), tail.astype(bf16)).astype(bf16)
+    inside, owner_y = line & 15, line >> 4
+    entry = owner_y * 3 + inside % 3
+    spot = jnp.where(inside < 12, (inside // 3) * 16 + entry, (entry // 4) * 16 + 12 + entry % 4)
+    pick = (column == spot) & (inside < 15)
+    ordered = mm(pick.astype(f32).astype(bf16), lower[16:].astype(bf16)).astype(bf16)
+    main = jnp.concatenate([upper, lower[:16]], axis=0).astype(bf16)
     for k in range(4):
+        B["low_x"][k] = main[24 * k : 24 * k + 24]
         B["low_z"][k] = ordered[16 * k : 16 * k + 16]
-    for k in range(1, 4):
-        wire.wait(B["two_x"].at[k - 1], 124 + k, place.at(0, 4 - k, 0))
-    main = half_x[z].astype(f32)
-    for k in range(3):
-        main = main + B["two_x"][k].astype(f32)
-    for k in range(4):
-        B["low_x"][k] = main[24 * k : 24 * k + 24].astype(bf16)
     for k in (2, 1, 3):
         to = (y + k) % 4
-        wire.send(B["low_x"].at[to], B["three_x"].at[k - 1], 130 + k, place.at(0, 0, k))
-        wire.send(B["low_z"].at[to], B["three_z"].at[k - 1], 133 + k, place.at(0, 0, k))
-
-    wire.wait(B["fin_p"].at[rows_b], 89, place.ym)
-    wire.wait(B["fin_m"].at[rows_a], 91, place.yp)
-    wire.wait(B["fin_p"].at[rows_a], 122, place.ym)
-    wire.wait(B["fin_m"].at[rows_b], 123, place.yp)
+        wire.send(B["low_x"].at[to], B["three_x"].at[k - 1], 142 + k, place.at(0, 0, k))
+        wire.send(B["low_z"].at[to], B["three_z"].at[k - 1], 145 + k, place.at(0, 0, k))
+
+    wire.wait(B["fin_p"].at[rows_b], 103, place.ym)
+    wire.wait(B["fin_m"].at[rows_a], 105, place.yp)
+    wire.wait(B["fin_p"].at[rows_a], 106, place.ym)
+    wire.wait(B["fin_m"].at[rows_b], 107, place.yp)
 
     def total_of(first_row, rows):
         at = pl.ds(first_row, rows)
@@ -769,14 +811,20 @@
 
     for l in range(LAYERS):
         for b in range(8):
-            gin[l, :, D * b : D * b + D] = total_of(576 * l + 48 * b, 48)
+            B["gin"][l, :, D * b : D * b + D] = total_of(576 * l + 48 * b, 48)
         for b in range(4):
-            gdn[l, 48 * b : 48 * b + 48, :] = total_of(576 * l + D + 48 * b, 48)
+            B["gdn"][l, 48 * b : 48 * b + 48, :] = total_of(576 * l + D + 48 * b, 48)
+    leaving = [
+        pltpu.make_async_copy(B["gin"], gin, local_sem.at[5]),
+        pltpu.make_async_copy(B["gdn"], gdn, local_sem.at[6]),
+    ]
+    for copy in leaving:
+        copy.start()
     gcls_out[...] = total_of(PACK - 48, 48)[:, 0:128].T[0:CLASSES]
 
     for k in range(1, 4):
-        wire.wait(B["three_x"].at[k - 1], 130 + k, place.at(0, 0, 4 - k))
-        wire.wait(B["three_z"].at[k - 1], 133 + k, place.at(0, 0, 4 - k))
+        wire.wait(B["three_x"].at[k - 1], 142 + k, place.at(0, 0, 4 - k))
+        wire.wait(B["three_z"].at[k - 1], 145 + k, place.at(0, 0, 4 - k))
     main = B["low_x"][y].astype(f32)
     tail = B["low_z"][y].astype(f32)
     for k in range(3):
@@ -787,6 +835,8 @@
         out_dn[:, D * q : D * q + D] = tail[3 * q : 3 * q + 3]
     out_pe[...] = tail[12:15, 0:192]
     out_pos[...] = tail[12:15, 256:272]
+    for copy in leaving:
+        copy.wait()
     wire.finish()
 
 
@@ -821,12 +871,12 @@
         step_kernel,
         out_shape=[jax.ShapeDtypeStruct(*s) for s in shapes],
         in_specs=[VMEM] * 6 + [ANY] * 4,
-        out_specs=[VMEM] * len(shapes),
+        out_specs=[VMEM, HBM, HBM] + [VMEM] * 5,
         scratch_shapes=[pltpu.VMEM(*s) for s in scratch]
         + [
             pltpu.SemaphoreType.DMA((N_SEM,)),
             pltpu.SemaphoreType.DMA((N_SEM,)),
-            pltpu.SemaphoreType.DMA((5,)),
+            pltpu.SemaphoreType.DMA((7,)),
             pltpu.SMEM((1, 128), jnp.int32),
         ],
         compiler_params=pltpu.CompilerParams(collective_id=0, has_side_effects=True, vmem_limit_bytes=67043328),

time: 113 us -> 110 us (0.973)
  Pallas kernels: 112 us -> 109 us
    pallas_call x1, Pallas kernels: 109 us -> 107 us  [per_device(): pl.pallas_call(step_kernel, out_shape=[jax.ShapeDtypeStruct(*s) for s in...]
where the time goes in v4:
time: 110 us
  Pallas kernels  109 us (99%)
    pallas_call x1, Pallas kernels, per_device(): pl.pallas_call(step_kernel, out_shape=[jax.ShapeDtypeStruct(*s) for s in...  107 us
    pallas_call x1, Pallas kernels, per_device(): pl.pallas_call(finish_kernel, out_shape=[jax.ShapeDtypeStruct(*s) for s i...  2.63 us

profile of v4, /device:TPU:0, one launch (start us, length us, event | category | flops | bytes accessed | tf_op | source)
XLA Modules:
  0.0 110.2 jit_solution(6010528947578968357)
XLA Ops:
  0.6 106.7 %step.1 = (f32[1,16]{1,0:T(1,128)}, f32[2,48,3072]{2,1,0:T(8,128)}, f32[2,192,384]{2,1,0:T(8,128)}, f32[10,48]{1,0:T(8,128)}, f32[24,384]{1,0:T(8,128)}, /*index...) custom-call(bf16[192,128]{1,0:T(8,128)(2,1)} %bitcast.14, bf16[192,384]{1,0:T(8,128)(2,1)} %embed.1, ...), custom_call_target="tpu_custom_call" | custom-call | tf_op jit(solution)/shard_map/step/pallas_call | solution.py:870
  107.4 2.6 %finish.1 = (f32[1,16]{1,0:T(1,128)}, f32[2,48,3072]{2,1,0:T(8,128)}, f32[2,192,384]{2,1,0:T(8,128)}, f32[10,48]{1,0:T(8,128)}, f32[24,384]{1,0:T(8,128)}, /*ind...) custom-call(f32[1,16]{1,0:T(1,128)} %get-tuple-element.24.refs_0_, f32[2,48,3072]{2,1,0:T(8,128)} %get-tuple-element.25.refs_1_, ...), custom_call_target="tpu_custom_call" | custom-call | tf_op jit(solution)/shard_map/finish/pallas_call | solution.py:896

commit v5 on v4

--- a/solution.py
+++ b/solution.py
@@ -74,7 +74,7 @@
     return jnp.where(iota((rows, 128), 1) < 64, v[:rows], v[rows:])
 
 
-def block_forward(l, rows, S, win, wdn):
+def block_forward(l, rows, S, win, middle=None):
     x = S["x"][l]
     hat, _ = norm(x)
     u1 = hat.astype(bf16)
@@ -100,11 +100,16 @@
     hat, _ = norm(x1)
     u2 = hat.astype(bf16)
     S["u2"][l] = u2
+    if middle is not None:
+        middle()
     for n in range(4):
         pre = mm(u2, win[l, :, 4 * D + D * n : 5 * D + D * n])
         S["pre"][l, :, D * n : D * n + D] = pre
         bent = jnp.tanh(GELU_A * (pre + GELU_B * pre * pre * pre))
         S["h"][l, :, D * n : D * n + D] = (0.5 * pre * (1.0 + bent)).astype(bf16)
+
+
+def block_end(l, S, wdn):
     return S["x1"][l] + mm(S["h"][l], wdn[l])
 
 
@@ -358,7 +363,8 @@
     win_s=((LAYERS, 48, 4 * D + FF), bf16),
     wdn_s=((LAYERS, 192, D), bf16),
     table=((1, 128), jnp.int32),
-    cut=((IMG, TOK, D), bf16),
+    pout=((IMG, TOK, 256), bf16),
+    pin=((IMG, TOK, 256), bf16),
     packed=((8, PACK, D), bf16),
     swapped=((4, PACK, D), bf16),
     from_m=((CUT_A, D), bf16),
@@ -369,10 +375,10 @@
     line_z=((4, 8, TOK, D), bf16),
     pick_x=((4, 8, TOK, D), bf16),
     pick_z=((4, 8, TOK, D), bf16),
-    got_x=((3, 8, TOK, D), bf16),
-    got_z=((3, 8, TOK, D), bf16),
-    picked=((8, TOK, D), bf16),
-    own=((IMG, TOK, D), bf16),
+    ret_x=((2, 4, TOK, D), bf16),
+    ret_z=((2, 4, TOK, D), bf16),
+    got_x=((2, 8, TOK, D), bf16),
+    got_z=((2, 8, TOK, D), bf16),
     order=((4, D, 512), bf16),
     dperm=((2, 128, 512), bf16),
     pp=((128, D), bf16),
@@ -417,8 +423,15 @@
     x, z, y, c, r = place.x, place.z, place.y, place.c, place.r
     shard = place.me // 8
     win, wdn, arrived, packed = B["win"], B["wdn"], B["arrived"], B["packed"]
+    B["pout"][...] = jnp.zeros_like(B["pout"])
+    B["pout"][:, :, 0:192] = patches_t[...].T.reshape(IMG, TOK, 192)
     place.greet(True, True)
     wire = Wire(send_sem, recv_sem)
+
+    for i in range(1, 8):
+        j = (r + i) % 8
+        wire.send(B["pout"].at[j], B["pin"].at[r], i, place.group + j)
+    B["pin"][r] = B["pout"][r]
 
     def owner(dy, other=False):
         return (y + dy) % 4 * 2 + (1 - c if other else c)
@@ -454,6 +467,7 @@
 
     loads[2].wait()
     spread_first(pieces[0])
+    spread_last(pieces[0])
     for n in (3, 0, 1):
         loads[n].wait()
 
@@ -492,27 +506,24 @@
         for part in range(2):
             wire.wait(window(l, down, owner(2, True), part), b + 9 + part, place.partner)
 
+    for i in range(1, 8):
+        j = (r - i + 8) % 8
+        wire.wait(B["pin"].at[j], i, place.group + j)
+    patch_rows = B["pin"][:, :, 0:192].reshape(128, 192)
     tiled = jnp.concatenate([positions[...].astype(f32)] * IMG, axis=0)
-    C["x"][0] = mm(patches_t[...], embed[...], 0, 0) + tiled
-    cut = block_forward(0, 128, C, win_c, wdn_c).astype(bf16)
-    B["cut"][...] = cut.reshape(IMG, TOK, D)
-    for i in range(1, 8):
-        j = (r + i) % 8
-        wire.send(B["cut"].at[j], arrived.at[x, z, r], i, place.group + j)
-    spread_last(pieces[0])
+    C["x"][0] = mm(patch_rows, embed[...]) + tiled
+    block_forward(0, 128, C, win_c)
+    cut = block_end(0, C, wdn_c).astype(bf16)
+    arrived[x, z] = cut.reshape(IMG, TOK, D)
+    first, second, third, fourth, fifth = plane_gather(wire, place, arrived, 52)
+    first()
     for piece in pieces[1:]:
         spread_first(piece)
         spread_last(piece)
-    arrived[x, z, r] = B["cut"][r]
     selector, hot, table = route(arow[...], labels[...], shard, r)
     B["table"][...] = table
     to_scalar = pltpu.make_async_copy(B["table"], source, local_sem.at[4])
     to_scalar.start()
-    first, second, third, fourth, fifth = plane_gather(wire, place, arrived, 52)
-    for i in range(1, 8):
-        j = (r - i + 8) % 8
-        wire.wait(arrived.at[x, z, j], i, place.group + j)
-    first()
     forward(pieces[0])
     second()
     col = iota((1, 512), 1)
@@ -525,7 +536,7 @@
         wanted = lane + (entry // 3) * 6 + entry % 3
         B["order"][1 + q] = ((iota((D, 512), 0) == wanted) & (at >= 12)).astype(f32).astype(bf16)
     B["pp"][...] = (iota((128, D), 1) - 256 == (iota((128, D), 0) & 15)).astype(f32).astype(bf16)
-    B["pp"][:, 0:192] = patches_t[...].T
+    B["pp"][:, 0:192] = B["pin"][:, :, 0:192].reshape(128, 192)
     packed[:, PACK - 48 :, :] = jnp.zeros((8, 48, D), bf16)
     forward(pieces[1])
     third()
@@ -536,15 +547,16 @@
     fifth()
     across(pieces[1])
     settle(pieces[0])
+
+    S["x"][0] = slot_rows(selector, arrived[...].reshape(2048, D))
+    block_forward(0, 256, S, win)
     settle(pieces[1])
-
-    S["x"][0] = slot_rows(selector, arrived[...].reshape(2048, D))
-    S["x"][1] = block_forward(0, 256, S, win, wdn)
+    S["x"][1] = block_end(0, S, wdn)
     across(pieces[2])
-    across(pieces[3])
     settle(pieces[2])
+    block_forward(1, 256, S, win, lambda: across(pieces[3]))
     settle(pieces[3])
-    S["x"][2] = block_forward(1, 256, S, win, wdn)
+    S["x"][2] = block_end(1, S, wdn)
     to_scalar.wait()
     ours = iota((CLASSES, SHARDS, D), 1) == shard
     table = jnp.sum(jnp.where(ours, classes[...].astype(f32), 0.0), axis=1).astype(bf16)
@@ -615,44 +627,71 @@
     wire.send(packed.at[row(1, c), rows_b], B["fin_p"].at[rows_b], 103, place.yp)
     for line in lines:
         line.rest()
+    pick_x, pick_z = B["pick_x"], B["pick_z"]
+
+    def ring_one(src, hop, end, h, up, down, k0, k):
+        if k == 2:
+            wire.send(src(2, 0), hop.at[0], k0, up)
+            wire.send(src(2, 1), hop.at[1], k0 + 1, down)
+        if k == 1:
+            wire.send(src(1, 1), end.at[0, pl.ds(h, h)], k0 + 2, up)
+        if k == 3:
+            wire.send(src(3, 0), end.at[1, pl.ds(0, h)], k0 + 3, down)
+
+    def ring_two(src, load, hop, end, h, up, down, k0):
+        wire.wait(hop.at[0], k0, down)
+        load(1, 0, hop)
+        wire.send(src(1, 0), end.at[0, pl.ds(0, h)], k0 + 4, up)
+        wire.wait(hop.at[1], k0 + 1, up)
+        load(3, 1, hop)
+        wire.send(src(3, 1), end.at[1, pl.ds(h, h)], k0 + 5, down)
+
+    def ring_three(end, h, up, down, k0):
+        wire.wait(end.at[0, pl.ds(h, h)], k0 + 2, down)
+        wire.wait(end.at[1, pl.ds(0, h)], k0 + 3, up)
+        wire.wait(end.at[0, pl.ds(0, h)], k0 + 4, down)
+        wire.wait(end.at[1, pl.ds(h, h)], k0 + 5, up)
+
+    def part_of(pick):
+        return lambda k, part: pick.at[k, pl.ds(4 * part, 4)]
+
+    def load_of(pick):
+        def load(k, part, hop):
+            for i in range(4):
+                at = 4 * part + i
+                pick[k, at] = (pick[k, at].astype(f32) + hop[part, i].astype(f32)).astype(bf16)
+
+        return load
+
     for k in (2, 1, 3, 0):
+        zd, xd = (z + k) % 4, (x + k) % 4
         for m in range(8):
-            zd, xd = (z + k) % 4, (x + k) % 4
             at = source[0, (x * 4 + zd) * 8 + m]
             here = ((at >> 4) & 3 == z) & ((at & 15) < 8)
-            B["pick_x"][k, m] = jnp.where(here, line_x[(at >> 6) & 3, at & 7].astype(f32), 0.0).astype(bf16)
+            pick_x[k, m] = jnp.where(here, line_x[(at >> 6) & 3, at & 7].astype(f32), 0.0).astype(bf16)
+        ring_one(part_of(pick_x), B["ret_x"], B["got_x"], 4, place.zp, place.zm, 88, k)
+        for m in range(8):
             at = source[0, (xd * 4 + z) * 8 + m]
             here = ((at >> 6) & 3 == x) & ((at & 15) >= 8)
-            B["pick_z"][k, m] = jnp.where(here, line_z[(at >> 4) & 3, at & 7].astype(f32), 0.0).astype(bf16)
-        if k:
-            wire.send(B["pick_x"].at[k], B["got_x"].at[k - 1], 87 + k, place.at(0, k, 0))
-            wire.send(B["pick_z"].at[k], B["got_z"].at[k - 1], 90 + k, place.at(k, 0, 0))
+            pick_z[k, m] = jnp.where(here, line_z[(at >> 4) & 3, at & 7].astype(f32), 0.0).astype(bf16)
+        ring_one(part_of(pick_z), B["ret_z"], B["got_z"], 4, place.xp, place.xm, 109, k)
     server_weights(0)
     swap(rows_a, 94)
-    for k in range(1, 4):
-        wire.wait(B["got_x"].at[k - 1], 87 + k, place.at(0, 4 - k, 0))
-        wire.wait(B["got_z"].at[k - 1], 90 + k, place.at(4 - k, 0, 0))
-    for m in range(8):
-        piece = B["pick_x"][0, m].astype(f32) + B["pick_z"][0, m].astype(f32)
-        for k in range(3):
-            piece = piece + B["got_x"][k, m].astype(f32) + B["got_z"][k, m].astype(f32)
-        B["picked"][m] = piece.astype(bf16)
-    own = B["own"]
-    own[r] = B["picked"][r]
-    for i in range(1, 8):
-        m = (r + i) % 8
-        wire.send(B["picked"].at[m], own.at[r], 108 + i, place.group + m)
+    ring_two(part_of(pick_x), load_of(pick_x), B["ret_x"], B["got_x"], 4, place.zp, place.zm, 88)
+    ring_two(part_of(pick_z), load_of(pick_z), B["ret_z"], B["got_z"], 4, place.xp, place.xm, 109)
     combine_a(2)
     wire.send(packed.at[row(2, c), rows_a], B["from_m"], 104, place.yp)
     combine_a(3)
     wire.send(packed.at[row(3, c), rows_a], B["fin_m"].at[rows_a], 105, place.ym)
     combine_a(1)
     combine_b(3)
-    for i in range(1, 8):
-        j = (r - i + 8) % 8
-        wire.wait(own.at[j], 108 + i, place.group + j)
-
-    C["dy"][...] = own[...].reshape(128, D).astype(f32)
+    ring_three(B["got_x"], 4, place.zp, place.zm, 88)
+    ring_three(B["got_z"], 4, place.xp, place.xm, 109)
+    for m in range(8):
+        piece = pick_x[0, m].astype(f32) + pick_z[0, m].astype(f32)
+        for k in range(2):
+            piece = piece + B["got_x"][k, m].astype(f32) + B["got_z"][k, m].astype(f32)
+        C["dy"][16 * m : 16 * m + 16] = piece
     cpack, cswap, cmine = B["cpack"], B["cswap"], B["cmine"]
     pairs = weight_pairs(C, 0)
 
@@ -700,26 +739,6 @@
     def src_z(k, part):
         return cmine.at[pl.ds(2 * part, 2), (z + k) % 4, Z]
 
-    def ring_one(src, hop, end, up, down, k0):
-        wire.send(src(2, 0), hop.at[0], k0, up)
-        wire.send(src(2, 1), hop.at[1], k0 + 1, down)
-        wire.send(src(1, 1), end.at[0, pl.ds(2, 2)], k0 + 2, up)
-        wire.send(src(3, 0), end.at[1, pl.ds(0, 2)], k0 + 3, down)
-
-    def ring_two(src, load, hop, end, up, down, k0):
-        wire.wait(hop.at[0], k0, down)
-        load(1, 0, hop)
-        wire.send(src(1, 0), end.at[0, pl.ds(0, 2)], k0 + 4, up)
-        wire.wait(hop.at[1], k0 + 1, up)
-        load(3, 1, hop)
-        wire.send(src(3, 1), end.at[1, pl.ds(2, 2)], k0 + 5, down)
-
-    def ring_three(end, up, down, k0):
-        wire.wait(end.at[0, pl.ds(2, 2)], k0 + 2, down)
-        wire.wait(end.at[1, pl.ds(0, 2)], k0 + 3, up)
-        wire.wait(end.at[0, pl.ds(0, 2)], k0 + 4, down)
-        wire.wait(end.at[1, pl.ds(2, 2)], k0 + 5, up)
-
     def load_x(k, part, hop):
         to = (x + k) % 4
         for i in range(2):
@@ -735,10 +754,12 @@
     for b in (4, 5, 6, 7, 0, 1, 2, 3):
         wire.wait(cswap.at[pl.ds(2 * b, 2), pl.ds(0, MAIN)], 116 + b, place.partner)
     fold(0, PART)
-    ring_one(src_x, B["hop_x"], B["end_x"], place.xp, place.xm, 125)
+    for k in (2, 1, 3):
+        ring_one(src_x, B["hop_x"], B["end_x"], 2, place.xp, place.xm, 125, k)
     wire.wait(cswap.at[:, pl.ds(MAIN, TAIL)], 124, place.partner)
     fold(PART, BLOCK)
-    ring_one(src_z, B["hop_z"], B["end_z"], place.zp, place.zm, 131)
+    for k in (2, 1, 3):
+        ring_one(src_z, B["hop_z"], B["end_z"], 2, place.zp, place.zm, 131, k)
 
     wire.wait(B["from_m"], 104, place.ym)
 
@@ -758,16 +779,16 @@
     lax.fori_loop(0, (PACK - CUT_A) // 48, add_b, 0)
     wire.send(packed.at[row(3, c), rows_b], B["fin_m"].at[rows_b], 107, place.ym)
 
-    ring_two(src_x, load_x, B["hop_x"], B["end_x"], place.xp, place.xm, 125)
-    ring_two(src_z, load_z, B["hop_z"], B["end_z"], place.zp, place.zm, 131)
+    ring_two(src_x, load_x, B["hop_x"], B["end_x"], 2, place.xp, place.xm, 125)
+    ring_two(src_z, load_z, B["hop_z"], B["end_z"], 2, place.zp, place.zm, 131)
     half_x, half_z = B["half_x"], B["half_z"]
-    ring_three(B["end_x"], place.xp, place.xm, 125)
+    ring_three(B["end_x"], 2, place.xp, place.xm, 125)
     for i in range(4):
         total = cmine[x, i, :PART].astype(f32) + B["end_x"][0, i].astype(f32) + B["end_x"][1, i].astype(f32)
         half_x[i] = total.astype(bf16)
     for k in (2, 1, 3):
         wire.send(half_x.at[(z + k) % 4], B["two_x"].at[k - 1], 136 + k, place.at(0, k, 0))
-    ring_three(B["end_z"], place.zp, place.zm, 131)
+    ring_three(B["end_z"], 2, place.zp, place.zm, 131)
     for i in range(4):
         total = cmine[i, z, PART:].astype(f32) + B["end_z"][0, i].astype(f32) + B["end_z"][1, i].astype(f32)
         half_z[i] = total.astype(bf16)

time: 110 us -> 105 us (0.955)
  Pallas kernels: 109 us -> 104 us
    pallas_call x1, Pallas kernels: 107 us -> 102 us  [per_device(): pl.pallas_call(step_kernel, out_shape=[jax.ShapeDtypeStruct(*s) for s in...]
where the time goes in v5:
time: 105 us
  Pallas kernels  104 us (99%)
    pallas_call x1, Pallas kernels, per_device(): pl.pallas_call(step_kernel, out_shape=[jax.ShapeDtypeStruct(*s) for s in...  102 us
    pallas_call x1, Pallas kernels, per_device(): pl.pallas_call(finish_kernel, out_shape=[jax.ShapeDtypeStruct(*s) for s i...  2.63 us

profile of v5, /device:TPU:0, one launch (start us, length us, event | category | flops | bytes accessed | tf_op | source)
XLA Modules:
  0.0 105.0 jit_solution(13678600265897915481)
XLA Ops:
  0.6 101.5 %step.1 = (f32[1,16]{1,0:T(1,128)}, f32[2,48,3072]{2,1,0:T(8,128)}, f32[2,192,384]{2,1,0:T(8,128)}, f32[10,48]{1,0:T(8,128)}, f32[24,384]{1,0:T(8,128)}, /*index...) custom-call(bf16[192,128]{1,0:T(8,128)(2,1)} %bitcast.14, bf16[192,384]{1,0:T(8,128)(2,1)} %embed.1, ...), custom_call_target="tpu_custom_call" | custom-call | tf_op jit(solution)/shard_map/step/pallas_call | solution.py:891
  102.2 2.6 %finish.1 = (f32[1,16]{1,0:T(1,128)}, f32[2,48,3072]{2,1,0:T(8,128)}, f32[2,192,384]{2,1,0:T(8,128)}, f32[10,48]{1,0:T(8,128)}, f32[24,384]{1,0:T(8,128)}, /*ind...) custom-call(f32[1,16]{1,0:T(1,128)} %get-tuple-element.24.refs_0_, f32[2,48,3072]{2,1,0:T(8,128)} %get-tuple-element.25.refs_1_, ...), custom_call_target="tpu_custom_call" | custom-call | tf_op jit(solution)/shard_map/finish/pallas_call | solution.py:917

commit v6 on v5

--- a/solution.py
+++ b/solution.py
@@ -104,9 +104,13 @@
         middle()
     for n in range(4):
         pre = mm(u2, win[l, :, 4 * D + D * n : 5 * D + D * n])
-        S["pre"][l, :, D * n : D * n + D] = pre
-        bent = jnp.tanh(GELU_A * (pre + GELU_B * pre * pre * pre))
-        S["h"][l, :, D * n : D * n + D] = (0.5 * pre * (1.0 + bent)).astype(bf16)
+        square = pre * pre
+        bent = jnp.tanh(pre * (GELU_A + GELU_A * GELU_B * square))
+        gate = 0.5 + 0.5 * bent
+        value = pre * gate
+        S["h"][l, :, D * n : D * n + D] = value.astype(bf16)
+        bend = value * (1.0 - bent)
+        S["slope"][l, :, D * n : D * n + D] = gate + bend * (GELU_A + 3.0 * GELU_A * GELU_B * square)
 
 
 def block_end(l, S, wdn):
@@ -119,10 +123,7 @@
     for n in range(4):
         cols = slice(D * n, D * n + D)
         dh = rounded(mm(dyb, wdn[l, cols, :], 1, 1))
-        pre = S["pre"][l, :, cols]
-        bent = jnp.tanh(GELU_A * (pre + GELU_B * pre * pre * pre))
-        slope = 0.5 * (1.0 + bent) + 0.5 * pre * (1.0 - bent * bent) * GELU_A * (1.0 + 3.0 * GELU_B * pre * pre)
-        S["dpre"][l, :, cols] = (dh * slope).astype(bf16)
+        S["dpre"][l, :, cols] = (dh * S["slope"][l, :, cols]).astype(bf16)
     if early is not None:
         early()
     du2 = rounded(mm(S["dpre"][l], win[l, :, 4 * D :], 1, 1))
@@ -169,7 +170,7 @@
         qkv=((layers, rows, 3 * D), bf16),
         prob=((layers, 3 * rows // 128, 256, 128), f32),
         att=((layers, rows, D), bf16),
-        pre=((layers, rows, FF), f32),
+        slope=((layers, rows, FF), f32),
         h=((layers, rows, FF), bf16),
         dyb=((layers, rows, D), bf16),
         dpre=((layers, rows, FF), bf16),
@@ -468,7 +469,10 @@
     loads[2].wait()
     spread_first(pieces[0])
     spread_last(pieces[0])
-    for n in (3, 0, 1):
+    loads[3].wait()
+    spread_first(pieces[1])
+    spread_last(pieces[1])
+    for n in (0, 1):
         loads[n].wait()
 
     def forward(piece):
@@ -517,15 +521,16 @@
     arrived[x, z] = cut.reshape(IMG, TOK, D)
     first, second, third, fourth, fifth = plane_gather(wire, place, arrived, 52)
     first()
-    for piece in pieces[1:]:
-        spread_first(piece)
-        spread_last(piece)
+    forward(pieces[0])
     selector, hot, table = route(arow[...], labels[...], shard, r)
     B["table"][...] = table
     to_scalar = pltpu.make_async_copy(B["table"], source, local_sem.at[4])
     to_scalar.start()
-    forward(pieces[0])
     second()
+    forward(pieces[1])
+    for piece in pieces[2:]:
+        spread_first(piece)
+        spread_last(piece)
     col = iota((1, 512), 1)
     at = col & 15
     lane = ((col >> 4) & 15) * 24 + (col >> 8) * 3
@@ -538,15 +543,14 @@
     B["pp"][...] = (iota((128, D), 1) - 256 == (iota((128, D), 0) & 15)).astype(f32).astype(bf16)
     B["pp"][:, 0:192] = B["pin"][:, :, 0:192].reshape(128, 192)
     packed[:, PACK - 48 :, :] = jnp.zeros((8, 48, D), bf16)
-    forward(pieces[1])
     third()
+    across(pieces[0])
+    across(pieces[1])
     forward(pieces[2])
     fourth()
+    settle(pieces[0])
     forward(pieces[3])
-    across(pieces[0])
     fifth()
-    across(pieces[1])
-    settle(pieces[0])
 
     S["x"][0] = slot_rows(selector, arrived[...].reshape(2048, D))
     block_forward(0, 256, S, win)
@@ -728,10 +732,17 @@
 
     X, Z = pl.ds(0, PART), pl.ds(PART, PART)
 
-    def fold(low, high):
-        for i in range(16):
-            total = cpack[i, c, low:high].astype(f32) + cswap[i, low:high].astype(f32)
-            cmine[i // 4, i % 4, low:high] = total.astype(bf16)
+    def fold_x(k):
+        for i in range(4):
+            to = (x + k) % 4
+            total = cpack[4 * to + i, c, :PART].astype(f32) + cswap[4 * to + i, :PART].astype(f32)
+            cmine[to, i, :PART] = total.astype(bf16)
+
+    def fold_z(k):
+        for i in range(4):
+            to = (z + k) % 4
+            total = cpack[4 * i + to, c, PART:].astype(f32) + cswap[4 * i + to, PART:].astype(f32)
+            cmine[i, to, PART:] = total.astype(bf16)
 
     def src_x(k, part):
         return cmine.at[(x + k) % 4, pl.ds(2 * part, 2), X]
@@ -753,13 +764,16 @@
 
     for b in (4, 5, 6, 7, 0, 1, 2, 3):
         wire.wait(cswap.at[pl.ds(2 * b, 2), pl.ds(0, MAIN)], 116 + b, place.partner)
-    fold(0, PART)
     for k in (2, 1, 3):
+        fold_x(k)
         ring_one(src_x, B["hop_x"], B["end_x"], 2, place.xp, place.xm, 125, k)
     wire.wait(cswap.at[:, pl.ds(MAIN, TAIL)], 124, place.partner)
-    fold(PART, BLOCK)
     for k in (2, 1, 3):
+        fold_z(k)
         ring_one(src_z, B["hop_z"], B["end_z"], 2, place.zp, place.zm, 131, k)
+
+    fold_x(0)
+    fold_z(0)
 
     wire.wait(B["from_m"], 104, place.ym)
 

time: 105 us -> 102 us (0.971)
  Pallas kernels: 104 us -> 101 us
    pallas_call x1, Pallas kernels: 102 us -> 98.4 us  [per_device(): pl.pallas_call(step_kernel, out_shape=[jax.ShapeDtypeStruct(*s) for s in...]
where the time goes in v6:
time: 102 us
  Pallas kernels  101 us (99%)
    pallas_call x1, Pallas kernels, per_device(): pl.pallas_call(step_kernel, out_shape=[jax.ShapeDtypeStruct(*s) for s in...  98.4 us
    pallas_call x1, Pallas kernels, per_device(): pl.pallas_call(finish_kernel, out_shape=[jax.ShapeDtypeStruct(*s) for s i...  2.63 us

profile of v6, /device:TPU:0, one launch (start us, length us, event | category | flops | bytes accessed | tf_op | source)
XLA Modules:
  0.0 101.8 jit_solution(2393792057807774256)
XLA Ops:
  0.6 98.4 %step.1 = (f32[1,16]{1,0:T(1,128)}, f32[2,48,3072]{2,1,0:T(8,128)}, f32[2,192,384]{2,1,0:T(8,128)}, f32[10,48]{1,0:T(8,128)}, f32[24,384]{1,0:T(8,128)}, /*index...) custom-call(bf16[192,128]{1,0:T(8,128)(2,1)} %bitcast.14, bf16[192,384]{1,0:T(8,128)(2,1)} %embed.1, ...), custom_call_target="tpu_custom_call" | custom-call | tf_op jit(solution)/shard_map/step/pallas_call | solution.py:905
  99.0 2.6 %finish.1 = (f32[1,16]{1,0:T(1,128)}, f32[2,48,3072]{2,1,0:T(8,128)}, f32[2,192,384]{2,1,0:T(8,128)}, f32[10,48]{1,0:T(8,128)}, f32[24,384]{1,0:T(8,128)}, /*ind...) custom-call(f32[1,16]{1,0:T(1,128)} %get-tuple-element.24.refs_0_, f32[2,48,3072]{2,1,0:T(8,128)} %get-tuple-element.25.refs_1_, ...), custom_call_target="tpu_custom_call" | custom-call | tf_op jit(solution)/shard_map/finish/pallas_call | solution.py:931

commit v7 on v6

--- a/solution.py
+++ b/solution.py
@@ -196,16 +196,13 @@
         x, z, y = (self.x + dx) % 4, (self.z + dz) % 4, (self.y + dy) % 4
         return ((x * 4 + z) * 4 + y) * 2 + self.c
 
-    def greet(self, group, plane):
-        peers = []
-        if group:
-            peers += [self.group + (self.r + i) % 8 for i in range(1, 8)]
-        if plane:
-            peers += [self.xp, self.xm, self.zp, self.zm]
+    def greet(self):
+        peers = [self.group + (self.r + i) % 8 for i in range(1, 8)]
+        peers += [self.xp, self.xm, self.zp, self.zm]
         barrier = pltpu.get_barrier_semaphore()
         for peer in peers:
             pl.semaphore_signal(barrier, inc=1, device_id=(peer,), device_id_type=MESH)
-        pl.semaphore_wait(barrier, len(peers))
+        return len(peers)
 
 
 class Wire:
@@ -359,6 +356,12 @@
     arrived=((4, 4, IMG, TOK, D), bf16),
     win=((LAYERS, D, 4 * D + FF), bf16),
     wdn=((LAYERS, FF, D), bf16),
+    patches_t=((192, 128), bf16),
+    embed=((192, D), bf16),
+    positions=((TOK, D), bf16),
+    arow=((1, 128), jnp.int32),
+    labels=((8, 128), jnp.int32),
+    classes=((CLASSES, SHARDS, D), bf16),
     win_c=((1, D, 4 * D + FF), bf16),
     wdn_c=((1, FF, D), bf16),
     win_s=((LAYERS, 48, 4 * D + FF), bf16),
@@ -401,11 +404,12 @@
     gin=((LAYERS, 48, 4 * D + FF), f32),
     gdn=((LAYERS, 192, D), f32),
 )
+LOADED = ("patches_t", "embed", "positions", "arow", "labels", "classes", "win_c", "wdn_c", "win_s", "wdn_s")
 N_SEM = 160
 
 
-def step_kernel(patches_t, embed, positions, arow, labels, classes, *refs):
-    sources, refs = refs[:4], refs[4:]
+def step_kernel(*refs):
+    sources, refs = refs[:10], refs[10:]
     losses, gin, gdn, gcls_out, out_in, out_dn, out_pe, out_pos = refs[:8]
     refs = list(refs[8:])
     C = dict(zip(CLIENT, refs[: len(CLIENT)]))
@@ -414,19 +418,20 @@
     refs = refs[len(SERVER) :]
     B = dict(zip(BUFFERS, refs[: len(BUFFERS)]))
     send_sem, recv_sem, local_sem, source = refs[len(BUFFERS) :]
-    win_c, wdn_c, win_s, wdn_s = B["win_c"], B["wdn_c"], B["win_s"], B["wdn_s"]
-    loads = []
-    for n, (src, dst) in enumerate(zip(sources, (win_c, wdn_c, win_s, wdn_s))):
-        loads.append(pltpu.make_async_copy(src, dst, local_sem.at[n]))
-    for n in (2, 3, 0, 1):
-        loads[n].start()
+    held = [B[name] for name in LOADED]
+    patches_t, embed, positions, arow, labels, classes, win_c, wdn_c, win_s, wdn_s = held
+    loads = [pltpu.make_async_copy(src, dst, local_sem.at[n]) for n, (src, dst) in enumerate(zip(sources, held))]
     place = Place()
     x, z, y, c, r = place.x, place.z, place.y, place.c, place.r
     shard = place.me // 8
     win, wdn, arrived, packed = B["win"], B["wdn"], B["arrived"], B["packed"]
+    met = place.greet()
+    for n in (8, 0, 9, 1, 2, 6, 7, 3, 4, 5):
+        loads[n].start()
     B["pout"][...] = jnp.zeros_like(B["pout"])
+    loads[0].wait()
     B["pout"][:, :, 0:192] = patches_t[...].T.reshape(IMG, TOK, 192)
-    place.greet(True, True)
+    pl.semaphore_wait(pltpu.get_barrier_semaphore(), met)
     wire = Wire(send_sem, recv_sem)
 
     for i in range(1, 8):
@@ -466,13 +471,13 @@
         wire.send(mine, here, base[piece] + 6, place.partner)
         here[...] = mine[...]
 
-    loads[2].wait()
+    loads[8].wait()
     spread_first(pieces[0])
     spread_last(pieces[0])
-    loads[3].wait()
+    loads[9].wait()
     spread_first(pieces[1])
     spread_last(pieces[1])
-    for n in (0, 1):
+    for n in range(1, 8):
         loads[n].wait()
 
     def forward(piece):
@@ -524,7 +529,7 @@
     forward(pieces[0])
     selector, hot, table = route(arow[...], labels[...], shard, r)
     B["table"][...] = table
-    to_scalar = pltpu.make_async_copy(B["table"], source, local_sem.at[4])
+    to_scalar = pltpu.make_async_copy(B["table"], source, local_sem.at[10])
     to_scalar.start()
     second()
     forward(pieces[1])
@@ -850,8 +855,8 @@
         for b in range(4):
             B["gdn"][l, 48 * b : 48 * b + 48, :] = total_of(576 * l + D + 48 * b, 48)
     leaving = [
-        pltpu.make_async_copy(B["gin"], gin, local_sem.at[5]),
-        pltpu.make_async_copy(B["gdn"], gdn, local_sem.at[6]),
+        pltpu.make_async_copy(B["gin"], gin, local_sem.at[11]),
+        pltpu.make_async_copy(B["gdn"], gdn, local_sem.at[12]),
     ]
     for copy in leaving:
         copy.start()
@@ -905,13 +910,13 @@
     results = pl.pallas_call(
         step_kernel,
         out_shape=[jax.ShapeDtypeStruct(*s) for s in shapes],
-        in_specs=[VMEM] * 6 + [ANY] * 4,
+        in_specs=[ANY] * 10,
         out_specs=[VMEM, HBM, HBM] + [VMEM] * 5,
         scratch_shapes=[pltpu.VMEM(*s) for s in scratch]
         + [
             pltpu.SemaphoreType.DMA((N_SEM,)),
             pltpu.SemaphoreType.DMA((N_SEM,)),
-            pltpu.SemaphoreType.DMA((7,)),
+            pltpu.SemaphoreType.DMA((13,)),
             pltpu.SMEM((1, 128), jnp.int32),
         ],
         compiler_params=pltpu.CompilerParams(collective_id=0, has_side_effects=True, vmem_limit_bytes=67043328),

time: 102 us -> 101 us (level)
  no operation moved by 1% of the time
where the time goes in v7:
time: 101 us
  Pallas kernels  100 us (99%)
    pallas_call x1, Pallas kernels, per_device(): pl.pallas_call(step_kernel, out_shape=[jax.ShapeDtypeStruct(*s) for s in...  97.5 us
    pallas_call x1, Pallas kernels, per_device(): pl.pallas_call(finish_kernel, out_shape=[jax.ShapeDtypeStruct(*s) for s i...  2.63 us

profile of v7, /device:TPU:0, one launch (start us, length us, event | category | flops | bytes accessed | tf_op | source)
XLA Modules:
  0.0 100.9 jit_solution(13681613244913312781)
XLA Ops:
  0.6 97.5 %step.1 = (f32[1,16]{1,0:T(1,128)}, f32[2,48,3072]{2,1,0:T(8,128)}, f32[2,192,384]{2,1,0:T(8,128)}, f32[10,48]{1,0:T(8,128)}, f32[24,384]{1,0:T(8,128)}, /*index...) custom-call(bf16[192,128]{1,0:T(8,128)(2,1)} %bitcast.14, bf16[192,384]{1,0:T(8,128)(2,1)} %refs_1_.1, ...), custom_call_target="tpu_custom_call" | custom-call | tf_op jit(solution)/shard_map/step/pallas_call | solution.py:910
  98.1 2.6 %finish.1 = (f32[1,16]{1,0:T(1,128)}, f32[2,48,3072]{2,1,0:T(8,128)}, f32[2,192,384]{2,1,0:T(8,128)}, f32[10,48]{1,0:T(8,128)}, f32[24,384]{1,0:T(8,128)}, /*ind...) custom-call(f32[1,16]{1,0:T(1,128)} %get-tuple-element.24.refs_0_, f32[2,48,3072]{2,1,0:T(8,128)} %get-tuple-element.25.refs_1_, ...), custom_call_target="tpu_custom_call" | custom-call | tf_op jit(solution)/shard_map/finish/pallas_call | solution.py:936
